TPU v7x, 128 devices: a whole 4x4x4 slice. The times are simulated.
128 devices in a mesh: zone: 4 (over y), tile: 32 (over x, z, core).
Axes of the slice: x: 4, y: 4, z: 4, core: 2. Of those that a mesh axis runs over, the one named last changes fastest.
Arguments:
- tiles: bfloat16 [384, 13, 256, 256], P(('zone', 'tile')), may hold values from -6 to 6
- seam_list: int32 [256], P(('zone', 'tile')), may hold values from 0 to 2, as said below
- source: int32 [3072], P('zone'), may hold values from 0 to 95, as said below
- offsets: int32 [3072, 2], P('zone'), may hold values from -2 to 2
- fractions: float32 [3072, 2], P('zone'), may hold values from 0 to 1
- blend: float32 [3072], P('zone'), may hold values from 0.25 to 0.75
Outputs:
- polar_blocks: bfloat16 [3072, 13, 128, 128], P(('zone', 'tile'))
Inputs may be any that keep to these rules, and one draw needn't show every extreme that they name: Within the blocks of one owner device, no source device (index v // 3 of the strip) supplies more than 2 blocks; in every draw each owner takes exactly 2 blocks from some source device. Source devices are unevenly popular. `seam_list`: the 2 entries of one device are distinct.
All inputs are finite; a program needn't handle non-finite values.
Results may differ from a plain program's by a relative error of at most 0.0062.
Values may be sent and summed in bfloat16 or wider, within the bound.
No kernel may reach another device: no remote copies, remote signals or barrier semaphores. Data moves between devices by JAX's collectives and lax.ppermute only.
A program may use at most 192 MiB of HBM per device.

v0:
```python
import jax
import jax.numpy as jnp
from jax import lax
from jax.sharding import PartitionSpec as P

batch_slots = 8


def passed_along(value, axis, steps):
    count = lax.axis_size(axis)
    initial, last = (max(0, -steps), min(count, count - steps))
    return lax.ppermute(value, axis, [(source, source + steps) for source in range(initial, last)])


def cubic_weight(dist):
    mag = jnp.abs(dist)
    near = (1.5 * mag - 2.5) * mag * mag + 1.0
    far = ((-0.5 * mag + 2.5) * mag - 4.0) * mag + 2.0
    return jnp.where(mag <= 1.0, near, jnp.where(mag < 2.0, far, jnp.zeros_like(mag)))


def kernel_matrix(out_len, in_len, shift):
    rows = jnp.arange(out_len, dtype=jnp.float32)[:, None]
    cols = jnp.arange(in_len, dtype=jnp.float32)[None, :]
    return cubic_weight(cols - (2.0 * rows + shift)).astype(jnp.bfloat16)


def resample(mixed, offset_pair, fraction_pair):
    height = mixed.shape[1]
    width = mixed.shape[2]
    row_kernel = kernel_matrix(
        height // 2, height, offset_pair[0].astype(jnp.float32) + fraction_pair[0]
    )
    col_kernel = kernel_matrix(
        width // 2, width, offset_pair[1].astype(jnp.float32) + fraction_pair[1]
    )
    across = jnp.einsum(
        "bkt,ot->bko", mixed, col_kernel, preferred_element_type=jnp.float32
    ).astype(jnp.bfloat16)
    result = jnp.einsum("ik,bko->bio", row_kernel, across, preferred_element_type=jnp.float32)
    return result.astype(jnp.bfloat16)


def local(tiles, seam_list, source, offsets, fractions, blend):
    tile_count = lax.axis_size("tile")
    myself = lax.axis_index("tile")
    zone_index = lax.axis_index("zone")
    local_count = tiles.shape[0]
    per_owner = source.shape[0] // tile_count
    capacity = max(2, 2 * per_owner // tile_count)
    slots = tile_count * capacity
    block_shape = (tiles.shape[1], tiles.shape[2] // 2, tiles.shape[3] // 2)
    src_device = (source // local_count).reshape(tile_count, per_owner)
    order_ids = jnp.arange(per_owner, dtype=jnp.int32)
    same_device = src_device[:, :, None] == src_device[:, None, :]
    earlier = order_ids[None, :] < order_ids[:, None]
    rank = jnp.sum((same_device & earlier[None]).astype(jnp.int32), axis=2)
    wanted = (src_device[:, None, :] == myself) & (
        rank[:, None, :] == jnp.arange(capacity, dtype=jnp.int32)[None, :, None]
    )
    slot_block = jnp.sum(wanted.astype(jnp.int32) * order_ids, axis=2).reshape(slots)
    slot_owner = jnp.arange(slots, dtype=jnp.int32) // capacity
    slot_index = slot_owner * per_owner + slot_block
    picked = tiles[seam_list]
    near_tiles, near_list = passed_along((picked, seam_list), "zone", 1)

    def neighbour(index):
        match = near_list == index
        position = jnp.sum(
            match.astype(jnp.int32) * jnp.arange(near_list.shape[0], dtype=jnp.int32)
        )
        return (near_tiles[position], jnp.any(match))

    has_left = (zone_index > 0).astype(jnp.float32)

    def render(slot):
        block_index = slot_index[slot]
        local_tile = source[block_index] % local_count
        other, flagged = neighbour(local_tile)
        weight = blend[block_index] * flagged.astype(jnp.float32) * has_left
        primary = tiles[local_tile]
        mixed = (
            (1.0 - weight) * primary.astype(jnp.float32) + weight * other.astype(jnp.float32)
        ).astype(jnp.bfloat16)
        return resample(mixed, offsets[block_index], fractions[block_index])

    render_group = jax.vmap(render)
    groups = jnp.arange(slots, dtype=jnp.int32).reshape(slots // batch_slots, batch_slots)
    outgoing = lax.map(render_group, groups).reshape((slots,) + block_shape)
    incoming = lax.all_to_all(
        outgoing.reshape((tile_count, capacity) + block_shape),
        "tile",
        split_axis=0,
        concat_axis=0,
        tiled=True,
    )
    pick = src_device[myself] * capacity + rank[myself]
    return incoming.reshape((slots,) + block_shape)[pick]


def solution(mesh):
    in_specs = (
        P(("zone", "tile"), None, None, None),
        P(("zone", "tile")),
        P("zone"),
        P("zone", None),
        P("zone", None),
        P("zone"),
    )
    out_specs = P(("zone", "tile"), None, None, None)
    return jax.shard_map(local, mesh=mesh, in_specs=in_specs, out_specs=out_specs, check_vma=False)
```

profile of v0, /device:TPU:60, one launch (start us, length us, event | category | flops | bytes accessed | tf_op | source)
XLA Modules:
  0.0 885.1 jit_solution(17090024782851903729)
XLA Ops:
  0.0 0.7 compare_select_fusion.6
  0.7 5.0 gather_fusion.7
  5.6 1.3 collective-permute-start.1
  6.9 1.3 collective-permute-start
  8.2 0.7 add_select_fusion
  10.2 1.6 copy.26
  11.8 1.6 copy.27
  13.5 69.8 %collective-permute-done = s32[2]{0:T(128)S(1)} collective-permute-done((s32[2]{0:T(128)}, s32[2]{0:T(128)S(1)}, u32[]{:S(2)}, u32[]{:S(2)}) %collective-permute-start) | collective-permute-done | bytes 40 | tf_op jit(solution)/shard_map/ppermute | solution.py:12
  83.3 295.0 %while.13 = (s32[]{:T(128)}, bf16[8,8,13,128,128]{3,4,2,1,0:T(8,128)(2,1)}, s32[2]{0:T(128)S(1)}, s32[8,8]{1,0:T(8,128)S(1)}, s32[64]{0:T(128)S(1)}, /*index=5*/...) while((s32[]{:T(128)}, ...), condition=%wide.region_5.6_spmd, body=%wide.region_2.5_spmd.sunk | while | flops 2672693760 | bytes 85237248 | solution.py:89
  83.3 0.6 gather_fusion
  84.0 1.6 gather_fusion.5
  85.5 1.6 gather_fusion.6
  87.4 1.3 gather_fusion.1
  88.9 6.4 gather_fusion.2
  95.3 9.1 %gather_fusion.3 = bf16[8,13,256,256]{3,2,1,0:T(8,128)(2,1)} fusion(bf16[3,13,256,256]{3,2,1,0:T(8,128)(2,1)} %get-tuple-element.406, s32[8]{0:T(128)S(1)} %get-tuple-element.364), kind=kCustom, calls=%fused_computation.3.clone.1 | custom fusion | bytes 27263104 | tf_op jit(solution)/shard_map/while/body/eval_jaxpr/vmap()/gather | solution.py:81
  105.1 14.7 %bitcast_dynamic-update-slice_fusion.2 = bf16[8,8,13,128,128]{3,4,2,1,0:T(8,128)(2,1)} fusion(bf16[8,8,13,128,128]{3,4,2,1,0:T(8,128)(2,1)} %get-tuple-element.386, s32[]{:T(128)} %get-tuple-element.385, bf16[8,13,256,256]{3,2,1,0:T(8,128)(2,1)} %gather_fusion.2, bf16[8,13,256,256]{3,2,1,0:T(8,128)(2,1)} %gather_fusion.3, ...), kind=kOutput, calls=%fused_computation.18.clone.1 | convolution fusion | flops 2672689152 | bytes 30679616 | tf_op jit(solution)/shard_map/while/body/eval_jaxpr/vmap(ik,bko->bio)/dot_general | solution.py:40
  119.9 0.6 gather_fusion
  120.6 1.6 gather_fusion.5
  122.1 1.6 gather_fusion.6
  124.0 1.3 gather_fusion.1
  125.5 6.5 gather_fusion.2
  132.0 9.1 %gather_fusion.3 = bf16[8,13,256,256]{3,2,1,0:T(8,128)(2,1)} fusion(bf16[3,13,256,256]{3,2,1,0:T(8,128)(2,1)} %get-tuple-element.406, s32[8]{0:T(128)S(1)} %get-tuple-element.364), kind=kCustom, calls=%fused_computation.3.clone.1 | custom fusion | bytes 27263104 | tf_op jit(solution)/shard_map/while/body/eval_jaxpr/vmap()/gather | solution.py:81
  141.9 14.8 %bitcast_dynamic-update-slice_fusion.2 = bf16[8,8,13,128,128]{3,4,2,1,0:T(8,128)(2,1)} fusion(bf16[8,8,13,128,128]{3,4,2,1,0:T(8,128)(2,1)} %get-tuple-element.386, s32[]{:T(128)} %get-tuple-element.385, bf16[8,13,256,256]{3,2,1,0:T(8,128)(2,1)} %gather_fusion.2, bf16[8,13,256,256]{3,2,1,0:T(8,128)(2,1)} %gather_fusion.3, ...), kind=kOutput, calls=%fused_computation.18.clone.1 | convolution fusion | flops 2672689152 | bytes 30679616 | tf_op jit(solution)/shard_map/while/body/eval_jaxpr/vmap(ik,bko->bio)/dot_general | solution.py:40
  156.7 0.6 gather_fusion
  157.4 1.6 gather_fusion.5
  158.9 1.6 gather_fusion.6
  160.8 1.3 gather_fusion.1
  162.3 6.5 gather_fusion.2
  168.8 9.2 %gather_fusion.3 = bf16[8,13,256,256]{3,2,1,0:T(8,128)(2,1)} fusion(bf16[3,13,256,256]{3,2,1,0:T(8,128)(2,1)} %get-tuple-element.406, s32[8]{0:T(128)S(1)} %get-tuple-element.364), kind=kCustom, calls=%fused_computation.3.clone.1 | custom fusion | bytes 27263104 | tf_op jit(solution)/shard_map/while/body/eval_jaxpr/vmap()/gather | solution.py:81
  178.8 14.8 %bitcast_dynamic-update-slice_fusion.2 = bf16[8,8,13,128,128]{3,4,2,1,0:T(8,128)(2,1)} fusion(bf16[8,8,13,128,128]{3,4,2,1,0:T(8,128)(2,1)} %get-tuple-element.386, s32[]{:T(128)} %get-tuple-element.385, bf16[8,13,256,256]{3,2,1,0:T(8,128)(2,1)} %gather_fusion.2, bf16[8,13,256,256]{3,2,1,0:T(8,128)(2,1)} %gather_fusion.3, ...), kind=kOutput, calls=%fused_computation.18.clone.1 | convolution fusion | flops 2672689152 | bytes 30679616 | tf_op jit(solution)/shard_map/while/body/eval_jaxpr/vmap(ik,bko->bio)/dot_general | solution.py:40
  194.3 1.6 gather_fusion.5
  195.8 1.6 gather_fusion.6
  197.7 1.3 gather_fusion.1
  199.2 6.6 gather_fusion.2
  205.8 9.2 %gather_fusion.3 = bf16[8,13,256,256]{3,2,1,0:T(8,128)(2,1)} fusion(bf16[3,13,256,256]{3,2,1,0:T(8,128)(2,1)} %get-tuple-element.406, s32[8]{0:T(128)S(1)} %get-tuple-element.364), kind=kCustom, calls=%fused_computation.3.clone.1 | custom fusion | bytes 27263104 | tf_op jit(solution)/shard_map/while/body/eval_jaxpr/vmap()/gather | solution.py:81
  215.8 14.8 %bitcast_dynamic-update-slice_fusion.2 = bf16[8,8,13,128,128]{3,4,2,1,0:T(8,128)(2,1)} fusion(bf16[8,8,13,128,128]{3,4,2,1,0:T(8,128)(2,1)} %get-tuple-element.386, s32[]{:T(128)} %get-tuple-element.385, bf16[8,13,256,256]{3,2,1,0:T(8,128)(2,1)} %gather_fusion.2, bf16[8,13,256,256]{3,2,1,0:T(8,128)(2,1)} %gather_fusion.3, ...), kind=kOutput, calls=%fused_computation.18.clone.1 | convolution fusion | flops 2672689152 | bytes 30679616 | tf_op jit(solution)/shard_map/while/body/eval_jaxpr/vmap(ik,bko->bio)/dot_general | solution.py:40
  231.3 1.6 gather_fusion.5
  232.9 1.6 gather_fusion.6
  234.8 1.3 gather_fusion.1
  236.2 6.7 gather_fusion.2
  243.0 9.2 %gather_fusion.3 = bf16[8,13,256,256]{3,2,1,0:T(8,128)(2,1)} fusion(bf16[3,13,256,256]{3,2,1,0:T(8,128)(2,1)} %get-tuple-element.406, s32[8]{0:T(128)S(1)} %get-tuple-element.364), kind=kCustom, calls=%fused_computation.3.clone.1 | custom fusion | bytes 27263104 | tf_op jit(solution)/shard_map/while/body/eval_jaxpr/vmap()/gather | solution.py:81
  253.0 14.7 %bitcast_dynamic-update-slice_fusion.2 = bf16[8,8,13,128,128]{3,4,2,1,0:T(8,128)(2,1)} fusion(bf16[8,8,13,128,128]{3,4,2,1,0:T(8,128)(2,1)} %get-tuple-element.386, s32[]{:T(128)} %get-tuple-element.385, bf16[8,13,256,256]{3,2,1,0:T(8,128)(2,1)} %gather_fusion.2, bf16[8,13,256,256]{3,2,1,0:T(8,128)(2,1)} %gather_fusion.3, ...), kind=kOutput, calls=%fused_computation.18.clone.1 | convolution fusion | flops 2672689152 | bytes 30679616 | tf_op jit(solution)/shard_map/while/body/eval_jaxpr/vmap(ik,bko->bio)/dot_general | solution.py:40
  268.4 1.6 gather_fusion.5
  270.0 1.6 gather_fusion.6
  271.9 1.3 gather_fusion.1
  273.3 6.5 gather_fusion.2
  279.8 9.0 %gather_fusion.3 = bf16[8,13,256,256]{3,2,1,0:T(8,128)(2,1)} fusion(bf16[3,13,256,256]{3,2,1,0:T(8,128)(2,1)} %get-tuple-element.406, s32[8]{0:T(128)S(1)} %get-tuple-element.364), kind=kCustom, calls=%fused_computation.3.clone.1 | custom fusion | bytes 27263104 | tf_op jit(solution)/shard_map/while/body/eval_jaxpr/vmap()/gather | solution.py:81
  289.6 14.8 %bitcast_dynamic-update-slice_fusion.2 = bf16[8,8,13,128,128]{3,4,2,1,0:T(8,128)(2,1)} fusion(bf16[8,8,13,128,128]{3,4,2,1,0:T(8,128)(2,1)} %get-tuple-element.386, s32[]{:T(128)} %get-tuple-element.385, bf16[8,13,256,256]{3,2,1,0:T(8,128)(2,1)} %gather_fusion.2, bf16[8,13,256,256]{3,2,1,0:T(8,128)(2,1)} %gather_fusion.3, ...), kind=kOutput, calls=%fused_computation.18.clone.1 | convolution fusion | flops 2672689152 | bytes 30679616 | tf_op jit(solution)/shard_map/while/body/eval_jaxpr/vmap(ik,bko->bio)/dot_general | solution.py:40
  305.0 1.6 gather_fusion.5
  306.6 1.6 gather_fusion.6
  308.5 1.3 gather_fusion.1
  309.9 6.4 gather_fusion.2
  316.3 9.2 %gather_fusion.3 = bf16[8,13,256,256]{3,2,1,0:T(8,128)(2,1)} fusion(bf16[3,13,256,256]{3,2,1,0:T(8,128)(2,1)} %get-tuple-element.406, s32[8]{0:T(128)S(1)} %get-tuple-element.364), kind=kCustom, calls=%fused_computation.3.clone.1 | custom fusion | bytes 27263104 | tf_op jit(solution)/shard_map/while/body/eval_jaxpr/vmap()/gather | solution.py:81
  326.3 14.8 %bitcast_dynamic-update-slice_fusion.2 = bf16[8,8,13,128,128]{3,4,2,1,0:T(8,128)(2,1)} fusion(bf16[8,8,13,128,128]{3,4,2,1,0:T(8,128)(2,1)} %get-tuple-element.386, s32[]{:T(128)} %get-tuple-element.385, bf16[8,13,256,256]{3,2,1,0:T(8,128)(2,1)} %gather_fusion.2, bf16[8,13,256,256]{3,2,1,0:T(8,128)(2,1)} %gather_fusion.3, ...), kind=kOutput, calls=%fused_computation.18.clone.1 | convolution fusion | flops 2672689152 | bytes 30679616 | tf_op jit(solution)/shard_map/while/body/eval_jaxpr/vmap(ik,bko->bio)/dot_general | solution.py:40
  341.8 1.6 gather_fusion.5
  343.4 1.6 gather_fusion.6
  345.3 1.3 gather_fusion.1
  346.7 6.6 gather_fusion.2
  353.3 9.4 %gather_fusion.3 = bf16[8,13,256,256]{3,2,1,0:T(8,128)(2,1)} fusion(bf16[3,13,256,256]{3,2,1,0:T(8,128)(2,1)} %get-tuple-element.406, s32[8]{0:T(128)S(1)} %get-tuple-element.364), kind=kCustom, calls=%fused_computation.3.clone.1 | custom fusion | bytes 27263104 | tf_op jit(solution)/shard_map/while/body/eval_jaxpr/vmap()/gather | solution.py:81
  363.4 14.8 %bitcast_dynamic-update-slice_fusion.2 = bf16[8,8,13,128,128]{3,4,2,1,0:T(8,128)(2,1)} fusion(bf16[8,8,13,128,128]{3,4,2,1,0:T(8,128)(2,1)} %get-tuple-element.386, s32[]{:T(128)} %get-tuple-element.385, bf16[8,13,256,256]{3,2,1,0:T(8,128)(2,1)} %gather_fusion.2, bf16[8,13,256,256]{3,2,1,0:T(8,128)(2,1)} %gather_fusion.3, ...), kind=kOutput, calls=%fused_computation.18.clone.1 | convolution fusion | flops 2672689152 | bytes 30679616 | tf_op jit(solution)/shard_map/while/body/eval_jaxpr/vmap(ik,bko->bio)/dot_general | solution.py:40
  378.2 35.9 %copy.28 = bf16[32,2,13,128,128]{4,3,2,1,0:T(8,128)(2,1)} copy(bf16[32,2,13,128,128]{3,4,2,1,0:T(8,128)(2,1)} %bitcast.61) | data formatting | bytes 54525952 | tf_op jit(solution)/shard_map/reshape;reshape | solution.py:91
  414.2 9.7 %all-to-all-start = ((bf16[32,2,13,128,128]{4,3,2,1,0:T(8,128)(2,1)}), bf16[32,2,13,128,128]{4,3,2,1,0:T(8,128)(2,1)}, u32[]{:S(2)}, u32[]{:S(2)}) async-start(bf16[32,2,13,128,128]{4,3,2,1,0:T(8,128)(2,1)} %copy.28), calls=%async_computation | async-start | bytes 54525952 | tf_op jit(solution)/shard_map/all_to_all | solution.py:90
  424.2 445.9 %all-to-all-done = bf16[32,2,13,128,128]{4,3,2,1,0:T(8,128)(2,1)} async-done(((bf16[32,2,13,128,128]{4,3,2,1,0:T(8,128)(2,1)}), bf16[32,2,13,128,128]{4,3,2,1,0:T(8,128)(2,1)}, u32[]{:S(2)}, u32[]{:S(2)}) %all-to-all-start) | async-done | bytes 27263008 | tf_op jit(solution)/shard_map/all_to_all | solution.py:90
  870.1 15.0 %gather_fusion.8 = bf16[24,13,128,128]{3,2,1,0:T(8,128)(2,1)} fusion(bf16[64,13,128,128]{3,2,1,0:T(8,128)(2,1)} %bitcast.16, s32[1024]{0:T(1024)S(1)} %pad_clamp_fusion.2), kind=kCustom, calls=%fused_computation.8 | custom fusion | bytes 20447328 | tf_op jit(solution)/shard_map/gather | solution.py:98
  (150 shorter events, 14.1 us)
Async XLA Ops:
  5.6 77.6 %collective-permute-start.1 = (bf16[2,13,256,256]{3,2,1,0:T(8,128)(2,1)}, bf16[2,13,256,256]{3,2,1,0:T(8,128)(2,1)S(1)}, u32[]{:S(2)}, u32[]{:S(2)}) collective-permute-start(bf16[2,13,256,256]{3,2,1,0:T(8,128)(2,1)} %gather_fusion.7), channel_id=1, source_target_pairs={{0,32},{32,64},{64,96},{1,33},{33,65},{65,97},{2,34},{34,66},{66,9... | collective-permute-start | bytes 10223624 | tf_op jit(solution)/shard_map/ppermute | solution.py:12
  6.9 76.4 %collective-permute-start = (s32[2]{0:T(128)}, s32[2]{0:T(128)S(1)}, u32[]{:S(2)}, u32[]{:S(2)}) collective-permute-start(s32[2]{0:T(128)} %param.9), channel_id=1, source_target_pairs={{0,32},{32,64},{64,96},{1,33},{33,65},{65,97},{2,34},{34,66},{66,9... | collective-permute-start | bytes 32 | tf_op jit(solution)/shard_map/ppermute | solution.py:12
  9.1 4.4 copy-start.1
  9.4 0.6 copy-start.3
  95.3 9.2 %copy-start = (f32[768]{0:T(1024)S(1)}, f32[768]{0:T(1024)}, u32[]{:S(2)}) copy-start(f32[768]{0:T(1024)} %get-tuple-element.404) | copy-start | bytes 9220 | tf_op jit(solution)/shard_map/while
  132.0 9.2 %copy-start = (f32[768]{0:T(1024)S(1)}, f32[768]{0:T(1024)}, u32[]{:S(2)}) copy-start(f32[768]{0:T(1024)} %get-tuple-element.404) | copy-start | bytes 9220 | tf_op jit(solution)/shard_map/while
  168.8 9.3 %copy-start = (f32[768]{0:T(1024)S(1)}, f32[768]{0:T(1024)}, u32[]{:S(2)}) copy-start(f32[768]{0:T(1024)} %get-tuple-element.404) | copy-start | bytes 9220 | tf_op jit(solution)/shard_map/while
  205.8 9.3 %copy-start = (f32[768]{0:T(1024)S(1)}, f32[768]{0:T(1024)}, u32[]{:S(2)}) copy-start(f32[768]{0:T(1024)} %get-tuple-element.404) | copy-start | bytes 9220 | tf_op jit(solution)/shard_map/while
  243.0 9.3 %copy-start = (f32[768]{0:T(1024)S(1)}, f32[768]{0:T(1024)}, u32[]{:S(2)}) copy-start(f32[768]{0:T(1024)} %get-tuple-element.404) | copy-start | bytes 9220 | tf_op jit(solution)/shard_map/while
  279.8 9.1 %copy-start = (f32[768]{0:T(1024)S(1)}, f32[768]{0:T(1024)}, u32[]{:S(2)}) copy-start(f32[768]{0:T(1024)} %get-tuple-element.404) | copy-start | bytes 9220 | tf_op jit(solution)/shard_map/while
  316.3 9.3 %copy-start = (f32[768]{0:T(1024)S(1)}, f32[768]{0:T(1024)}, u32[]{:S(2)}) copy-start(f32[768]{0:T(1024)} %get-tuple-element.404) | copy-start | bytes 9220 | tf_op jit(solution)/shard_map/while
  353.3 9.5 %copy-start = (f32[768]{0:T(1024)S(1)}, f32[768]{0:T(1024)}, u32[]{:S(2)}) copy-start(f32[768]{0:T(1024)} %get-tuple-element.404) | copy-start | bytes 9220 | tf_op jit(solution)/shard_map/while
  414.2 9.8 %copy-start.2 = (s32[32,24]{0,1:T(8,128)S(1)}, s32[32,24]{0,1:T(8,128)}, u32[]{:S(2)}) copy-start(s32[32,24]{0,1:T(8,128)} %copy-done.1) | copy-start | bytes 9220
  414.2 9.8 %copy-start.4 = (s32[32,24]{0,1:T(8,128)S(1)}, s32[32,24]{0,1:T(8,128)}, u32[]{:S(2)}) copy-start(s32[32,24]{0,1:T(8,128)} %copy-done.3) | copy-start | bytes 9220
  414.2 455.9 %all-to-all-start = ((bf16[32,2,13,128,128]{4,3,2,1,0:T(8,128)(2,1)}), bf16[32,2,13,128,128]{4,3,2,1,0:T(8,128)(2,1)}, u32[]{:S(2)}, u32[]{:S(2)}) async-start(bf16[32,2,13,128,128]{4,3,2,1,0:T(8,128)(2,1)} %copy.28), calls=%async_computation | async-start | bytes 54525952 | tf_op jit(solution)/shard_map/all_to_all | solution.py:90
where the time goes:
time: 887 us; the launch traced here: 885 us
  waiting for transfers between devices  516 us (58%)
  local copies, waits for them, and re-layouts  232 us (26%)
  matrix products  118 us (13%)
  starting transfers between devices  12.3 us (1%)
    all_to_all x1, waiting for transfers between devices, local(): lax.all_to_all(outgoing.reshape((tile_count, capacity) + block_shape), 't...  446 us
    dot_general x8, matrix products, resample(): jnp.einsum('ik,bko->bio', row_kernel, across, preferred_element_type=jnp....  118 us
    gather x8, local copies, waits for them, and re-layouts, render(): primary = tiles[local_tile]  73.6 us
    ppermute x2, waiting for transfers between devices, passed_along(): lax.ppermute(value, axis, [(source, source + steps) for source in range(i...  69.8 us
    gather x8, local copies, waits for them, and re-layouts, neighbour(): return (near_tiles[position], jnp.any(match))  52.3 us
    another operation x1, local copies, waits for them, and re-layouts, local(): outgoing.reshape((tile_count, capacity) + block_shape)  35.9 us
    gather x16, local copies, waits for them, and re-layouts, render(): return resample(mixed, offsets[block_index], fractions[block_index])  25.3 us
  transfers between devices with their start and end apart: 3, of which 2 were waited for; matrix products, arithmetic and copies ran while one was open for 1% of the time, Pallas kernels for 0%

commit v1 on v0

v1 whole, which is shorter than its diff:
```python
import functools

import jax
import jax.numpy as jnp
from jax import lax
from jax.experimental import pallas as pl
from jax.experimental.pallas import tpu as pltpu
from jax.sharding import PartitionSpec as P

CHUNKS = (1, 2, 3, 4, 3)


def passed_along(value, axis, steps):
    count = lax.axis_size(axis)
    initial, last = (max(0, -steps), min(count, count - steps))
    return lax.ppermute(value, axis, [(source, source + steps) for source in range(initial, last)])


def cubic_weight(dist):
    mag = jnp.abs(dist)
    near = (1.5 * mag - 2.5) * mag * mag + 1.0
    far = ((-0.5 * mag + 2.5) * mag - 4.0) * mag + 2.0
    return jnp.where(mag <= 1.0, near, jnp.where(mag < 2.0, far, jnp.zeros_like(mag)))


def render_kernel(
    local_count, first, bands, count_ref, blocks_ref, slots_ref, source_ref, offsets_ref, fractions_ref, blend_ref,
    listed_ref, tiles_ref, near_ref, out_ref, held, beside, done, in_sem, out_sem,
):
    load = pltpu.make_async_copy(tiles_ref.at[:, pl.ds(first, bands)], held, in_sem.at[0])
    load_near = pltpu.make_async_copy(near_ref, beside, in_sem.at[1])
    load.start()
    load_near.start()
    load.wait()
    load_near.wait()
    height, width = held.shape[2], held.shape[3]
    count = count_ref[0]

    def store(index, way):
        return pltpu.make_async_copy(done.at[way], out_ref.at[slots_ref[index]], out_sem.at[way])

    def taps(shape, out_dim, shift):
        out_pos = lax.broadcasted_iota(jnp.int32, shape, out_dim).astype(jnp.float32)
        in_pos = lax.broadcasted_iota(jnp.int32, shape, 1 - out_dim).astype(jnp.float32)
        return cubic_weight(in_pos - (2.0 * out_pos + shift)).astype(jnp.bfloat16)

    def one(index, carry):
        way = lax.rem(index, 2)
        block = blocks_ref[index]
        tile = lax.rem(source_ref[block], local_count)
        second = listed_ref[1] == tile
        flagged = (second | (listed_ref[0] == tile)) & (listed_ref[2] > 0)
        place = jnp.where(second, 1, 0)
        weight = jnp.where(flagged, blend_ref[block], 0.0)
        row_kernel = taps(
            (height // 2, height), 0, offsets_ref[2 * block].astype(jnp.float32) + fractions_ref[2 * block]
        )
        col_kernel = taps(
            (width, width // 2), 1, offsets_ref[2 * block + 1].astype(jnp.float32) + fractions_ref[2 * block + 1]
        )

        @pl.when(index >= 2)
        def _():
            store(index - 2, way).wait()

        def resample(mixed, band):
            across = jnp.dot(mixed, col_kernel, preferred_element_type=jnp.float32).astype(jnp.bfloat16)
            result = jnp.dot(row_kernel, across, preferred_element_type=jnp.float32)
            done[way, band] = result.astype(jnp.bfloat16)

        @pl.when(weight == 0.0)
        def _():
            for band in range(bands):
                resample(held[tile, band], band)

        @pl.when(weight != 0.0)
        def _():
            for band in range(bands):
                mixed = (1.0 - weight) * held[tile, band].astype(jnp.float32) + weight * beside[
                    place, band
                ].astype(jnp.float32)
                resample(mixed.astype(jnp.bfloat16), band)

        store(index, way).start()
        return carry

    lax.fori_loop(0, count, one, 0)

    @pl.when(count >= 2)
    def _():
        store(count - 2, lax.rem(count, 2)).wait()

    @pl.when(count >= 1)
    def _():
        store(count - 1, lax.rem(count + 1, 2)).wait()


def render(scalars, tiles, near, first, bands, slots):
    local_count, _, height, width = tiles.shape
    block = (bands, height // 2, width // 2)
    flops = 24 * bands * (2 * height * width * width // 2 + height * width * height // 2)
    return pl.pallas_call(
        functools.partial(render_kernel, local_count, first, bands),
        out_shape=jax.ShapeDtypeStruct((slots,) + block, jnp.bfloat16),
        in_specs=[pl.BlockSpec(memory_space=pltpu.SMEM)] * len(scalars) + [pl.BlockSpec(memory_space=pl.ANY)] * 2,
        out_specs=pl.BlockSpec(memory_space=pl.ANY),
        scratch_shapes=[
            pltpu.VMEM((local_count, bands, height, width), jnp.bfloat16),
            pltpu.VMEM((near.shape[0], bands, height, width), jnp.bfloat16),
            pltpu.VMEM((2,) + block, jnp.bfloat16),
            pltpu.SemaphoreType.DMA((2,)),
            pltpu.SemaphoreType.DMA((2,)),
        ],
        cost_estimate=pl.CostEstimate(flops=8 * flops, bytes_accessed=24 * bands * height * width // 2, transcendentals=0),
        name="render",
    )(*scalars, tiles, near)


def place_kernel(first, bands, pick_ref, incoming_ref, *refs):
    out_ref, held, in_sem, out_sem = refs[-4:]
    count = out_ref.shape[0]

    def take(index):
        return pltpu.make_async_copy(incoming_ref.at[pick_ref[index]], held.at[index], in_sem.at[index])

    def put(index):
        return pltpu.make_async_copy(held.at[index], out_ref.at[index, pl.ds(first, bands)], out_sem.at[index])

    for index in range(count):
        take(index).start()
    for index in range(count):
        take(index).wait()
        put(index).start()
    for index in range(count):
        put(index).wait()


def place(pick, incoming, output, first, shape):
    bands = incoming.shape[1]
    held = (shape[0], bands) + shape[2:]
    arrays = [incoming] + ([] if output is None else [output])
    return pl.pallas_call(
        functools.partial(place_kernel, first, bands),
        out_shape=jax.ShapeDtypeStruct(shape, jnp.bfloat16),
        in_specs=[pl.BlockSpec(memory_space=pltpu.SMEM)] + [pl.BlockSpec(memory_space=pl.ANY)] * len(arrays),
        out_specs=pl.BlockSpec(memory_space=pl.ANY),
        scratch_shapes=[
            pltpu.VMEM(held, jnp.bfloat16),
            pltpu.SemaphoreType.DMA((shape[0],)),
            pltpu.SemaphoreType.DMA((shape[0],)),
        ],
        input_output_aliases={} if output is None else {2: 0},
        cost_estimate=pl.CostEstimate(flops=0, bytes_accessed=4 * shape[0] * bands * shape[2] * shape[3], transcendentals=0),
        name="place",
    )(pick, *arrays)


def local(tiles, seam_list, source, offsets, fractions, blend):
    tile_count = lax.axis_size("tile")
    myself = lax.axis_index("tile")
    zone_index = lax.axis_index("zone")
    local_count, band_count, height, width = tiles.shape
    per_owner = source.shape[0] // tile_count
    capacity = max(2, 2 * per_owner // tile_count)
    slots = tile_count * capacity

    near_list = passed_along(seam_list, "zone", 1)
    listed = jnp.concatenate([near_list, zone_index[None].astype(jnp.int32)])

    src_device = (source // local_count).reshape(tile_count, per_owner)
    order_ids = jnp.arange(per_owner, dtype=jnp.int32)
    owner_ids = jnp.arange(tile_count, dtype=jnp.int32)
    mine = src_device == myself
    earlier = order_ids[None, :] < order_ids[:, None]
    rank = jnp.sum((mine[:, None, :] & earlier[None]).astype(jnp.int32), axis=2)
    held_by = jnp.sum(mine.astype(jnp.int32), axis=1)
    ahead = jnp.sum(jnp.where(owner_ids[None, :] < owner_ids[:, None], held_by[None, :], 0), axis=1)
    turn = jnp.where(mine, rank + ahead[:, None], -1)
    hit = turn[None] == jnp.arange(slots, dtype=jnp.int32)[:, None, None]
    block_ids = owner_ids[:, None] * per_owner + order_ids[None, :]
    slot_ids = owner_ids[:, None] * capacity + rank
    blocks = jnp.sum(jnp.where(hit, block_ids[None], 0), axis=(1, 2))
    into = jnp.sum(jnp.where(hit, slot_ids[None], 0), axis=(1, 2))
    count = jnp.sum(held_by)[None]

    own = lax.dynamic_index_in_dim(src_device, myself, 0, keepdims=False)
    own_rank = jnp.sum(((own[:, None] == own[None, :]) & earlier).astype(jnp.int32), axis=1)
    pick = own * capacity + own_rank

    scalars = (count, blocks, into, source, offsets.reshape(-1), fractions.reshape(-1), blend, listed)
    shape = (per_owner, band_count, height // 2, width // 2)
    output = None
    first = 0
    for bands in CHUNKS:
        part = tiles[:, first : first + bands]
        picked = jnp.concatenate(
            [lax.dynamic_index_in_dim(part, seam_list[i], 0) for i in range(seam_list.shape[0])], axis=0
        )
        near = passed_along(picked, "zone", 1)
        outgoing = render(scalars, tiles, near, first, bands, slots)
        incoming = lax.all_to_all(
            outgoing.reshape((tile_count, capacity) + outgoing.shape[1:]), "tile", split_axis=0, concat_axis=0, tiled=True
        )
        output = place(pick, incoming.reshape((slots,) + outgoing.shape[1:]), output, first, shape)
        first += bands
    return output


def solution(mesh):
    in_specs = (
        P(("zone", "tile"), None, None, None),
        P(("zone", "tile")),
        P("zone"),
        P("zone", None),
        P("zone", None),
        P("zone"),
    )
    out_specs = P(("zone", "tile"), None, None, None)
    return jax.shard_map(local, mesh=mesh, in_specs=in_specs, out_specs=out_specs, check_vma=False)
```

time: 887 us -> 574 us (0.65)
  local copies, waits for them, and re-layouts: 232 us -> 12.5 us
  waiting for transfers between devices: 516 us -> 305 us
  starting transfers between devices: 12.3 us -> 180 us
  matrix products: 118 us -> 0 us
  Pallas kernels: 0 us -> 61.2 us
    all_to_all x1 -> x5, waiting for transfers between devices: 446 us -> 222 us  [local(): lax.all_to_all(outgoing.reshape((tile_count, capacity) + outgoing.shape[1...]
    gather x58 -> x0, local copies, waits for them, and re-layouts: 192 us -> none  [the longest x8 73.6 us: render(): primary = tiles[local_tile]]
    all_to_all x1 -> x5, starting transfers between devices: 9.75 us -> 173 us  [local(): lax.all_to_all(outgoing.reshape((tile_count, capacity) + outgoing.shape[1...]
    dot_general x8 -> x0, matrix products: 118 us -> none  [resample(): jnp.einsum('ik,bko->bio', row_kernel, across, preferred_element_type=jnp....]
    pallas_call x0 -> x10, Pallas kernels: none -> 61.2 us  [the longest x5 44.4 us: render(): pl.pallas_call(functools.partial(render_kernel, local_count, first, bands...]
    another operation x3 -> x0, local copies, waits for them, and re-layouts: 36.1 us -> none  [the longest x1 35.9 us: local(): outgoing.reshape((tile_count, capacity) + block_shape)]
    ppermute x2 -> x6, waiting for transfers between devices: 69.8 us -> 82.7 us  [passed_along(): lax.ppermute(value, axis, [(source, source + steps) for source in range(i...]
  transfers between devices with their start and end apart: 3 -> 11, of which waited for: 2 -> 9; matrix products, arithmetic and copies ran while one was open for 1% -> 2% of each run, Pallas kernels for 0% -> 9%
where the time goes in v1:
time: 574 us; the launch traced here: 568 us
  waiting for transfers between devices  305 us (53%)
  starting transfers between devices  180 us (31%)
  Pallas kernels  61.2 us (11%)
  local copies, waits for them, and re-layouts  12.5 us (2%)
    all_to_all x5, waiting for transfers between devices, local(): lax.all_to_all(outgoing.reshape((tile_count, capacity) + outgoing.shape[1...  222 us
    all_to_all x5, starting transfers between devices, local(): lax.all_to_all(outgoing.reshape((tile_count, capacity) + outgoing.shape[1...  173 us
    ppermute x6, waiting for transfers between devices, passed_along(): lax.ppermute(value, axis, [(source, source + steps) for source in range(i...  82.7 us
    pallas_call x5, Pallas kernels, render(): pl.pallas_call(functools.partial(render_kernel, local_count, first, bands...  44.4 us
    pallas_call x5, Pallas kernels, place(): pl.pallas_call(functools.partial(place_kernel, first, bands), out_shape=j...  16.8 us
  transfers between devices with their start and end apart: 11, of which 9 were waited for; matrix products, arithmetic and copies ran while one was open for 2% of the time, Pallas kernels for 9%

profile of v1, /device:TPU:60, one launch (start us, length us, event | category | flops | bytes accessed | tf_op | source)
XLA Modules:
  0.0 567.6 jit_solution(14626569962119336057)
XLA Ops:
  0.0 1.3 collective-permute-start
  1.3 1.4 fusion.3
  5.2 1.0 slice.35
  7.6 1.3 collective-permute-start.5
  8.9 1.3 convert_reduce_fusion.3
  10.2 0.1 reshape.123
  10.3 0.1 copy.16
  10.4 0.1 select_reduce_fusion.2
  10.5 0.2 convert_reduce_fusion
  10.7 0.1 iota_add_fusion
  10.8 0.1 copy.17
  10.9 0.1 copy.18
  10.9 0.9 copy.19
  11.8 0.8 reshape.124.offsets_ref
  12.6 0.9 copy.20
  13.5 0.8 reshape.125.fractions_ref
  14.3 1.0 select_reduce_fusion
  15.4 0.0 collective-permute-done
  15.4 0.6 pad_add_fusion.listed_ref
  16.0 2.1 collective-permute-done.5.near_ref
  18.1 0.7 copy-done.5
  18.8 6.4 %render.9 = bf16[64,1,128,128]{3,2,1,0:T(8,128)(2,1)} custom-call(s32[1]{0:T(128)} %bitcast.1.count_ref, s32[64]{0:T(128)} %get-tuple-element.6.blocks_ref, s32[64]{0:T(128)} %get-tuple-element.5.slots_ref, s32[768]{0:T(1024)} %source_ref.9, s32[1536]{0:T(1024)} %reshape.124.offsets_ref, f32[1536]{0:T(1024)} %reshape.125.fractions_ref, f32[768]{0:T(1024)} %blend_ref.9, ...), custom_call_target="tpu_custom_call" | custom-call | flops 4831838208 | bytes 786432 | tf_op jit(solution)/shard_map/render/pallas_call | solution.py:102
  25.2 0.0 slice-start
  25.2 38.3 %all-to-all-start.4 = ((bf16[32,2,1,128,128]{4,3,1,2,0:T(8,128)(2,1)}), bf16[32,2,1,128,128]{4,3,1,2,0:T(8,128)(2,1)S(1)}, u32[]{:S(2)}, u32[]{:S(2)}) async-start(bf16[32,2,1,128,128]{4,3,1,2,0:T(8,128)(2,1)} %bitcast.25), calls=%async_computation.4 | async-start | bytes 4194304 | tf_op jit(solution)/shard_map/all_to_all | solution.py:201
  63.6 0.1 pad_maximum_fusion.3
  63.7 1.3 collective-permute-start.4
  65.0 14.5 %collective-permute-done.4.near_ref = bf16[2,2,256,256]{3,2,1,0:T(8,128)(2,1)S(1)} collective-permute-done((bf16[2,2,256,256]{3,2,1,0:T(8,128)(2,1)S(1)}, bf16[2,2,256,256]{3,2,1,0:T(8,128)(2,1)S(1)}, u32[]{:S(2)}, u32[]{:S(2)}) %collective-permute-start.4) | collective-permute-done | bytes 524320 | tf_op jit(solution)/shard_map/ppermute | solution.py:16
  79.5 0.8 copy-done.4
  80.3 8.0 %render.8 = bf16[64,2,128,128]{3,2,1,0:T(8,128)(2,1)} custom-call(s32[1]{0:T(128)} %bitcast.1.count_ref, s32[64]{0:T(128)} %get-tuple-element.6.blocks_ref, s32[64]{0:T(128)} %get-tuple-element.5.slots_ref, s32[768]{0:T(1024)} %source_ref.9, s32[1536]{0:T(1024)} %reshape.124.offsets_ref, f32[1536]{0:T(1024)} %reshape.125.fractions_ref, f32[768]{0:T(1024)} %blend_ref.9, ...), custom_call_target="tpu_custom_call" | custom-call | flops 9663676416 | bytes 1572864 | tf_op jit(solution)/shard_map/render/pallas_call | solution.py:102
  88.3 0.0 all-to-all-done.4
  88.3 0.0 copy-start
  88.3 50.8 %all-to-all-start.3 = ((bf16[32,2,2,128,128]{4,3,2,1,0:T(8,128)(2,1)}), bf16[32,2,2,128,128]{4,3,2,1,0:T(8,128)(2,1)}, u32[]{:S(2)}, u32[]{:S(2)}) async-start(bf16[32,2,2,128,128]{4,3,2,1,0:T(8,128)(2,1)} %bitcast.24), calls=%async_computation.3 | async-start | bytes 8388608 | tf_op jit(solution)/shard_map/all_to_all | solution.py:201
  139.1 1.8 fusion.2
  140.9 0.1 constant_dynamic-slice_fusion.5
  141.1 0.1 pad_maximum_fusion.2
  141.2 1.3 collective-permute-start.3
  142.5 20.2 %collective-permute-done.3.near_ref = bf16[2,3,256,256]{3,2,1,0:T(8,128)(2,1)S(1)} collective-permute-done((bf16[2,3,256,256]{3,2,1,0:T(8,128)(2,1)S(1)}, bf16[2,3,256,256]{3,2,1,0:T(8,128)(2,1)S(1)}, u32[]{:S(2)}, u32[]{:S(2)}) %collective-permute-start.3) | collective-permute-done | bytes 786464 | tf_op jit(solution)/shard_map/ppermute | solution.py:16
  162.6 0.9 copy-done.3
  163.5 9.5 %render.7 = bf16[64,3,128,128]{3,2,1,0:T(8,128)(2,1)} custom-call(s32[1]{0:T(128)} %bitcast.1.count_ref, s32[64]{0:T(128)} %get-tuple-element.6.blocks_ref, s32[64]{0:T(128)} %get-tuple-element.5.slots_ref, s32[768]{0:T(1024)} %source_ref.9, s32[1536]{0:T(1024)} %reshape.124.offsets_ref, f32[1536]{0:T(1024)} %reshape.125.fractions_ref, f32[768]{0:T(1024)} %blend_ref.9, ...), custom_call_target="tpu_custom_call" | custom-call | flops 14495514624 | bytes 2359296 | tf_op jit(solution)/shard_map/render/pallas_call | solution.py:102
  173.0 16.3 %all-to-all-done.3 = bf16[32,2,2,128,128]{4,3,2,1,0:T(8,128)(2,1)} async-done(((bf16[32,2,2,128,128]{4,3,2,1,0:T(8,128)(2,1)}), bf16[32,2,2,128,128]{4,3,2,1,0:T(8,128)(2,1)}, u32[]{:S(2)}, u32[]{:S(2)}) %all-to-all-start.3) | async-done | bytes 4194336 | tf_op jit(solution)/shard_map/all_to_all | solution.py:201
  189.3 47.2 %all-to-all-start.2 = ((bf16[32,2,3,128,128]{4,3,2,1,0:T(8,128)(2,1)}), bf16[32,2,3,128,128]{4,3,2,1,0:T(8,128)(2,1)}, u32[]{:S(2)}, u32[]{:S(2)}) async-start(bf16[32,2,3,128,128]{4,3,2,1,0:T(8,128)(2,1)} %bitcast.23), calls=%async_computation.2 | async-start | bytes 12582912 | tf_op jit(solution)/shard_map/all_to_all | solution.py:201
  236.5 0.1 constant_dynamic-slice_fusion.7
  236.6 0.1 pad_maximum_fusion
  236.7 1.3 collective-permute-start.2
  238.0 25.8 %collective-permute-done.2.near_ref = bf16[2,4,256,256]{3,2,1,0:T(8,128)(2,1)S(1)} collective-permute-done((bf16[2,4,256,256]{3,2,1,0:T(8,128)(2,1)S(1)}, bf16[2,4,256,256]{3,2,1,0:T(8,128)(2,1)S(1)}, u32[]{:S(2)}, u32[]{:S(2)}) %collective-permute-start.2) | collective-permute-done | bytes 1048608 | tf_op jit(solution)/shard_map/ppermute | solution.py:16
  263.8 1.0 copy-done.1
  264.8 11.0 %render.6 = bf16[64,4,128,128]{3,2,1,0:T(8,128)(2,1)} custom-call(s32[1]{0:T(128)} %bitcast.1.count_ref, s32[64]{0:T(128)} %get-tuple-element.6.blocks_ref, s32[64]{0:T(128)} %get-tuple-element.5.slots_ref, s32[768]{0:T(1024)} %source_ref.9, s32[1536]{0:T(1024)} %reshape.124.offsets_ref, f32[1536]{0:T(1024)} %reshape.125.fractions_ref, f32[768]{0:T(1024)} %blend_ref.9, ...), custom_call_target="tpu_custom_call" | custom-call | flops 19327352832 | bytes 3145728 | tf_op jit(solution)/shard_map/render/pallas_call | solution.py:102
  275.9 45.7 %all-to-all-done.2 = bf16[32,2,3,128,128]{4,3,2,1,0:T(8,128)(2,1)} async-done(((bf16[32,2,3,128,128]{4,3,2,1,0:T(8,128)(2,1)}), bf16[32,2,3,128,128]{4,3,2,1,0:T(8,128)(2,1)}, u32[]{:S(2)}, u32[]{:S(2)}) %all-to-all-start.2) | async-done | bytes 6291488 | tf_op jit(solution)/shard_map/all_to_all | solution.py:201
  321.6 30.4 %all-to-all-start.1 = ((bf16[32,2,4,128,128]{4,3,2,1,0:T(8,128)(2,1)}), bf16[32,2,4,128,128]{4,3,2,1,0:T(8,128)(2,1)}, u32[]{:S(2)}, u32[]{:S(2)}) async-start(bf16[32,2,4,128,128]{4,3,2,1,0:T(8,128)(2,1)} %bitcast.20), calls=%async_computation.1 | async-start | bytes 16777216 | tf_op jit(solution)/shard_map/all_to_all | solution.py:201
  352.0 0.1 pad_maximum_fusion.1
  352.1 1.3 collective-permute-start.1
  353.4 20.2 %collective-permute-done.1.near_ref = bf16[2,3,256,256]{3,2,1,0:T(8,128)(2,1)S(1)} collective-permute-done((bf16[2,3,256,256]{3,2,1,0:T(8,128)(2,1)S(1)}, bf16[2,3,256,256]{3,2,1,0:T(8,128)(2,1)S(1)}, u32[]{:S(2)}, u32[]{:S(2)}) %collective-permute-start.1) | collective-permute-done | bytes 786464 | tf_op jit(solution)/shard_map/ppermute | solution.py:16
  373.5 0.9 copy-done.2
  374.4 9.5 %render.5 = bf16[64,3,128,128]{3,2,1,0:T(8,128)(2,1)} custom-call(s32[1]{0:T(128)} %bitcast.1.count_ref, s32[64]{0:T(128)} %get-tuple-element.6.blocks_ref, s32[64]{0:T(128)} %get-tuple-element.5.slots_ref, s32[768]{0:T(1024)} %source_ref.9, s32[1536]{0:T(1024)} %reshape.124.offsets_ref, f32[1536]{0:T(1024)} %reshape.125.fractions_ref, f32[768]{0:T(1024)} %blend_ref.9, ...), custom_call_target="tpu_custom_call" | custom-call | flops 14495514624 | bytes 2359296 | tf_op jit(solution)/shard_map/render/pallas_call | solution.py:102
  383.9 89.8 %all-to-all-done.1 = bf16[32,2,4,128,128]{4,3,2,1,0:T(8,128)(2,1)} async-done(((bf16[32,2,4,128,128]{4,3,2,1,0:T(8,128)(2,1)}), bf16[32,2,4,128,128]{4,3,2,1,0:T(8,128)(2,1)}, u32[]{:S(2)}, u32[]{:S(2)}) %all-to-all-start.1) | async-done | bytes 8388640 | tf_op jit(solution)/shard_map/all_to_all | solution.py:201
  473.7 6.0 %all-to-all-start = ((bf16[32,2,3,128,128]{4,3,2,1,0:T(8,128)(2,1)}), bf16[32,2,3,128,128]{4,3,2,1,0:T(8,128)(2,1)}, u32[]{:S(2)}, u32[]{:S(2)}) async-start(bf16[32,2,3,128,128]{4,3,2,1,0:T(8,128)(2,1)} %bitcast.22), calls=%async_computation | async-start | bytes 12582912 | tf_op jit(solution)/shard_map/all_to_all | solution.py:201
  479.7 0.2 convert_reduce_fusion.2
  479.9 0.6 multiply_add_fusion.pick_ref
  480.5 2.8 place.5.refs_0_
  483.3 3.1 place.6.refs_0_
  486.4 3.5 place.7.refs_0_
  489.9 3.9 place.8.refs_0_
  493.8 70.3 %all-to-all-done = bf16[32,2,3,128,128]{4,3,2,1,0:T(8,128)(2,1)} async-done(((bf16[32,2,3,128,128]{4,3,2,1,0:T(8,128)(2,1)}), bf16[32,2,3,128,128]{4,3,2,1,0:T(8,128)(2,1)}, u32[]{:S(2)}, u32[]{:S(2)}) %all-to-all-start) | async-done | bytes 6291488 | tf_op jit(solution)/shard_map/all_to_all | solution.py:201
  564.2 3.5 place.9
  (18 shorter events, 0.2 us)
Async XLA Ops:
  0.0 15.4 %collective-permute-start = (s32[2]{0:T(128)}, s32[2]{0:T(128)S(1)}, u32[]{:S(2)}, u32[]{:S(2)}) collective-permute-start(s32[2]{0:T(128)} %param.7), channel_id=1, source_target_pairs={{0,32},{32,64},{64,96},{1,33},{33,65},{65,97},{2,34},{34,66},{66,9... | collective-permute-start | bytes 32 | tf_op jit(solution)/shard_map/ppermute | solution.py:16
  7.6 10.5 %collective-permute-start.5 = (bf16[2,1,256,256]{3,2,1,0:T(8,128)(2,1)S(1)}, bf16[2,1,256,256]{3,2,1,0:T(8,128)(2,1)S(1)}, u32[]{:S(2)}, u32[]{:S(2)}) collective-permute-start(bf16[2,1,256,256]{3,2,1,0:T(8,128)(2,1)S(1)} %pad_maximum_fusion.4), channel_id=1, source_target_pairs={{0,32},{32,64},{64,96},{1,33},{33,65},{65,97},{2,34},{34,66},{66,9... | collective-permute-start | bytes 786440 | tf_op jit(solution)/shard_map/ppermute | solution.py:16
  18.1 0.7 copy-start.5
  25.2 38.4 %slice-start = ((bf16[3,13,256,256]{3,2,1,0:T(8,128)(2,1)}), bf16[3,2,256,256]{3,2,1,0:T(8,128)(2,1)S(1)}, s32[]{:S(2)}) async-start(bf16[3,13,256,256]{3,2,1,0:T(8,128)(2,1)} %tiles_ref.9), calls=%async_computation.5 | async-start | bytes 1572864 | tf_op jit(solution)/shard_map/slice | solution.py:195
  25.2 63.1 %all-to-all-start.4 = ((bf16[32,2,1,128,128]{4,3,1,2,0:T(8,128)(2,1)}), bf16[32,2,1,128,128]{4,3,1,2,0:T(8,128)(2,1)S(1)}, u32[]{:S(2)}, u32[]{:S(2)}) async-start(bf16[32,2,1,128,128]{4,3,1,2,0:T(8,128)(2,1)} %bitcast.25), calls=%async_computation.4 | async-start | bytes 4194304 | tf_op jit(solution)/shard_map/all_to_all | solution.py:201
  63.7 15.8 %collective-permute-start.4 = (bf16[2,2,256,256]{3,2,1,0:T(8,128)(2,1)S(1)}, bf16[2,2,256,256]{3,2,1,0:T(8,128)(2,1)S(1)}, u32[]{:S(2)}, u32[]{:S(2)}) collective-permute-start(bf16[2,2,256,256]{3,2,1,0:T(8,128)(2,1)S(1)} %pad_maximum_fusion.3), channel_id=1, source_target_pairs={{0,32},{32,64},{64,96},{1,33},{33,65},{65,97},{2,34},{34,66},{66,9... | collective-permute-start | bytes 1572872 | tf_op jit(solution)/shard_map/ppermute | solution.py:16
  79.5 0.8 copy-start.4
  88.3 52.6 %copy-start = (bf16[32,2,1,128,128]{4,3,1,2,0:T(8,128)(2,1)}, bf16[32,2,1,128,128]{4,3,1,2,0:T(8,128)(2,1)S(1)}, u32[]{:S(2)}) copy-start(bf16[32,2,1,128,128]{4,3,1,2,0:T(8,128)(2,1)S(1)} %all-to-all-done.4) | copy-start | bytes 6291460
  88.3 101.0 %all-to-all-start.3 = ((bf16[32,2,2,128,128]{4,3,2,1,0:T(8,128)(2,1)}), bf16[32,2,2,128,128]{4,3,2,1,0:T(8,128)(2,1)}, u32[]{:S(2)}, u32[]{:S(2)}) async-start(bf16[32,2,2,128,128]{4,3,2,1,0:T(8,128)(2,1)} %bitcast.24), calls=%async_computation.3 | async-start | bytes 8388608 | tf_op jit(solution)/shard_map/all_to_all | solution.py:201
  141.2 21.5 %collective-permute-start.3 = (bf16[2,3,256,256]{3,2,1,0:T(8,128)(2,1)S(1)}, bf16[2,3,256,256]{3,2,1,0:T(8,128)(2,1)S(1)}, u32[]{:S(2)}, u32[]{:S(2)}) collective-permute-start(bf16[2,3,256,256]{3,2,1,0:T(8,128)(2,1)S(1)} %pad_maximum_fusion.2), channel_id=1, source_target_pairs={{0,32},{32,64},{64,96},{1,33},{33,65},{65,97},{2,34},{34,66},{66,9... | collective-permute-start | bytes 2359304 | tf_op jit(solution)/shard_map/ppermute | solution.py:16
  162.6 0.9 copy-start.3
  189.3 47.2 %slice-start.1 = ((bf16[3,13,256,256]{3,2,1,0:T(8,128)(2,1)}), bf16[3,4,256,256]{3,2,1,0:T(8,128)(2,1)S(1)}, s32[]{:S(2)}) async-start(bf16[3,13,256,256]{3,2,1,0:T(8,128)(2,1)} %tiles_ref.9), calls=%async_computation.6 | async-start | bytes 3145728 | tf_op jit(solution)/shard_map/slice | solution.py:195
  189.3 132.3 %all-to-all-start.2 = ((bf16[32,2,3,128,128]{4,3,2,1,0:T(8,128)(2,1)}), bf16[32,2,3,128,128]{4,3,2,1,0:T(8,128)(2,1)}, u32[]{:S(2)}, u32[]{:S(2)}) async-start(bf16[32,2,3,128,128]{4,3,2,1,0:T(8,128)(2,1)} %bitcast.23), calls=%async_computation.2 | async-start | bytes 12582912 | tf_op jit(solution)/shard_map/all_to_all | solution.py:201
  236.7 27.1 %collective-permute-start.2 = (bf16[2,4,256,256]{3,2,1,0:T(8,128)(2,1)S(1)}, bf16[2,4,256,256]{3,2,1,0:T(8,128)(2,1)S(1)}, u32[]{:S(2)}, u32[]{:S(2)}) collective-permute-start(bf16[2,4,256,256]{3,2,1,0:T(8,128)(2,1)S(1)} %pad_maximum_fusion), channel_id=1, source_target_pairs={{0,32},{32,64},{64,96},{1,33},{33,65},{65,97},{2,34},{34,66},{66,9... | collective-permute-start | bytes 3145736 | tf_op jit(solution)/shard_map/ppermute | solution.py:16
  263.8 1.0 copy-start.1
  321.6 152.1 %all-to-all-start.1 = ((bf16[32,2,4,128,128]{4,3,2,1,0:T(8,128)(2,1)}), bf16[32,2,4,128,128]{4,3,2,1,0:T(8,128)(2,1)}, u32[]{:S(2)}, u32[]{:S(2)}) async-start(bf16[32,2,4,128,128]{4,3,2,1,0:T(8,128)(2,1)} %bitcast.20), calls=%async_computation.1 | async-start | bytes 16777216 | tf_op jit(solution)/shard_map/all_to_all | solution.py:201
  352.1 21.5 %collective-permute-start.1 = (bf16[2,3,256,256]{3,2,1,0:T(8,128)(2,1)S(1)}, bf16[2,3,256,256]{3,2,1,0:T(8,128)(2,1)S(1)}, u32[]{:S(2)}, u32[]{:S(2)}) collective-permute-start(bf16[2,3,256,256]{3,2,1,0:T(8,128)(2,1)S(1)} %pad_maximum_fusion.1), channel_id=1, source_target_pairs={{0,32},{32,64},{64,96},{1,33},{33,65},{65,97},{2,34},{34,66},{66,9... | collective-permute-start | bytes 2359304 | tf_op jit(solution)/shard_map/ppermute | solution.py:16
  373.5 0.9 copy-start.2
  473.7 90.5 %all-to-all-start = ((bf16[32,2,3,128,128]{4,3,2,1,0:T(8,128)(2,1)}), bf16[32,2,3,128,128]{4,3,2,1,0:T(8,128)(2,1)}, u32[]{:S(2)}, u32[]{:S(2)}) async-start(bf16[32,2,3,128,128]{4,3,2,1,0:T(8,128)(2,1)} %bitcast.22), calls=%async_computation | async-start | bytes 12582912 | tf_op jit(solution)/shard_map/all_to_all | solution.py:201

commit v2 on v1

--- a/solution.py
+++ b/solution.py
@@ -7,7 +7,10 @@
 from jax.experimental.pallas import tpu as pltpu
 from jax.sharding import PartitionSpec as P
 
-CHUNKS = (1, 2, 3, 4, 3)
+
+CHUNKS = (2, 4, 7)
+ABREAST = 4
+STEPS = (-1, 0, 1, 2)
 
 
 def passed_along(value, axis, steps):
@@ -24,75 +27,71 @@
 
 
 def render_kernel(
-    local_count, first, bands, count_ref, blocks_ref, slots_ref, source_ref, offsets_ref, fractions_ref, blend_ref,
-    listed_ref, tiles_ref, near_ref, out_ref, held, beside, done, in_sem, out_sem,
+    local_count, first, bands, count_ref, blocks_ref, slots_ref, source_ref, offsets_ref, taps_ref, blend_ref,
+    listed_ref, tiles_ref, near_ref, out_ref, held, beside, row_lag, col_lag, done, in_sem, out_sem,
 ):
     load = pltpu.make_async_copy(tiles_ref.at[:, pl.ds(first, bands)], held, in_sem.at[0])
     load_near = pltpu.make_async_copy(near_ref, beside, in_sem.at[1])
     load.start()
     load_near.start()
+    height, width = held.shape[2], held.shape[3]
+    row_lag[...] = lax.broadcasted_iota(jnp.int32, row_lag.shape, 1) - 2 * lax.broadcasted_iota(jnp.int32, row_lag.shape, 0)
+    col_lag[...] = lax.broadcasted_iota(jnp.int32, col_lag.shape, 0) - 2 * lax.broadcasted_iota(jnp.int32, col_lag.shape, 1)
     load.wait()
     load_near.wait()
-    height, width = held.shape[2], held.shape[3]
     count = count_ref[0]
 
-    def store(index, way):
+    def store(index):
+        way = lax.rem(index, 2 * ABREAST)
         return pltpu.make_async_copy(done.at[way], out_ref.at[slots_ref[index]], out_sem.at[way])
 
-    def taps(shape, out_dim, shift):
-        out_pos = lax.broadcasted_iota(jnp.int32, shape, out_dim).astype(jnp.float32)
-        in_pos = lax.broadcasted_iota(jnp.int32, shape, 1 - out_dim).astype(jnp.float32)
-        return cubic_weight(in_pos - (2.0 * out_pos + shift)).astype(jnp.bfloat16)
-
-    def one(index, carry):
-        way = lax.rem(index, 2)
+    def kernel_matrix(lag_ref, block, axis):
+        lag = lag_ref[...] - offsets_ref[2 * block + axis]
+        kernel = jnp.zeros(lag.shape, jnp.float32)
+        for place, step in enumerate(STEPS):
+            kernel = jnp.where(lag == step, taps_ref[(len(STEPS) * axis + place) * source_ref.shape[0] + block], kernel)
+        return kernel.astype(jnp.bfloat16)
+
+    def render_one(index):
         block = blocks_ref[index]
         tile = lax.rem(source_ref[block], local_count)
         second = listed_ref[1] == tile
         flagged = (second | (listed_ref[0] == tile)) & (listed_ref[2] > 0)
         place = jnp.where(second, 1, 0)
         weight = jnp.where(flagged, blend_ref[block], 0.0)
-        row_kernel = taps(
-            (height // 2, height), 0, offsets_ref[2 * block].astype(jnp.float32) + fractions_ref[2 * block]
-        )
-        col_kernel = taps(
-            (width, width // 2), 1, offsets_ref[2 * block + 1].astype(jnp.float32) + fractions_ref[2 * block + 1]
-        )
-
-        @pl.when(index >= 2)
-        def _():
-            store(index - 2, way).wait()
-
-        def resample(mixed, band):
-            across = jnp.dot(mixed, col_kernel, preferred_element_type=jnp.float32).astype(jnp.bfloat16)
-            result = jnp.dot(row_kernel, across, preferred_element_type=jnp.float32)
-            done[way, band] = result.astype(jnp.bfloat16)
-
-        @pl.when(weight == 0.0)
-        def _():
-            for band in range(bands):
-                resample(held[tile, band], band)
-
-        @pl.when(weight != 0.0)
-        def _():
-            for band in range(bands):
-                mixed = (1.0 - weight) * held[tile, band].astype(jnp.float32) + weight * beside[
-                    place, band
-                ].astype(jnp.float32)
-                resample(mixed.astype(jnp.bfloat16), band)
-
-        store(index, way).start()
+        row_kernel = kernel_matrix(row_lag, block, 0)
+        col_kernel = kernel_matrix(col_lag, block, 1)
+        mixed = (1.0 - weight) * held[tile].astype(jnp.float32) + weight * beside[place].astype(jnp.float32)
+        mixed = mixed.astype(jnp.bfloat16).reshape(bands * height, width)
+        across = jnp.dot(mixed, col_kernel, preferred_element_type=jnp.float32).astype(jnp.bfloat16)
+        beside_each = jnp.concatenate([across[b * height : (b + 1) * height] for b in range(bands)], axis=1)
+        return jnp.dot(row_kernel, beside_each, preferred_element_type=jnp.float32).astype(jnp.bfloat16)
+
+    def some(turn, carry):
+        start = turn * ABREAST
+        for ahead in range(ABREAST):
+            @pl.when(turn >= 2)
+            def _():
+                store(start + ahead - 2 * ABREAST).wait()
+        results = [render_one(jnp.minimum(start + ahead, count - 1)) for ahead in range(ABREAST)]
+        for ahead in range(ABREAST):
+            way = lax.rem(start + ahead, 2 * ABREAST)
+            for b in range(bands):
+                done[way, b] = results[ahead][:, b * (width // 2) : (b + 1) * (width // 2)]
+        for ahead in range(ABREAST):
+            @pl.when(start + ahead < count)
+            def _():
+                store(start + ahead).start()
         return carry
 
-    lax.fori_loop(0, count, one, 0)
-
-    @pl.when(count >= 2)
-    def _():
-        store(count - 2, lax.rem(count, 2)).wait()
-
-    @pl.when(count >= 1)
-    def _():
-        store(count - 1, lax.rem(count + 1, 2)).wait()
+    turns = lax.div(count + ABREAST - 1, ABREAST)
+    lax.fori_loop(0, turns, some, 0)
+
+    def drain(index, carry):
+        store(index).wait()
+        return carry
+
+    lax.fori_loop(jnp.maximum(turns - 2, 0) * ABREAST, count, drain, 0)
 
 
 def render(scalars, tiles, near, first, bands, slots):
@@ -107,9 +106,11 @@
         scratch_shapes=[
             pltpu.VMEM((local_count, bands, height, width), jnp.bfloat16),
             pltpu.VMEM((near.shape[0], bands, height, width), jnp.bfloat16),
-            pltpu.VMEM((2,) + block, jnp.bfloat16),
+            pltpu.VMEM((height // 2, height), jnp.int32),
+            pltpu.VMEM((width, width // 2), jnp.int32),
+            pltpu.VMEM((2 * ABREAST,) + block, jnp.bfloat16),
             pltpu.SemaphoreType.DMA((2,)),
-            pltpu.SemaphoreType.DMA((2,)),
+            pltpu.SemaphoreType.DMA((2 * ABREAST,)),
         ],
         cost_estimate=pl.CostEstimate(flops=8 * flops, bytes_accessed=24 * bands * height * width // 2, transcendentals=0),
         name="render",
@@ -187,22 +188,31 @@
     own_rank = jnp.sum(((own[:, None] == own[None, :]) & earlier).astype(jnp.int32), axis=1)
     pick = own * capacity + own_rank
 
-    scalars = (count, blocks, into, source, offsets.reshape(-1), fractions.reshape(-1), blend, listed)
+    taps = jnp.concatenate([cubic_weight(step - fractions[:, axis]) for axis in range(2) for step in STEPS])
+    scalars = (count, blocks, into, source, offsets.reshape(-1), taps, blend, listed)
     shape = (per_owner, band_count, height // 2, width // 2)
+    starts = [sum(CHUNKS[:part]) for part in range(len(CHUNKS))]
+    nears = []
+    for first, bands in zip(starts, CHUNKS):
+        picked = jnp.concatenate(
+            [
+                lax.dynamic_slice(tiles, (seam_list[i], first, 0, 0), (1, bands, height, width))
+                for i in range(seam_list.shape[0])
+            ],
+            axis=0,
+        )
+        nears.append(passed_along(picked, "zone", 1))
     output = None
-    first = 0
-    for bands in CHUNKS:
-        part = tiles[:, first : first + bands]
-        picked = jnp.concatenate(
-            [lax.dynamic_index_in_dim(part, seam_list[i], 0) for i in range(seam_list.shape[0])], axis=0
-        )
-        near = passed_along(picked, "zone", 1)
-        outgoing = render(scalars, tiles, near, first, bands, slots)
+    for part, (first, bands) in enumerate(zip(starts, CHUNKS)):
+        outgoing = render(scalars, tiles, nears[part], first, bands, slots)
         incoming = lax.all_to_all(
-            outgoing.reshape((tile_count, capacity) + outgoing.shape[1:]), "tile", split_axis=0, concat_axis=0, tiled=True
+            outgoing.reshape((tile_count, capacity) + outgoing.shape[1:]),
+            "tile",
+            split_axis=0,
+            concat_axis=0,
+            tiled=True,
         )
         output = place(pick, incoming.reshape((slots,) + outgoing.shape[1:]), output, first, shape)
-        first += bands
     return output
 
 

time: 574 us -> 495 us (0.86)
  starting transfers between devices: 180 us -> 26.5 us
  Pallas kernels: 61.2 us -> 122 us
  waiting for transfers between devices: 305 us -> 324 us
    all_to_all x5 -> x3, starting transfers between devices: 173 us -> 21.3 us  [local(): lax.all_to_all(outgoing.reshape((tile_count, capacity) + outgoing.shape[1...]
    pallas_call x5 -> x3, Pallas kernels: 44.4 us -> 109 us  [render(): pl.pallas_call(functools.partial(render_kernel, local_count, first, bands...]
    all_to_all x5 -> x3, waiting for transfers between devices: 222 us -> 248 us  [local(): lax.all_to_all(outgoing.reshape((tile_count, capacity) + outgoing.shape[1...]
    ppermute x6 -> x4, waiting for transfers between devices: 82.7 us -> 76.7 us  [passed_along(): lax.ppermute(value, axis, [(source, source + steps) for source in range(i...]
    pallas_call x5 -> x3, Pallas kernels: 16.8 us -> 12.9 us  [place(): pl.pallas_call(functools.partial(place_kernel, first, bands), out_shape=j...]
  transfers between devices with their start and end apart: 11 -> 7, of which waited for: 9 -> 5; matrix products, arithmetic and copies ran while one was open for 2% -> 3% of each run, Pallas kernels for 9% -> 18%
where the time goes in v2:
time: 495 us; the launch traced here: 493 us
  waiting for transfers between devices  324 us (65%)
  Pallas kernels  122 us (25%)
  starting transfers between devices  26.5 us (5%)
  local copies, waits for them, and re-layouts  10.3 us (2%)
  other arithmetic  5.47 us (1%)
    all_to_all x3, waiting for transfers between devices, local(): lax.all_to_all(outgoing.reshape((tile_count, capacity) + outgoing.shape[1...  248 us
    pallas_call x3, Pallas kernels, render(): pl.pallas_call(functools.partial(render_kernel, local_count, first, bands...  109 us
    ppermute x4, waiting for transfers between devices, passed_along(): lax.ppermute(value, axis, [(source, source + steps) for source in range(i...  76.7 us
    all_to_all x3, starting transfers between devices, local(): lax.all_to_all(outgoing.reshape((tile_count, capacity) + outgoing.shape[1...  21.3 us
    pallas_call x3, Pallas kernels, place(): pl.pallas_call(functools.partial(place_kernel, first, bands), out_shape=j...  12.9 us
  transfers between devices with their start and end apart: 7, of which 5 were waited for; matrix products, arithmetic and copies ran while one was open for 3% of the time, Pallas kernels for 18%

profile of v2, /device:TPU:60, one launch (start us, length us, event | category | flops | bytes accessed | tf_op | source)
XLA Modules:
  0.0 492.9 jit_solution(2175724083578682722)
XLA Ops:
  0.0 1.3 collective-permute-start
  1.3 1.4 fusion.26
  6.7 1.1 constant_dynamic-slice_fusion.1
  7.8 0.1 pad_maximum_fusion.2
  7.8 1.3 collective-permute-start.3
  9.2 1.4 convert_reduce_fusion.3
  10.6 0.1 reshape.132
  10.7 0.1 copy.10
  10.8 0.1 select_reduce_fusion.2
  10.9 0.2 convert_reduce_fusion
  11.1 0.1 copy.11
  11.2 0.1 iota_add_fusion
  11.2 0.1 copy.12
  11.3 0.8 abs_reduce_fusion
  12.2 0.9 copy.13
  13.0 0.8 reshape.133.offsets_ref
  13.9 1.1 select_reduce_fusion
  15.0 0.0 copy-start.3
  15.0 0.0 collective-permute-done
  15.1 0.7 pad_add_fusion.listed_ref
  15.7 8.3 %collective-permute-done.3.near_ref = bf16[2,2,256,256]{3,2,1,0:T(8,128)(2,1)S(1)} collective-permute-done((bf16[2,2,256,256]{3,2,1,0:T(8,128)(2,1)S(1)}, bf16[2,2,256,256]{3,2,1,0:T(8,128)(2,1)S(1)}, u32[]{:S(2)}, u32[]{:S(2)}) %collective-permute-start.3) | collective-permute-done | bytes 524320 | tf_op jit(solution)/shard_map/ppermute | solution.py:19
  24.0 0.0 copy-start.2
  24.0 0.0 copy-done.3
  24.0 0.8 copy-done.2
  24.8 25.4 %render.5 = bf16[64,2,128,128]{3,2,1,0:T(8,128)(2,1)} custom-call(s32[1]{0:T(128)} %bitcast.1.count_ref, s32[64]{0:T(128)} %get-tuple-element.6.blocks_ref, s32[64]{0:T(128)} %get-tuple-element.5.slots_ref, s32[768]{0:T(1024)} %source_ref.5, s32[1536]{0:T(1024)} %reshape.133.offsets_ref, f32[6144]{0:T(1024)} %copy-done.3, f32[768]{0:T(1024)} %blend_ref.5, ...), custom_call_target="tpu_custom_call" | custom-call | flops 9663676416 | bytes 1572864 | tf_op jit(solution)/shard_map/render/pallas_call | solution.py:101
  50.1 7.9 %all-to-all-start.2 = ((bf16[32,2,2,128,128]{4,3,2,1,0:T(8,128)(2,1)}), bf16[32,2,2,128,128]{4,3,2,1,0:T(8,128)(2,1)}, u32[]{:S(2)}, u32[]{:S(2)}) async-start(bf16[32,2,2,128,128]{4,3,2,1,0:T(8,128)(2,1)} %bitcast.16), calls=%async_computation.2 | async-start | bytes 8388608 | tf_op jit(solution)/shard_map/all_to_all | solution.py:208
  58.0 1.3 constant_dynamic-slice_fusion.3
  59.3 0.1 pad_maximum_fusion.1
  59.4 1.3 collective-permute-start.2
  60.7 25.8 %collective-permute-done.2.near_ref = bf16[2,4,256,256]{3,2,1,0:T(8,128)(2,1)S(1)} collective-permute-done((bf16[2,4,256,256]{3,2,1,0:T(8,128)(2,1)S(1)}, bf16[2,4,256,256]{3,2,1,0:T(8,128)(2,1)S(1)}, u32[]{:S(2)}, u32[]{:S(2)}) %collective-permute-start.2) | collective-permute-done | bytes 1048608 | tf_op jit(solution)/shard_map/ppermute | solution.py:19
  86.5 0.0 copy-start.1
  86.5 1.0 copy-done.1
  87.5 34.6 %render.4 = bf16[64,4,128,128]{3,2,1,0:T(8,128)(2,1)} custom-call(s32[1]{0:T(128)} %bitcast.1.count_ref, s32[64]{0:T(128)} %get-tuple-element.6.blocks_ref, s32[64]{0:T(128)} %get-tuple-element.5.slots_ref, s32[768]{0:T(1024)} %source_ref.5, s32[1536]{0:T(1024)} %reshape.133.offsets_ref, f32[6144]{0:T(1024)} %copy-done.3, f32[768]{0:T(1024)} %blend_ref.5, ...), custom_call_target="tpu_custom_call" | custom-call | flops 19327352832 | bytes 3145728 | tf_op jit(solution)/shard_map/render/pallas_call | solution.py:101
  122.1 0.0 all-to-all-done.2
  122.1 7.5 %all-to-all-start.1 = ((bf16[32,2,4,128,128]{4,3,2,1,0:T(8,128)(2,1)}), bf16[32,2,4,128,128]{4,3,2,1,0:T(8,128)(2,1)}, u32[]{:S(2)}, u32[]{:S(2)}) async-start(bf16[32,2,4,128,128]{4,3,2,1,0:T(8,128)(2,1)} %bitcast.15), calls=%async_computation.1 | async-start | bytes 16777216 | tf_op jit(solution)/shard_map/all_to_all | solution.py:208
  129.5 1.6 constant_dynamic-slice_fusion.5
  131.1 0.2 pad_maximum_fusion
  131.3 1.3 collective-permute-start.1
  132.6 42.6 %collective-permute-done.1.near_ref = bf16[2,7,256,256]{3,2,1,0:T(8,128)(2,1)S(1)} collective-permute-done((bf16[2,7,256,256]{3,2,1,0:T(8,128)(2,1)S(1)}, bf16[2,7,256,256]{3,2,1,0:T(8,128)(2,1)S(1)}, u32[]{:S(2)}, u32[]{:S(2)}) %collective-permute-start.1) | collective-permute-done | bytes 1835040 | tf_op jit(solution)/shard_map/ppermute | solution.py:19
  175.2 0.0 copy-start
  175.2 1.2 copy-done
  176.5 49.2 %render.3 = bf16[64,7,128,128]{3,2,1,0:T(8,128)(2,1)} custom-call(s32[1]{0:T(128)} %bitcast.1.count_ref, s32[64]{0:T(128)} %get-tuple-element.6.blocks_ref, s32[64]{0:T(128)} %get-tuple-element.5.slots_ref, s32[768]{0:T(1024)} %source_ref.5, s32[1536]{0:T(1024)} %reshape.133.offsets_ref, f32[6144]{0:T(1024)} %copy-done.3, f32[768]{0:T(1024)} %blend_ref.5, ...), custom_call_target="tpu_custom_call" | custom-call | flops 33822867456 | bytes 5505024 | tf_op jit(solution)/shard_map/render/pallas_call | solution.py:101
  225.7 25.5 %all-to-all-done.1 = bf16[32,2,4,128,128]{4,3,2,1,0:T(8,128)(2,1)} async-done(((bf16[32,2,4,128,128]{4,3,2,1,0:T(8,128)(2,1)}), bf16[32,2,4,128,128]{4,3,2,1,0:T(8,128)(2,1)}, u32[]{:S(2)}, u32[]{:S(2)}) %all-to-all-start.1) | async-done | bytes 8388640 | tf_op jit(solution)/shard_map/all_to_all | solution.py:208
  251.2 6.0 %all-to-all-start = ((bf16[32,2,7,128,128]{4,3,2,1,0:T(8,128)(2,1)}), bf16[32,2,7,128,128]{4,3,2,1,0:T(8,128)(2,1)}, u32[]{:S(2)}, u32[]{:S(2)}) async-start(bf16[32,2,7,128,128]{4,3,2,1,0:T(8,128)(2,1)} %bitcast.14), calls=%async_computation | async-start | bytes 29360128 | tf_op jit(solution)/shard_map/all_to_all | solution.py:208
  257.2 0.2 convert_reduce_fusion.2
  257.4 0.5 multiply_add_fusion.pick_ref
  257.9 3.1 place.3.refs_0_
  261.1 3.9 place.4.refs_0_
  265.0 222.1 %all-to-all-done = bf16[32,2,7,128,128]{4,3,2,1,0:T(8,128)(2,1)} async-done(((bf16[32,2,7,128,128]{4,3,2,1,0:T(8,128)(2,1)}), bf16[32,2,7,128,128]{4,3,2,1,0:T(8,128)(2,1)}, u32[]{:S(2)}, u32[]{:S(2)}) %all-to-all-start) | async-done | bytes 14680096 | tf_op jit(solution)/shard_map/all_to_all | solution.py:208
  487.1 5.9 %place.5 = bf16[24,13,128,128]{3,2,1,0:T(8,128)(2,1)} custom-call(s32[24]{0:T(128)} %multiply_add_fusion.pick_ref, bf16[64,7,128,128]{3,2,1,0:T(8,128)(2,1)} %bitcast.6.incoming_ref, bf16[24,13,128,128]{3,2,1,0:T(8,128)(2,1)} %place.4.refs_0_), custom_call_target="tpu_custom_call", output_to_operand_aliasing={{}: (2, {})} | custom-call | bytes 11010048 | tf_op jit(solution)/shard_map/place/pallas_call | solution.py:143
  (15 shorter events, 0.2 us)
Async XLA Ops:
  0.0 15.1 %collective-permute-start = (s32[2]{0:T(128)}, s32[2]{0:T(128)S(1)}, u32[]{:S(2)}, u32[]{:S(2)}) collective-permute-start(s32[2]{0:T(128)} %param.7), channel_id=1, source_target_pairs={{0,32},{32,64},{64,96},{1,33},{33,65},{65,97},{2,34},{34,66},{66,9... | collective-permute-start | bytes 32 | tf_op jit(solution)/shard_map/ppermute | solution.py:19
  7.8 16.2 %collective-permute-start.3 = (bf16[2,2,256,256]{3,2,1,0:T(8,128)(2,1)S(1)}, bf16[2,2,256,256]{3,2,1,0:T(8,128)(2,1)S(1)}, u32[]{:S(2)}, u32[]{:S(2)}) collective-permute-start(bf16[2,2,256,256]{3,2,1,0:T(8,128)(2,1)S(1)} %pad_maximum_fusion.2), channel_id=1, source_target_pairs={{0,32},{32,64},{64,96},{1,33},{33,65},{65,97},{2,34},{34,66},{66,9... | collective-permute-start | bytes 1572872 | tf_op jit(solution)/shard_map/ppermute | solution.py:19
  15.0 8.9 %copy-start.3 = (f32[6144]{0:T(1024)}, f32[6144]{0:T(1024)S(1)}, u32[]{:S(2)}) copy-start(f32[6144]{0:T(1024)S(1)} %fusion.23.taps_ref) | copy-start | bytes 73732
  24.0 0.8 copy-start.2
  50.1 71.9 %all-to-all-start.2 = ((bf16[32,2,2,128,128]{4,3,2,1,0:T(8,128)(2,1)}), bf16[32,2,2,128,128]{4,3,2,1,0:T(8,128)(2,1)}, u32[]{:S(2)}, u32[]{:S(2)}) async-start(bf16[32,2,2,128,128]{4,3,2,1,0:T(8,128)(2,1)} %bitcast.16), calls=%async_computation.2 | async-start | bytes 8388608 | tf_op jit(solution)/shard_map/all_to_all | solution.py:208
  59.4 27.1 %collective-permute-start.2 = (bf16[2,4,256,256]{3,2,1,0:T(8,128)(2,1)S(1)}, bf16[2,4,256,256]{3,2,1,0:T(8,128)(2,1)S(1)}, u32[]{:S(2)}, u32[]{:S(2)}) collective-permute-start(bf16[2,4,256,256]{3,2,1,0:T(8,128)(2,1)S(1)} %pad_maximum_fusion.1), channel_id=1, source_target_pairs={{0,32},{32,64},{64,96},{1,33},{33,65},{65,97},{2,34},{34,66},{66,9... | collective-permute-start | bytes 3145736 | tf_op jit(solution)/shard_map/ppermute | solution.py:19
  86.5 1.0 copy-start.1
  122.1 129.1 %all-to-all-start.1 = ((bf16[32,2,4,128,128]{4,3,2,1,0:T(8,128)(2,1)}), bf16[32,2,4,128,128]{4,3,2,1,0:T(8,128)(2,1)}, u32[]{:S(2)}, u32[]{:S(2)}) async-start(bf16[32,2,4,128,128]{4,3,2,1,0:T(8,128)(2,1)} %bitcast.15), calls=%async_computation.1 | async-start | bytes 16777216 | tf_op jit(solution)/shard_map/all_to_all | solution.py:208
  131.3 43.9 %collective-permute-start.1 = (bf16[2,7,256,256]{3,2,1,0:T(8,128)(2,1)S(1)}, bf16[2,7,256,256]{3,2,1,0:T(8,128)(2,1)S(1)}, u32[]{:S(2)}, u32[]{:S(2)}) collective-permute-start(bf16[2,7,256,256]{3,2,1,0:T(8,128)(2,1)S(1)} %pad_maximum_fusion), channel_id=1, source_target_pairs={{0,32},{32,64},{64,96},{1,33},{33,65},{65,97},{2,34},{34,66},{66,9... | collective-permute-start | bytes 5505032 | tf_op jit(solution)/shard_map/ppermute | solution.py:19
  175.2 1.2 copy-start
  251.2 235.8 %all-to-all-start = ((bf16[32,2,7,128,128]{4,3,2,1,0:T(8,128)(2,1)}), bf16[32,2,7,128,128]{4,3,2,1,0:T(8,128)(2,1)}, u32[]{:S(2)}, u32[]{:S(2)}) async-start(bf16[32,2,7,128,128]{4,3,2,1,0:T(8,128)(2,1)} %bitcast.14), calls=%async_computation | async-start | bytes 29360128 | tf_op jit(solution)/shard_map/all_to_all | solution.py:208

commit v3 on v2

v3 whole, which is shorter than its diff:
```python
import functools

import jax
import jax.numpy as jnp
from jax import lax
from jax.experimental import pallas as pl
from jax.experimental.pallas import tpu as pltpu
from jax.sharding import PartitionSpec as P


EARLY = 3
PLACE_VMEM = 16 * 1024 * 1024
ABREAST = 4
STEPS = (-1, 0, 1, 2)


def passed_along(value, axis, steps):
    count = lax.axis_size(axis)
    initial, last = (max(0, -steps), min(count, count - steps))
    return lax.ppermute(value, axis, [(source, source + steps) for source in range(initial, last)])


def cubic_weight(dist):
    mag = jnp.abs(dist)
    near = (1.5 * mag - 2.5) * mag * mag + 1.0
    far = ((-0.5 * mag + 2.5) * mag - 4.0) * mag + 2.0
    return jnp.where(mag <= 1.0, near, jnp.where(mag < 2.0, far, jnp.zeros_like(mag)))


def pick_kernel(first, bands, listed_ref, tiles_ref, picked_ref, held, in_sem, out_sem):
    count = picked_ref.shape[0]
    for index in range(count):
        pltpu.make_async_copy(
            tiles_ref.at[listed_ref[index], pl.ds(first, bands)], held.at[index], in_sem.at[index]
        ).start()
    for index in range(count):
        pltpu.make_async_copy(
            tiles_ref.at[listed_ref[index], pl.ds(first, bands)], held.at[index], in_sem.at[index]
        ).wait()
        pltpu.make_async_copy(held.at[index], picked_ref.at[index], out_sem.at[index]).start()
    for index in range(count):
        pltpu.make_async_copy(held.at[index], picked_ref.at[index], out_sem.at[index]).wait()


def pick(listed, tiles, first, bands):
    shape = (listed.shape[0], bands) + tiles.shape[2:]
    return pl.pallas_call(
        functools.partial(pick_kernel, first, bands),
        out_shape=jax.ShapeDtypeStruct(shape, tiles.dtype),
        in_specs=[pl.BlockSpec(memory_space=pltpu.SMEM), pl.BlockSpec(memory_space=pl.ANY)],
        out_specs=pl.BlockSpec(memory_space=pl.ANY),
        scratch_shapes=[
            pltpu.VMEM(shape, tiles.dtype),
            pltpu.SemaphoreType.DMA((shape[0],)),
            pltpu.SemaphoreType.DMA((shape[0],)),
        ],
        name="pick",
    )(listed, tiles)


def render_kernel(
    local_count, first, bands, seams, range_ref, blocks_ref, slots_ref, source_ref, offsets_ref, taps_ref, blend_ref,
    listed_ref, tiles_ref, *refs,
):
    if seams:
        near_ref, _, out_ref, held, beside, row_lag, col_lag, done, in_sem, out_sem = refs
        load_near = pltpu.make_async_copy(near_ref, beside, in_sem.at[1])
        load_near.start()
        start, stop = range_ref[0], range_ref[1]
    else:
        out_ref, held, row_lag, col_lag, done, in_sem, out_sem = refs
        start, stop = 0, range_ref[0]
    load = pltpu.make_async_copy(tiles_ref.at[:, pl.ds(first, bands)], held, in_sem.at[0])
    load.start()
    height, width = held.shape[2], held.shape[3]
    row_lag[...] = lax.broadcasted_iota(jnp.int32, row_lag.shape, 1) - 2 * lax.broadcasted_iota(jnp.int32, row_lag.shape, 0)
    col_lag[...] = lax.broadcasted_iota(jnp.int32, col_lag.shape, 0) - 2 * lax.broadcasted_iota(jnp.int32, col_lag.shape, 1)
    load.wait()
    if seams:
        load_near.wait()

    def store(index):
        way = lax.rem(index - start, 2 * ABREAST)
        return pltpu.make_async_copy(done.at[way], out_ref.at[slots_ref[index]], out_sem.at[way])

    def kernel_matrix(lag_ref, block, axis):
        lag = lag_ref[...] - offsets_ref[2 * block + axis]
        kernel = jnp.zeros(lag.shape, jnp.float32)
        for place, step in enumerate(STEPS):
            kernel = jnp.where(lag == step, taps_ref[(len(STEPS) * axis + place) * source_ref.shape[0] + block], kernel)
        return kernel.astype(jnp.bfloat16)

    def render_one(index):
        block = blocks_ref[index]
        tile = lax.rem(source_ref[block], local_count)
        row_kernel = kernel_matrix(row_lag, block, 0)
        col_kernel = kernel_matrix(col_lag, block, 1)
        if seams:
            place = jnp.where(listed_ref[1] == tile, 1, 0)
            weight = blend_ref[block]
            mixed = (1.0 - weight) * held[tile].astype(jnp.float32) + weight * beside[place].astype(jnp.float32)
            mixed = mixed.astype(jnp.bfloat16)
        else:
            mixed = held[tile]
        mixed = mixed.reshape(bands * height, width)
        across = jnp.dot(mixed, col_kernel, preferred_element_type=jnp.float32).astype(jnp.bfloat16)
        beside_each = jnp.concatenate([across[b * height : (b + 1) * height] for b in range(bands)], axis=1)
        return jnp.dot(row_kernel, beside_each, preferred_element_type=jnp.float32).astype(jnp.bfloat16)

    def some(turn, carry):
        begin = start + turn * ABREAST
        for ahead in range(ABREAST):

            @pl.when(turn >= 2)
            def _():
                store(begin + ahead - 2 * ABREAST).wait()

        results = [render_one(jnp.minimum(begin + ahead, stop - 1)) for ahead in range(ABREAST)]
        for ahead in range(ABREAST):
            way = lax.rem(turn, 2) * ABREAST + ahead
            for b in range(bands):
                done[way, b] = results[ahead][:, b * (width // 2) : (b + 1) * (width // 2)]
        for ahead in range(ABREAST):

            @pl.when(begin + ahead < stop)
            def _():
                store(begin + ahead).start()

        return carry

    turns = lax.div(stop - start + ABREAST - 1, ABREAST)
    lax.fori_loop(0, turns, some, 0)

    def drain(index, carry):
        store(index).wait()
        return carry

    lax.fori_loop(start + jnp.maximum(turns - 2, 0) * ABREAST, stop, drain, 0)


def render(scalars, tiles, first, bands, slots, near=None, begun=None):
    local_count, _, height, width = tiles.shape
    block = (bands, height // 2, width // 2)
    seams = near is not None
    arrays = (tiles, near, begun) if seams else (tiles,)
    flops = 12 * bands * (2 * height * width * width // 2 + height * width * height // 2)
    return pl.pallas_call(
        functools.partial(render_kernel, local_count, first, bands, seams),
        out_shape=jax.ShapeDtypeStruct((slots,) + block, jnp.bfloat16),
        in_specs=[pl.BlockSpec(memory_space=pltpu.SMEM)] * len(scalars)
        + [pl.BlockSpec(memory_space=pl.ANY)] * len(arrays),
        out_specs=pl.BlockSpec(memory_space=pl.ANY),
        scratch_shapes=[pltpu.VMEM((local_count, bands, height, width), jnp.bfloat16)]
        + ([pltpu.VMEM(near.shape, jnp.bfloat16)] if seams else [])
        + [
            pltpu.VMEM((height // 2, height), jnp.int32),
            pltpu.VMEM((width, width // 2), jnp.int32),
            pltpu.VMEM((2 * ABREAST,) + block, jnp.bfloat16),
            pltpu.SemaphoreType.DMA((2,)),
            pltpu.SemaphoreType.DMA((2 * ABREAST,)),
        ],
        input_output_aliases={len(scalars) + 2: 0} if seams else {},
        cost_estimate=pl.CostEstimate(flops=8 * flops, bytes_accessed=12 * bands * height * width // 2, transcendentals=0),
        name="seams" if seams else "render",
    )(*scalars, *arrays)


def place_kernel(taken_ref, early_ref, late_ref, out_ref, held, early_sem, late_sem, out_sem):
    count = out_ref.shape[0]
    early, late = early_ref.shape[1], late_ref.shape[1]

    def take(index):
        return pltpu.make_async_copy(
            early_ref.at[taken_ref[index]], held.at[index, pl.ds(0, early)], early_sem.at[index]
        )

    def take_late(index):
        return pltpu.make_async_copy(
            late_ref.at[taken_ref[index]], held.at[index, pl.ds(early, late)], late_sem.at[index]
        )

    def put(index):
        return pltpu.make_async_copy(held.at[index], out_ref.at[index], out_sem.at[index])

    for index in range(count):
        take(index).start()
        take_late(index).start()
    for index in range(count):
        take(index).wait()
        take_late(index).wait()
        put(index).start()
    for index in range(count):
        put(index).wait()


def place(taken, early, late, count):
    shape = (count, early.shape[1] + late.shape[1]) + early.shape[2:]
    return pl.pallas_call(
        place_kernel,
        out_shape=jax.ShapeDtypeStruct(shape, jnp.bfloat16),
        in_specs=[pl.BlockSpec(memory_space=pltpu.SMEM)] + [pl.BlockSpec(memory_space=pl.ANY)] * 2,
        out_specs=pl.BlockSpec(memory_space=pl.ANY),
        scratch_shapes=[
            pltpu.VMEM(shape, jnp.bfloat16),
            pltpu.SemaphoreType.DMA((count,)),
            pltpu.SemaphoreType.DMA((count,)),
            pltpu.SemaphoreType.DMA((count,)),
        ],
        compiler_params=pltpu.CompilerParams(vmem_limit_bytes=PLACE_VMEM),
        name="place",
    )(taken, early, late)


def swap(outgoing, capacity):
    slots = outgoing.shape[0]
    pairs = outgoing.reshape((slots // capacity, capacity) + outgoing.shape[1:])
    return lax.all_to_all(pairs, "tile", split_axis=0, concat_axis=0, tiled=True).reshape(outgoing.shape)


def local(tiles, seam_list, source, offsets, fractions, blend):
    tile_count = lax.axis_size("tile")
    myself = lax.axis_index("tile")
    zone_index = lax.axis_index("zone")
    local_count, band_count, _, _ = tiles.shape
    per_owner = source.shape[0] // tile_count
    capacity = max(2, 2 * per_owner // tile_count)
    slots = tile_count * capacity

    near_early = passed_along(pick(seam_list, tiles, 0, EARLY), "zone", 1)
    near_list = passed_along(seam_list, "zone", 1)
    near_late = passed_along(pick(seam_list, tiles, EARLY, band_count - EARLY), "zone", 1)

    tile_of = (source % local_count).reshape(tile_count, per_owner)
    src_device = (source // local_count).reshape(tile_count, per_owner)
    order_ids = jnp.arange(per_owner, dtype=jnp.int32)
    owner_ids = jnp.arange(tile_count, dtype=jnp.int32)
    mine = src_device == myself
    flagged = mine & jnp.any(tile_of[:, :, None] == near_list[None, None, :], axis=2) & (zone_index > 0)
    plain = mine & ~flagged
    earlier = order_ids[None, :] < order_ids[:, None]
    owners_ahead = owner_ids[None, :] < owner_ids[:, None]

    def place_in_line(members):
        within = jnp.sum((members[:, None, :] & earlier[None]).astype(jnp.int32), axis=2)
        each = jnp.sum(members.astype(jnp.int32), axis=1)
        ahead = jnp.sum(jnp.where(owners_ahead, each[None, :], 0), axis=1)
        return within, within + ahead[:, None], jnp.sum(each)

    plain_rank, plain_turn, plain_count = place_in_line(plain)
    seam_rank, seam_turn, seam_count = place_in_line(flagged)
    turn = jnp.where(plain, plain_turn, jnp.where(flagged, plain_count + seam_turn, -1))
    hit = turn[None] == jnp.arange(slots, dtype=jnp.int32)[:, None, None]
    block_ids = owner_ids[:, None] * per_owner + order_ids[None, :]
    slot_ids = owner_ids[:, None] * capacity + plain_rank + seam_rank
    blocks = jnp.sum(jnp.where(hit, block_ids[None], 0), axis=(1, 2))
    into = jnp.sum(jnp.where(hit, slot_ids[None], 0), axis=(1, 2))
    ranges = jnp.stack([plain_count, plain_count + seam_count])

    own = lax.dynamic_index_in_dim(src_device, myself, 0, keepdims=False)
    own_rank = jnp.sum(((own[:, None] == own[None, :]) & earlier).astype(jnp.int32), axis=1)
    taken = own * capacity + own_rank

    taps = jnp.concatenate([cubic_weight(step - fractions[:, axis]) for axis in range(2) for step in STEPS])
    scalars = (ranges, blocks, into, source, offsets.reshape(-1), taps, blend, near_list)
    outgoing = render(scalars, tiles, 0, EARLY, slots)
    outgoing = render(scalars, tiles, 0, EARLY, slots, near_early, outgoing)
    early = swap(outgoing, capacity)
    outgoing = render(scalars, tiles, EARLY, band_count - EARLY, slots)
    outgoing = render(scalars, tiles, EARLY, band_count - EARLY, slots, near_late, outgoing)
    outgoing, taken = lax.optimization_barrier((outgoing, taken))
    late = swap(outgoing, capacity)
    return place(taken, early, late, per_owner)


def solution(mesh):
    in_specs = (
        P(("zone", "tile"), None, None, None),
        P(("zone", "tile")),
        P("zone"),
        P("zone", None),
        P("zone", None),
        P("zone"),
    )
    out_specs = P(("zone", "tile"), None, None, None)
    return jax.shard_map(local, mesh=mesh, in_specs=in_specs, out_specs=out_specs, check_vma=False)
```

time: 495 us -> 423 us (0.85); the launches traced: 493 us -> 416 us
  waiting for transfers between devices: 324 us -> 35.8 us
  blocking collectives: 0 us -> 237 us
  starting transfers between devices: 26.5 us -> 11.3 us
  local copies, waits for them, and re-layouts: 10.3 us -> 4.74 us
    all_to_all x3 -> x1, waiting for transfers between devices: 248 us -> 0.01 us  [swap(): lax.all_to_all(pairs, 'tile', split_axis=0, concat_axis=0, tiled=True)]
    all_to_all x0 -> x1, blocking collectives: none -> 237 us  [swap(): lax.all_to_all(pairs, 'tile', split_axis=0, concat_axis=0, tiled=True)]
    ppermute x4 -> x3, waiting for transfers between devices: 76.7 us -> 35.8 us  [passed_along(): lax.ppermute(value, axis, [(source, source + steps) for source in range(i...]
    all_to_all x3 -> x1, starting transfers between devices: 21.3 us -> 7.49 us  [swap(): lax.all_to_all(pairs, 'tile', split_axis=0, concat_axis=0, tiled=True)]
    pallas_call x3 -> x4, Pallas kernels: 109 us -> 104 us  [render(): pl.pallas_call(functools.partial(render_kernel, local_count, first, bands...]
  transfers between devices with their start and end apart: 7 -> 4, of which waited for: 5 -> 1; matrix products, arithmetic and copies ran while one was open for 3% -> 2% of each run, Pallas kernels for 18% -> 21%
where the time goes in v3:
time: 423 us; the launch traced here: 416 us
  blocking collectives  237 us (56%)
  Pallas kernels  118 us (28%)
  waiting for transfers between devices  35.8 us (8%)
  starting transfers between devices  11.3 us (3%)
  other arithmetic  6.74 us (2%)
  local copies, waits for them, and re-layouts  4.74 us (1%)
    all_to_all x1, blocking collectives, swap(): lax.all_to_all(pairs, 'tile', split_axis=0, concat_axis=0, tiled=True)  237 us
    pallas_call x4, Pallas kernels, render(): pl.pallas_call(functools.partial(render_kernel, local_count, first, bands...  104 us
    ppermute x3, waiting for transfers between devices, passed_along(): lax.ppermute(value, axis, [(source, source + steps) for source in range(i...  35.8 us
  transfers between devices with their start and end apart: 4, of which 1 were waited for; matrix products, arithmetic and copies ran while one was open for 2% of the time, Pallas kernels for 21%

profile of v3, /device:TPU:60, one launch (start us, length us, event | category | flops | bytes accessed | tf_op | source)
XLA Modules:
  0.0 415.8 jit_solution(5199822062174118900)
XLA Ops:
  0.0 1.3 collective-permute-start
  1.3 2.6 pick.3
  3.9 1.3 collective-permute-start.2
  5.2 0.7 add_select_fusion
  5.9 0.7 broadcast_compare_fusion.1
  6.6 0.1 reshape.167
  6.7 0.1 copy.12
  6.8 0.1 eq.68
  6.9 0.1 copy.10
  6.9 0.1 iota_add_fusion
  7.0 0.8 abs_reduce_fusion
  7.9 0.9 copy.15
  8.7 0.8 reshape.168.offsets_ref
  9.7 0.0 copy-start.3
  9.7 0.0 collective-permute-done.listed_ref
  9.7 0.0 copy-start
  9.7 0.1 compare_reduce_fusion
  9.8 0.1 copy.11
  10.0 0.1 reduce_or.12
  10.1 0.2 convert_reduce_fusion.1
  10.3 0.1 select_reduce_fusion.2
  10.4 0.7 convert_reduce_fusion.5
  11.1 0.6 select_select_fusion
  11.7 0.1 copy.13
  11.8 0.1 copy.14
  13.2 1.1 select_reduce_fusion
  14.2 1.3 pad_add_fusion.range_ref
  15.5 0.0 copy-done.3
  15.5 0.0 copy-done
  15.5 13.0 %render.3.refs_1_ = bf16[64,3,128,128]{3,2,1,0:T(8,128)(2,1)} custom-call(s32[2]{0:T(128)} %pad_add_fusion.range_ref, s32[64]{0:T(128)} %get-tuple-element.10.blocks_ref, s32[64]{0:T(128)} %get-tuple-element.9.slots_ref, s32[768]{0:T(1024)} %source_ref.7, s32[1536]{0:T(1024)} %reshape.168.offsets_ref, f32[6144]{0:T(1024)} %copy-done.3, f32[768]{0:T(1024)} %blend_ref.7, ...), custom_call_target="tpu_custom_call" | custom-call | flops 7247757312 | bytes 1179648 | tf_op jit(solution)/shard_map/render/pallas_call | solution.py:147
  28.5 0.0 collective-permute-done.2.refs_0_
  28.5 0.0 copy-start.2
  28.5 0.9 copy-done.2
  29.4 21.3 %seams.3 = bf16[64,3,128,128]{3,2,1,0:T(8,128)(2,1)} custom-call(s32[2]{0:T(128)} %pad_add_fusion.range_ref, s32[64]{0:T(128)} %get-tuple-element.10.blocks_ref, s32[64]{0:T(128)} %get-tuple-element.9.slots_ref, s32[768]{0:T(1024)} %source_ref.7, s32[1536]{0:T(1024)} %reshape.168.offsets_ref, f32[6144]{0:T(1024)} %copy-done.3, ...), custom_call_target="tpu_custom_call", output_to_operand_aliasing={{}: (10, {})} | custom-call | flops 7247757312 | bytes 1179648 | tf_op jit(solution)/shard_map/seams/pallas_call | solution.py:147
  50.7 7.5 %all-to-all-start = ((bf16[32,2,3,128,128]{4,3,2,1,0:T(8,128)(2,1)}), bf16[32,2,3,128,128]{4,3,2,1,0:T(8,128)(2,1)}, u32[]{:S(2)}, u32[]{:S(2)}) async-start(bf16[32,2,3,128,128]{4,3,2,1,0:T(8,128)(2,1)} %bitcast.12), calls=%async_computation | async-start | bytes 12582912 | tf_op jit(solution)/shard_map/all_to_all | solution.py:217
  58.2 3.5 pick.2
  61.7 1.3 collective-permute-start.1
  63.0 0.2 convert_reduce_fusion.2
  63.2 25.6 %render.2.refs_1_ = bf16[64,10,128,128]{3,2,1,0:T(8,128)(2,1)} custom-call(s32[2]{0:T(128)} %pad_add_fusion.range_ref, s32[64]{0:T(128)} %get-tuple-element.10.blocks_ref, s32[64]{0:T(128)} %get-tuple-element.9.slots_ref, s32[768]{0:T(1024)} %source_ref.7, s32[1536]{0:T(1024)} %reshape.168.offsets_ref, f32[6144]{0:T(1024)} %copy-done.3, f32[768]{0:T(1024)} %blend_ref.7, ...), custom_call_target="tpu_custom_call" | custom-call | flops 24159191040 | bytes 3932160 | tf_op jit(solution)/shard_map/render/pallas_call | solution.py:147
  88.9 35.8 %collective-permute-done.1.refs_0_ = bf16[2,10,256,256]{3,2,1,0:T(8,128)(2,1)S(1)} collective-permute-done((bf16[2,10,256,256]{3,2,1,0:T(8,128)(2,1)}, bf16[2,10,256,256]{3,2,1,0:T(8,128)(2,1)S(1)}, u32[]{:S(2)}, u32[]{:S(2)}) %collective-permute-start.1) | collective-permute-done | bytes 2621472 | tf_op jit(solution)/shard_map/ppermute | solution.py:20
  124.7 0.0 copy-start.1
  124.7 1.5 copy-done.1
  126.2 44.6 %seams.2 = bf16[64,10,128,128]{3,2,1,0:T(8,128)(2,1)} custom-call(s32[2]{0:T(128)} %pad_add_fusion.range_ref, s32[64]{0:T(128)} %get-tuple-element.10.blocks_ref, s32[64]{0:T(128)} %get-tuple-element.9.slots_ref, s32[768]{0:T(1024)} %source_ref.7, s32[1536]{0:T(1024)} %reshape.168.offsets_ref, f32[6144]{0:T(1024)} %copy-done.3, ...), custom_call_target="tpu_custom_call", output_to_operand_aliasing={{}: (10, {})} | custom-call | flops 24159191040 | bytes 3932160 | tf_op jit(solution)/shard_map/seams/pallas_call | solution.py:147
  170.8 0.0 all-to-all-done
  170.8 237.5 %all_to_all.10 = bf16[32,2,10,128,128]{4,3,2,1,0:T(8,128)(2,1)S(1)} all-to-all(bf16[32,2,10,128,128]{4,3,2,1,0:T(8,128)(2,1)} %bitcast.11), channel_id=1, replica_groups=mesh['zone'=4,'tile'=32] {'tile'}, dimensions={0} | all-to-all | bytes 41943040 | tf_op jit(solution)/shard_map/all_to_all | solution.py:217
  408.3 7.6 %place.1 = bf16[24,13,128,128]{3,2,1,0:T(8,128)(2,1)} custom-call(s32[24]{0:T(128)S(1)} %multiply_add_fusion.taken_ref, bf16[64,3,128,128]{3,2,1,0:T(8,128)(2,1)} %bitcast.4.early_ref, bf16[64,10,128,128]{3,2,1,0:T(8,128)(2,1)S(1)} %bitcast.10), custom_call_target="tpu_custom_call" | custom-call | tf_op jit(solution)/shard_map/place/pallas_call | solution.py:198
  (16 shorter events, 0.2 us)
Async XLA Ops:
  0.0 9.7 %collective-permute-start = (s32[2]{0:T(128)}, s32[2]{0:T(128)S(1)}, u32[]{:S(2)}, u32[]{:S(2)}) collective-permute-start(s32[2]{0:T(128)} %listed_ref.3), channel_id=1, source_target_pairs={{0,32},{32,64},{64,96},{1,33},{33,65},{65,97},{2,34},{34,66},{66,9... | collective-permute-start | bytes 32 | tf_op jit(solution)/shard_map/ppermute | solution.py:20
  3.9 24.6 %collective-permute-start.2 = (bf16[2,3,256,256]{3,2,1,0:T(8,128)(2,1)}, bf16[2,3,256,256]{3,2,1,0:T(8,128)(2,1)S(1)}, u32[]{:S(2)}, u32[]{:S(2)}) collective-permute-start(bf16[2,3,256,256]{3,2,1,0:T(8,128)(2,1)} %pick.3), channel_id=1, source_target_pairs={{0,32},{32,64},{64,96},{1,33},{33,65},{65,97},{2,34},{34,66},{66,9... | collective-permute-start | bytes 2359304 | tf_op jit(solution)/shard_map/ppermute | solution.py:20
  9.7 5.8 %copy-start.3 = (f32[6144]{0:T(1024)}, f32[6144]{0:T(1024)S(1)}, u32[]{:S(2)}) copy-start(f32[6144]{0:T(1024)S(1)} %fusion.23.taps_ref) | copy-start | bytes 73732
  9.7 5.8 %copy-start = (s32[2]{0:T(128)}, s32[2]{0:T(128)S(1)}, u32[]{:S(2)}) copy-start(s32[2]{0:T(128)S(1)} %collective-permute-done.listed_ref) | copy-start | bytes 28
  28.5 0.9 copy-start.2
  50.7 120.1 %all-to-all-start = ((bf16[32,2,3,128,128]{4,3,2,1,0:T(8,128)(2,1)}), bf16[32,2,3,128,128]{4,3,2,1,0:T(8,128)(2,1)}, u32[]{:S(2)}, u32[]{:S(2)}) async-start(bf16[32,2,3,128,128]{4,3,2,1,0:T(8,128)(2,1)} %bitcast.12), calls=%async_computation | async-start | bytes 12582912 | tf_op jit(solution)/shard_map/all_to_all | solution.py:217
  61.7 62.9 %collective-permute-start.1 = (bf16[2,10,256,256]{3,2,1,0:T(8,128)(2,1)}, bf16[2,10,256,256]{3,2,1,0:T(8,128)(2,1)S(1)}, u32[]{:S(2)}, u32[]{:S(2)}) collective-permute-start(bf16[2,10,256,256]{3,2,1,0:T(8,128)(2,1)} %pick.2), channel_id=1, source_target_pairs={{0,32},{32,64},{64,96},{1,33},{33,65},{65,97},{2,34},{34,66},{66,9... | collective-permute-start | bytes 7864328 | tf_op jit(solution)/shard_map/ppermute | solution.py:20
  124.7 1.5 copy-start.1

commit v4 on v2

v4 whole, which is shorter than its diff:
```python
import functools

import jax
import jax.numpy as jnp
from jax import lax
from jax.experimental import pallas as pl
from jax.experimental.pallas import tpu as pltpu
from jax.sharding import PartitionSpec as P


CHUNKS = (("x", 2), ("z", 2), ("x", 5), ("z", 4))
RING = 4
LANES = 2 * RING
ABREAST = 4
STEPS = (-1, 0, 1, 2)


def passed_along(value, axis, steps):
    count = lax.axis_size(axis)
    initial, last = (max(0, -steps), min(count, count - steps))
    return lax.ppermute(value, axis, [(source, source + steps) for source in range(initial, last)])


def cubic_weight(dist):
    mag = jnp.abs(dist)
    near = (1.5 * mag - 2.5) * mag * mag + 1.0
    far = ((-0.5 * mag + 2.5) * mag - 4.0) * mag + 2.0
    return jnp.where(mag <= 1.0, near, jnp.where(mag < 2.0, far, jnp.zeros_like(mag)))


def hop(value, along, steps, cross=0):
    pairs = []
    for x in range(RING):
        for z in range(RING):
            for core in range(2):
                to_x, to_z = ((x + steps) % RING, z) if along == "x" else (x, (z + steps) % RING)
                pairs.append(((x * RING + z) * 2 + core, (to_x * RING + to_z) * 2 + (core ^ cross)))
    return lax.ppermute(value, "tile", pairs)


def pick_kernel(first, bands, listed_ref, tiles_ref, picked_ref, held, in_sem, out_sem):
    count = picked_ref.shape[0]
    for index in range(count):
        pltpu.make_async_copy(
            tiles_ref.at[listed_ref[index], pl.ds(first, bands)], held.at[index], in_sem.at[index]
        ).start()
    for index in range(count):
        pltpu.make_async_copy(
            tiles_ref.at[listed_ref[index], pl.ds(first, bands)], held.at[index], in_sem.at[index]
        ).wait()
        pltpu.make_async_copy(held.at[index], picked_ref.at[index], out_sem.at[index]).start()
    for index in range(count):
        pltpu.make_async_copy(held.at[index], picked_ref.at[index], out_sem.at[index]).wait()


def pick(listed, tiles, first, bands):
    shape = (listed.shape[0], bands) + tiles.shape[2:]
    return pl.pallas_call(
        functools.partial(pick_kernel, first, bands),
        out_shape=jax.ShapeDtypeStruct(shape, tiles.dtype),
        in_specs=[pl.BlockSpec(memory_space=pltpu.SMEM), pl.BlockSpec(memory_space=pl.ANY)],
        out_specs=pl.BlockSpec(memory_space=pl.ANY),
        scratch_shapes=[
            pltpu.VMEM(shape, tiles.dtype),
            pltpu.SemaphoreType.DMA((shape[0],)),
            pltpu.SemaphoreType.DMA((shape[0],)),
        ],
        name="pick",
    )(listed, tiles)


def render_kernel(
    local_count, first, bands, count_ref, blocks_ref, into_ref, side_ref, source_ref, offsets_ref, taps_ref, blend_ref,
    listed_ref, tiles_ref, beyond_ref, near_ref, near_beyond_ref, stay_ref, up_ref, down_ref,
    held, beside, row_lag, col_lag, done, in_sem, out_sem,
):
    seams = near_ref.shape[0]
    loads = (
        pltpu.make_async_copy(tiles_ref.at[:, pl.ds(first, bands)], held.at[pl.ds(0, local_count)], in_sem.at[0]),
        pltpu.make_async_copy(beyond_ref, held.at[pl.ds(local_count, local_count)], in_sem.at[1]),
        pltpu.make_async_copy(near_ref, beside.at[pl.ds(0, seams)], in_sem.at[2]),
        pltpu.make_async_copy(near_beyond_ref, beside.at[pl.ds(seams, seams)], in_sem.at[3]),
    )
    for load in loads:
        load.start()
    height, width = held.shape[2], held.shape[3]
    row_lag[...] = lax.broadcasted_iota(jnp.int32, row_lag.shape, 1) - 2 * lax.broadcasted_iota(jnp.int32, row_lag.shape, 0)
    col_lag[...] = lax.broadcasted_iota(jnp.int32, col_lag.shape, 0) - 2 * lax.broadcasted_iota(jnp.int32, col_lag.shape, 1)
    for load in loads:
        load.wait()
    count = count_ref[0]

    def start_store(index, way):
        into = into_ref[index]
        slot = lax.rem(into, 64)
        for number, out_ref in ((0, stay_ref), (1, up_ref), (3, down_ref)):

            @pl.when(lax.div(into, 64) == number)
            def _():
                pltpu.make_async_copy(done.at[way], out_ref.at[slot], out_sem.at[way]).start()

    def wait_store(way):
        pltpu.make_async_copy(done.at[way], stay_ref.at[0], out_sem.at[way]).wait()

    def kernel_matrix(lag_ref, block, axis):
        lag = lag_ref[...] - offsets_ref[2 * block + axis]
        kernel = jnp.zeros(lag.shape, jnp.float32)
        for place, step in enumerate(STEPS):
            kernel = jnp.where(lag == step, taps_ref[(len(STEPS) * axis + place) * source_ref.shape[0] + block], kernel)
        return kernel.astype(jnp.bfloat16)

    def render_one(index):
        block = blocks_ref[index]
        side = side_ref[index]
        tile = lax.rem(source_ref[block], local_count)
        second = listed_ref[seams * side + 1] == tile
        flagged = (second | (listed_ref[seams * side] == tile)) & (listed_ref[2 * seams] > 0)
        place = seams * side + jnp.where(second, 1, 0)
        weight = jnp.where(flagged, blend_ref[block], 0.0)
        row_kernel = kernel_matrix(row_lag, block, 0)
        col_kernel = kernel_matrix(col_lag, block, 1)
        primary = held[local_count * side + tile].astype(jnp.float32)
        mixed = (1.0 - weight) * primary + weight * beside[place].astype(jnp.float32)
        mixed = mixed.astype(jnp.bfloat16).reshape(bands * height, width)
        across = jnp.dot(mixed, col_kernel, preferred_element_type=jnp.float32).astype(jnp.bfloat16)
        beside_each = jnp.concatenate([across[b * height : (b + 1) * height] for b in range(bands)], axis=1)
        return jnp.dot(row_kernel, beside_each, preferred_element_type=jnp.float32).astype(jnp.bfloat16)

    def some(turn, carry):
        begin = turn * ABREAST
        half = lax.rem(turn, 2) * ABREAST
        for ahead in range(ABREAST):

            @pl.when(turn >= 2)
            def _():
                wait_store(half + ahead)

        results = [render_one(jnp.minimum(begin + ahead, count - 1)) for ahead in range(ABREAST)]
        for ahead in range(ABREAST):
            for b in range(bands):
                done[half + ahead, b] = results[ahead][:, b * (width // 2) : (b + 1) * (width // 2)]
        for ahead in range(ABREAST):

            @pl.when(begin + ahead < count)
            def _():
                start_store(begin + ahead, half + ahead)

        return carry

    turns = lax.div(count + ABREAST - 1, ABREAST)
    lax.fori_loop(0, turns, some, 0)

    def drain(index, carry):
        wait_store(lax.rem(index, 2 * ABREAST))
        return carry

    lax.fori_loop(jnp.maximum(turns - 2, 0) * ABREAST, count, drain, 0)


def render(scalars, tiles, beyond, near, near_beyond, first):
    local_count, _, height, width = tiles.shape
    bands = beyond.shape[1]
    block = (bands, height // 2, width // 2)
    flops = 24 * bands * (2 * height * width * width // 2 + height * width * height // 2)
    return pl.pallas_call(
        functools.partial(render_kernel, local_count, first, bands),
        out_shape=[jax.ShapeDtypeStruct((slots,) + block, jnp.bfloat16) for slots in (4 * LANES, 2 * LANES, 2 * LANES)],
        in_specs=[pl.BlockSpec(memory_space=pltpu.SMEM)] * len(scalars) + [pl.BlockSpec(memory_space=pl.ANY)] * 4,
        out_specs=[pl.BlockSpec(memory_space=pl.ANY)] * 3,
        scratch_shapes=[
            pltpu.VMEM((2 * local_count, bands, height, width), jnp.bfloat16),
            pltpu.VMEM((2 * near.shape[0], bands, height, width), jnp.bfloat16),
            pltpu.VMEM((height // 2, height), jnp.int32),
            pltpu.VMEM((width, width // 2), jnp.int32),
            pltpu.VMEM((2 * ABREAST,) + block, jnp.bfloat16),
            pltpu.SemaphoreType.DMA((4,)),
            pltpu.SemaphoreType.DMA((2 * ABREAST,)),
        ],
        cost_estimate=pl.CostEstimate(flops=8 * flops, bytes_accessed=24 * bands * height * width // 2, transcendentals=0),
        name="render",
    )(*scalars, tiles, beyond, near, near_beyond)


def pack_kernel(stay_ref, up_ref, down_ref, *refs):
    outs, (held, in_sem, out_sem) = refs[:LANES], refs[LANES:]
    copies = []
    for lane in range(LANES):
        copies += [
            pltpu.make_async_copy(stay_ref.at[pl.ds(4 * lane, 4)], held.at[lane, pl.ds(0, 4)], in_sem.at[lane, 0]),
            pltpu.make_async_copy(up_ref.at[pl.ds(2 * lane, 2)], held.at[lane, pl.ds(4, 2)], in_sem.at[lane, 1]),
            pltpu.make_async_copy(down_ref.at[pl.ds(2 * lane, 2)], held.at[lane, pl.ds(6, 2)], in_sem.at[lane, 2]),
        ]
    for copy in copies:
        copy.start()
    puts = [pltpu.make_async_copy(held.at[lane], outs[lane], out_sem.at[lane]) for lane in range(LANES)]
    for lane in range(LANES):
        for copy in copies[3 * lane : 3 * lane + 3]:
            copy.wait()
        puts[lane].start()
    for put in puts:
        put.wait()


def pack(stay, up, down):
    shape = (8,) + stay.shape[1:]
    return pl.pallas_call(
        pack_kernel,
        out_shape=[jax.ShapeDtypeStruct(shape, stay.dtype)] * LANES,
        in_specs=[pl.BlockSpec(memory_space=pl.ANY)] * 3,
        out_specs=[pl.BlockSpec(memory_space=pl.ANY)] * LANES,
        scratch_shapes=[
            pltpu.VMEM((LANES,) + shape, stay.dtype),
            pltpu.SemaphoreType.DMA((LANES, 3)),
            pltpu.SemaphoreType.DMA((LANES,)),
        ],
        name="pack",
    )(stay, up, down)


def place_kernel(parts, x_lane_ref, x_slot_ref, z_lane_ref, z_slot_ref, *refs):
    arrays, (out_ref, held, in_sem, out_sem) = refs[: LANES * len(parts)], refs[LANES * len(parts) :]
    count = out_ref.shape[0]

    def take(index, carry):
        for number, (axis, first, bands) in enumerate(parts):
            lane_ref, slot_ref = (x_lane_ref, x_slot_ref) if axis == "x" else (z_lane_ref, z_slot_ref)
            for lane in range(LANES):

                @pl.when(lane_ref[index] == lane)
                def _():
                    pltpu.make_async_copy(
                        arrays[LANES * number + lane].at[slot_ref[index]],
                        held.at[index, pl.ds(first, bands)],
                        in_sem.at[number, index],
                    ).start()

        return carry

    lax.fori_loop(0, count, take, 0)

    def put(index, carry):
        for number, (axis, first, bands) in enumerate(parts):
            pltpu.make_async_copy(
                arrays[LANES * number].at[0], held.at[index, pl.ds(first, bands)], in_sem.at[number, index]
            ).wait()
        pltpu.make_async_copy(held.at[index], out_ref.at[index], out_sem.at[index]).start()
        return carry

    lax.fori_loop(0, count, put, 0)

    def finish(index, carry):
        pltpu.make_async_copy(held.at[index], out_ref.at[index], out_sem.at[index]).wait()
        return carry

    lax.fori_loop(0, count, finish, 0)


def place(parts, taken, arrays, shape):
    return pl.pallas_call(
        functools.partial(place_kernel, parts),
        out_shape=jax.ShapeDtypeStruct(shape, jnp.bfloat16),
        in_specs=[pl.BlockSpec(memory_space=pltpu.SMEM)] * 4 + [pl.BlockSpec(memory_space=pl.ANY)] * len(arrays),
        out_specs=pl.BlockSpec(memory_space=pl.ANY),
        scratch_shapes=[
            pltpu.VMEM(shape, jnp.bfloat16),
            pltpu.SemaphoreType.DMA((len(parts), shape[0])),
            pltpu.SemaphoreType.DMA((shape[0],)),
        ],
        name="place",
    )(*taken, *arrays)


def local(tiles, seam_list, source, offsets, fractions, blend):
    tile_count = lax.axis_size("tile")
    myself = lax.axis_index("tile")
    zone_index = lax.axis_index("zone")
    local_count, band_count, height, width = tiles.shape
    per_owner = source.shape[0] // tile_count
    slots = 8 * LANES

    parts, first = [], 0
    for axis, bands in CHUNKS:
        parts.append((axis, first, bands))
        first += bands

    nears, beyonds, nears_beyond = [], [], []
    for axis, first, bands in parts:
        nears.append(passed_along(pick(seam_list, tiles, first, bands), "zone", 1))
        beyonds.append(hop(tiles[:, first : first + bands], axis, 1))
        nears_beyond.append(hop(nears[-1], axis, 1))
    near_list = passed_along(seam_list, "zone", 1)

    def coordinates(device):
        return device // (2 * RING), (device // 2) % RING, device % 2

    order_ids = jnp.arange(per_owner, dtype=jnp.int32)
    owner_ids = jnp.arange(tile_count, dtype=jnp.int32)
    src_device = (source // local_count).reshape(tile_count, per_owner)
    earlier = order_ids[None, :] < order_ids[:, None]
    owners_ahead = owner_ids[None, :] < owner_ids[:, None]
    same = src_device[:, :, None] == src_device[:, None, :]
    rank = jnp.sum((same & earlier[None]).astype(jnp.int32), axis=2)
    block_ids = owner_ids[:, None] * per_owner + order_ids[None, :]
    my_x, my_z, my_core = coordinates(myself)
    src_x, src_z, src_core = coordinates(src_device)
    own_x, own_z, own_core = coordinates(owner_ids[:, None])
    own_src = lax.dynamic_index_in_dim(src_device, myself, 0, keepdims=False)
    own_rank = jnp.sum(((own_src[:, None] == own_src[None, :]) & earlier).astype(jnp.int32), axis=1)
    from_x, from_z, from_core = coordinates(own_src)

    def lists(my_p, my_q, src_p, src_q, own_p, own_q):
        behind = (my_p - src_p) & (RING - 1)
        ahead = (own_p - my_p) & (RING - 1)
        mine = (src_core == my_core) & (src_q == my_q)
        mine = mine & (((behind == 0) & ((ahead == 0) | (ahead == 3))) | ((behind == 1) & ((ahead == 0) | (ahead == 1))))
        lane = 2 * ((own_q - my_q) & (RING - 1)) + (own_core != my_core).astype(jnp.int32)
        slot = jnp.where(ahead == 0, 4 * lane + 2 * behind + rank, 2 * lane + rank)
        within = jnp.sum((mine[:, None, :] & earlier[None]).astype(jnp.int32), axis=2)
        each = jnp.sum(mine.astype(jnp.int32), axis=1)
        turn = within + jnp.sum(jnp.where(owners_ahead, each[None, :], 0), axis=1)[:, None]
        hit = mine[None] & (turn[None] == jnp.arange(slots, dtype=jnp.int32)[:, None, None])

        def listed(values):
            return jnp.sum(jnp.where(hit, values[None], 0), axis=(1, 2))

        return jnp.sum(each)[None], listed(block_ids), listed(64 * ahead + slot), listed(behind)

    def taken(my_p, my_q, src_p, src_q):
        lane = 2 * ((my_q - src_q) & (RING - 1)) + (from_core != my_core).astype(jnp.int32)
        return lane, 2 * ((my_p - src_p) & (RING - 1)) + own_rank

    by_axis = {
        "x": lists(my_x, my_z, src_x, src_z, own_x, own_z),
        "z": lists(my_z, my_x, src_z, src_x, own_z, own_x),
    }
    picks = taken(my_x, my_z, from_x, from_z) + taken(my_z, my_x, from_z, from_x)
    taps = jnp.concatenate([cubic_weight(step - fractions[:, axis]) for axis in range(2) for step in STEPS])
    flat_offsets = offsets.reshape(-1)
    zone_flag = zone_index[None].astype(jnp.int32)
    listed_by = {axis: jnp.concatenate([near_list, hop(near_list, axis, 1), zone_flag]) for axis in ("x", "z")}

    arrays = []
    for part, (axis, first, bands) in enumerate(parts):
        scalars = by_axis[axis] + (source, flat_offsets, taps, blend, listed_by[axis])
        stay, up, down = render(scalars, tiles, beyonds[part], nears[part], nears_beyond[part], first)
        came_up, came_down = hop(up, axis, 1), hop(down, axis, -1)
        packed = pack(stay, came_up, came_down)
        other = "z" if axis == "x" else "x"
        arrays += [packed[0]] + [hop(packed[lane], other, lane // 2, lane % 2) for lane in range(1, LANES)]
    shape = (per_owner, band_count, height // 2, width // 2)
    return place(tuple(parts), picks, arrays, shape)


def solution(mesh):
    in_specs = (
        P(("zone", "tile"), None, None, None),
        P(("zone", "tile")),
        P("zone"),
        P("zone", None),
        P("zone", None),
        P("zone"),
    )
    out_specs = P(("zone", "tile"), None, None, None)
    return jax.shard_map(local, mesh=mesh, in_specs=in_specs, out_specs=out_specs, check_vma=False)
```

time: 495 us -> 575 us (1.16)
  starting transfers between devices: 26.5 us -> 130 us
  waiting for transfers between devices: 324 us -> 298 us
    ppermute x0 -> x46, waiting for transfers between devices: none -> 267 us  [hop(): return lax.ppermute(value, 'tile', pairs)]
    all_to_all x3 -> x0, waiting for transfers between devices: 248 us -> none  [local(): lax.all_to_all(outgoing.reshape((tile_count, capacity) + outgoing.shape[1...]
    ppermute x0 -> x46, starting transfers between devices: none -> 124 us  [hop(): return lax.ppermute(value, 'tile', pairs)]
    ppermute x4 -> x5, waiting for transfers between devices: 76.7 us -> 30.8 us  [passed_along(): lax.ppermute(value, axis, [(source, source + steps) for source in range(i...]
    pallas_call x3 -> x9, Pallas kernels: 12.9 us -> 41.6 us  [the longest x4 22.6 us: pack(): pl.pallas_call(pack_kernel, out_shape=[jax.ShapeDtypeStruct(shape, stay.d...]
    pallas_call x3 -> x4, Pallas kernels: 109 us -> 84 us  [render(): pl.pallas_call(functools.partial(render_kernel, local_count, first, bands...]
    all_to_all x3 -> x0, starting transfers between devices: 21.3 us -> none  [local(): lax.all_to_all(outgoing.reshape((tile_count, capacity) + outgoing.shape[1...]
  transfers between devices with their start and end apart: 7 -> 51, of which waited for: 5 -> 21; matrix products, arithmetic and copies ran while one was open for 3% -> 2% of each run, Pallas kernels for 18% -> 21%
where the time goes in v4:
time: 575 us; the launch traced here: 570 us
  waiting for transfers between devices  298 us (52%)
  starting transfers between devices  130 us (23%)
  Pallas kernels  126 us (22%)
  local copies, waits for them, and re-layouts  8.98 us (2%)
  other arithmetic  5.95 us (1%)
    ppermute x46, waiting for transfers between devices, hop(): return lax.ppermute(value, 'tile', pairs)  267 us
    ppermute x46, starting transfers between devices, hop(): return lax.ppermute(value, 'tile', pairs)  124 us
    pallas_call x4, Pallas kernels, render(): pl.pallas_call(functools.partial(render_kernel, local_count, first, bands...  84 us
    ppermute x5, waiting for transfers between devices, passed_along(): lax.ppermute(value, axis, [(source, source + steps) for source in range(i...  30.8 us
    pallas_call x4, Pallas kernels, pack(): pl.pallas_call(pack_kernel, out_shape=[jax.ShapeDtypeStruct(shape, stay.d...  22.6 us
  transfers between devices with their start and end apart: 51, of which 21 were waited for; matrix products, arithmetic and copies ran while one was open for 2% of the time, Pallas kernels for 21%

profile of v4, /device:TPU:60, one launch (start us, length us, event | category | flops | bytes accessed | tf_op | source)
XLA Modules:
  0.0 569.8 jit_solution(13163122233723936084)
XLA Ops:
  0.0 1.3 collective-permute-start
  1.3 2.9 pick.6
  4.2 1.3 collective-permute-start.28
  5.5 1.5 fusion.49
  7.0 2.0 collective-permute-start.15
  9.0 2.4 pick.5
  11.4 1.3 collective-permute-start.16
  12.7 2.4 pick.4
  15.2 1.3 collective-permute-start.3
  19.1 30.8 %collective-permute-done.16.near_ref = bf16[2,2,256,256]{3,2,1,0:T(8,128)(2,1)} collective-permute-done((bf16[2,2,256,256]{3,2,1,0:T(8,128)(2,1)}, bf16[2,2,256,256]{3,2,1,0:T(8,128)(2,1)}, u32[]{:S(2)}, u32[]{:S(2)}) %collective-permute-start.16) | collective-permute-done | bytes 524320 | tf_op jit(solution)/shard_map/ppermute | solution.py:21
  49.9 1.9 collective-permute-start.17
  52.2 2.8 pick.7
  56.4 1.8 select_reduce_fusion
  58.2 1.3 collective-permute-start.1
  59.5 2.4 collective-permute-done.1
  61.9 1.6 collective-permute-start.14
  63.5 1.9 collective-permute-done.14
  65.4 1.3 collective-permute-start.40
  67.4 1.2 collective-permute-start.2
  68.6 1.7 collective-permute-start.4
  70.3 16.4 %render.5 = (bf16[32,2,128,128]{3,2,1,0:T(8,128)(2,1)}, bf16[16,2,128,128]{3,2,1,0:T(8,128)(2,1)}, bf16[16,2,128,128]{3,2,1,0:T(8,128)(2,1)}) custom-call(s32[1]{0:T(128)} %bitcast.3.count_ref, s32[64]{0:T(128)} %get-tuple-element.95.blocks_ref, s32[64]{0:T(128)} %get-tuple-element.94.into_ref, s32[64]{0:T(128)} %get-tuple-element.93.side_ref, ...), custom_call_target="tpu_custom_call" | custom-call | flops 9663676416 | bytes 1572864 | tf_op jit(solution)/shard_map/render/pallas_call | solution.py:165
  86.7 11.1 %collective-permute-start.18 = (bf16[16,2,128,128]{3,2,1,0:T(8,128)(2,1)}, bf16[16,2,128,128]{3,2,1,0:T(8,128)(2,1)}, u32[]{:S(2)}, u32[]{:S(2)}) collective-permute-start(bf16[16,2,128,128]{3,2,1,0:T(8,128)(2,1)} %get-tuple-element.61), channel_id=1, source_target_pairs={{0,2},{1,3},{2,4},{3,5},{4,6},{5,7},{6,0},{7,1},{8,10},{9,11},{10,... | collective-permute-start | bytes 3145736 | tf_op jit(solution)/shard_map/ppermute | solution.py:38
  97.8 1.7 slice.28
  100.5 1.5 slice.29
  102.0 2.1 collective-permute-start.39
  104.1 17.8 %render.4 = (bf16[32,2,128,128]{3,2,1,0:T(8,128)(2,1)}, bf16[16,2,128,128]{3,2,1,0:T(8,128)(2,1)}, bf16[16,2,128,128]{3,2,1,0:T(8,128)(2,1)}) custom-call(s32[1]{0:T(128)} %bitcast.1.count_ref, s32[64]{0:T(128)} %get-tuple-element.126.blocks_ref, s32[64]{0:T(128)} %get-tuple-element.127.into_ref, s32[64]{0:T(128)} %get-tuple-element.128.side_ref, ...), custom_call_target="tpu_custom_call" | custom-call | flops 9663676416 | bytes 1572864 | tf_op jit(solution)/shard_map/render/pallas_call | solution.py:165
  122.1 2.0 collective-permute-start.6
  124.2 3.8 pack.5
  128.0 27.3 %collective-permute-done.39.beyond_ref = bf16[3,4,256,256]{3,2,1,0:T(8,128)(2,1)} collective-permute-done((bf16[3,4,256,256]{3,2,1,0:T(8,128)(2,1)S(1)}, bf16[3,4,256,256]{3,2,1,0:T(8,128)(2,1)}, u32[]{:S(2)}, u32[]{:S(2)}) %collective-permute-start.39) | collective-permute-done | bytes 1572896 | tf_op jit(solution)/shard_map/ppermute | solution.py:38
  155.3 16.7 %collective-permute-done.41.near_beyond_ref = bf16[2,4,256,256]{3,2,1,0:T(8,128)(2,1)} collective-permute-done((bf16[2,4,256,256]{3,2,1,0:T(8,128)(2,1)}, bf16[2,4,256,256]{3,2,1,0:T(8,128)(2,1)}, u32[]{:S(2)}, u32[]{:S(2)}) %collective-permute-start.41) | collective-permute-done | bytes 1048608 | tf_op jit(solution)/shard_map/ppermute | solution.py:38
  172.3 22.3 %render.7 = (bf16[32,4,128,128]{3,2,1,0:T(8,128)(2,1)}, bf16[16,4,128,128]{3,2,1,0:T(8,128)(2,1)}, bf16[16,4,128,128]{3,2,1,0:T(8,128)(2,1)}) custom-call(s32[1]{0:T(128)} %bitcast.3.count_ref, s32[64]{0:T(128)} %get-tuple-element.95.blocks_ref, s32[64]{0:T(128)} %get-tuple-element.94.into_ref, s32[64]{0:T(128)} %get-tuple-element.93.side_ref, ...), custom_call_target="tpu_custom_call" | custom-call | flops 19327352832 | bytes 3145728 | tf_op jit(solution)/shard_map/render/pallas_call | solution.py:165
  194.6 2.2 collective-permute-done.29.near_beyond_ref
  196.8 13.7 %collective-permute-start.42 = (bf16[16,4,128,128]{3,2,1,0:T(8,128)(2,1)}, bf16[16,4,128,128]{3,2,1,0:T(8,128)(2,1)}, u32[]{:S(2)}, u32[]{:S(2)}) collective-permute-start(bf16[16,4,128,128]{3,2,1,0:T(8,128)(2,1)} %get-tuple-element.83), channel_id=1, source_target_pairs={{0,2},{1,3},{2,4},{3,5},{4,6},{5,7},{6,0},{7,1},{8,10},{9,11},{10,... | collective-permute-start | bytes 6291464 | tf_op jit(solution)/shard_map/ppermute | solution.py:38
  210.6 6.2 %collective-permute-done.22.refs_11_ = bf16[8,2,128,128]{3,2,1,0:T(8,128)(2,1)S(1)} collective-permute-done((bf16[8,2,128,128]{3,2,1,0:T(8,128)(2,1)}, bf16[8,2,128,128]{3,2,1,0:T(8,128)(2,1)S(1)}, u32[]{:S(2)}, u32[]{:S(2)}) %collective-permute-start.22) | collective-permute-done | bytes 524320 | tf_op jit(solution)/shard_map/ppermute | solution.py:38
  216.9 18.4 %collective-permute-start.25 = (bf16[8,2,128,128]{3,2,1,0:T(8,128)(2,1)}, bf16[8,2,128,128]{3,2,1,0:T(8,128)(2,1)}, u32[]{:S(2)}, u32[]{:S(2)}) collective-permute-start(bf16[8,2,128,128]{3,2,1,0:T(8,128)(2,1)} %get-tuple-element.69), channel_id=1, source_target_pairs={{0,24},{1,25},{2,26},{3,27},{4,28},{5,29},{6,30},{7,31},{8,0},{9,1... | collective-permute-start | bytes 1572872 | tf_op jit(solution)/shard_map/ppermute | solution.py:38
  235.2 27.5 %render.6 = (bf16[32,5,128,128]{3,2,1,0:T(8,128)(2,1)}, bf16[16,5,128,128]{3,2,1,0:T(8,128)(2,1)}, bf16[16,5,128,128]{3,2,1,0:T(8,128)(2,1)}) custom-call(s32[1]{0:T(128)} %bitcast.1.count_ref, s32[64]{0:T(128)} %get-tuple-element.126.blocks_ref, s32[64]{0:T(128)} %get-tuple-element.127.into_ref, s32[64]{0:T(128)} %get-tuple-element.128.side_ref, ...), custom_call_target="tpu_custom_call" | custom-call | flops 24159191040 | bytes 3932160 | tf_op jit(solution)/shard_map/render/pallas_call | solution.py:165
  263.6 3.8 pack.4
  267.5 2.1 collective-permute-start.31
  269.6 11.1 %collective-permute-done.10.refs_4_ = bf16[8,2,128,128]{3,2,1,0:T(8,128)(2,1)S(1)} collective-permute-done((bf16[8,2,128,128]{3,2,1,0:T(8,128)(2,1)}, bf16[8,2,128,128]{3,2,1,0:T(8,128)(2,1)S(1)}, u32[]{:S(2)}, u32[]{:S(2)}) %collective-permute-start.10) | collective-permute-done | bytes 524320 | tf_op jit(solution)/shard_map/ppermute | solution.py:38
  280.8 14.6 %collective-permute-done.11.refs_5_ = bf16[8,2,128,128]{3,2,1,0:T(8,128)(2,1)} collective-permute-done((bf16[8,2,128,128]{3,2,1,0:T(8,128)(2,1)}, bf16[8,2,128,128]{3,2,1,0:T(8,128)(2,1)}, u32[]{:S(2)}, u32[]{:S(2)}) %collective-permute-start.11) | collective-permute-done | bytes 524320 | tf_op jit(solution)/shard_map/ppermute | solution.py:38
  295.4 4.5 collective-permute-start.12
  299.9 11.8 %collective-permute-done.12.refs_6_ = bf16[8,2,128,128]{3,2,1,0:T(8,128)(2,1)} collective-permute-done((bf16[8,2,128,128]{3,2,1,0:T(8,128)(2,1)}, bf16[8,2,128,128]{3,2,1,0:T(8,128)(2,1)}, u32[]{:S(2)}, u32[]{:S(2)}) %collective-permute-start.12) | collective-permute-done | bytes 524320 | tf_op jit(solution)/shard_map/ppermute | solution.py:38
  311.7 1.3 collective-permute-start.13
  313.0 1.3 collective-permute-start.7
  314.3 6.6 %pack.7 = (bf16[8,4,128,128]{3,2,1,0:T(8,128)(2,1)}, bf16[8,4,128,128]{3,2,1,0:T(8,128)(2,1)}, bf16[8,4,128,128]{3,2,1,0:T(8,128)(2,1)}, bf16[8,4,128,128]{3,2,1...) custom-call(bf16[32,4,128,128]{3,2,1,0:T(8,128)(2,1)} %get-tuple-ele, ...), custom_call_target="tpu_custom_call" | custom-call | tf_op jit(solution)/shard_map/pack/pallas_call | solution.py:206
  320.9 4.7 collective-permute-done.13.refs_7_
  325.8 2.7 collective-permute-done.8.refs_2_
  329.0 1.1 collective-permute-start.9
  330.1 8.3 %pack.6 = (bf16[8,5,128,128]{3,2,1,0:T(8,128)(2,1)}, bf16[8,5,128,128]{3,2,1,0:T(8,128)(2,1)}, bf16[8,5,128,128]{3,2,1,0:T(8,128)(2,1)}, bf16[8,5,128,128]{3,2,1...) custom-call(bf16[32,5,128,128]{3,2,1,0:T(8,128)(2,1)} %get-tuple-ele, ...), custom_call_target="tpu_custom_call" | custom-call | tf_op jit(solution)/shard_map/pack/pallas_call | solution.py:206
  338.4 6.1 %collective-permute-done.9.refs_3_ = bf16[8,2,128,128]{3,2,1,0:T(8,128)(2,1)S(1)} collective-permute-done((bf16[8,2,128,128]{3,2,1,0:T(8,128)(2,1)}, bf16[8,2,128,128]{3,2,1,0:T(8,128)(2,1)S(1)}, u32[]{:S(2)}, u32[]{:S(2)}) %collective-permute-start.9) | collective-permute-done | bytes 524320 | tf_op jit(solution)/shard_map/ppermute | solution.py:38
  344.5 1.5 collective-permute-start.33
  346.0 6.1 %collective-permute-done.45.refs_26_ = bf16[8,4,128,128]{3,2,1,0:T(8,128)(2,1)} collective-permute-done((bf16[8,4,128,128]{3,2,1,0:T(8,128)(2,1)}, bf16[8,4,128,128]{3,2,1,0:T(8,128)(2,1)}, u32[]{:S(2)}, u32[]{:S(2)}) %collective-permute-start.45) | collective-permute-done | bytes 1048608 | tf_op jit(solution)/shard_map/ppermute | solution.py:38
  352.1 21.3 %collective-permute-done.46.refs_27_ = bf16[8,4,128,128]{3,2,1,0:T(8,128)(2,1)} collective-permute-done((bf16[8,4,128,128]{3,2,1,0:T(8,128)(2,1)}, bf16[8,4,128,128]{3,2,1,0:T(8,128)(2,1)}, u32[]{:S(2)}, u32[]{:S(2)}) %collective-permute-start.46) | collective-permute-done | bytes 1048608 | tf_op jit(solution)/shard_map/ppermute | solution.py:38
  374.0 23.8 %collective-permute-done.47.refs_28_ = bf16[8,4,128,128]{3,2,1,0:T(8,128)(2,1)} collective-permute-done((bf16[8,4,128,128]{3,2,1,0:T(8,128)(2,1)}, bf16[8,4,128,128]{3,2,1,0:T(8,128)(2,1)}, u32[]{:S(2)}, u32[]{:S(2)}) %collective-permute-start.47) | collective-permute-done | bytes 1048608 | tf_op jit(solution)/shard_map/ppermute | solution.py:38
  397.8 20.4 %collective-permute-done.48.refs_29_ = bf16[8,4,128,128]{3,2,1,0:T(8,128)(2,1)S(1)} collective-permute-done((bf16[8,4,128,128]{3,2,1,0:T(8,128)(2,1)}, bf16[8,4,128,128]{3,2,1,0:T(8,128)(2,1)S(1)}, u32[]{:S(2)}, u32[]{:S(2)}) %collective-permute-start.48) | collective-permute-done | bytes 1048608 | tf_op jit(solution)/shard_map/ppermute | solution.py:38
  418.3 2.3 collective-permute-start.34
  420.6 28.5 %collective-permute-start.35 = (bf16[8,5,128,128]{3,2,1,0:T(8,128)(2,1)}, bf16[8,5,128,128]{3,2,1,0:T(8,128)(2,1)}, u32[]{:S(2)}, u32[]{:S(2)}) collective-permute-start(bf16[8,5,128,128]{3,2,1,0:T(8,128)(2,1)} %get-tuple-element.78), channel_id=1, source_target_pairs={{0,4},{1,5},{2,6},{3,7},{4,0},{5,1},{6,2},{7,3},{8,12},{9,13},{10,... | collective-permute-start | bytes 3932168 | tf_op jit(solution)/shard_map/ppermute | solution.py:38
  449.0 21.6 %collective-permute-start.36 = (bf16[8,5,128,128]{3,2,1,0:T(8,128)(2,1)}, bf16[8,5,128,128]{3,2,1,0:T(8,128)(2,1)}, u32[]{:S(2)}, u32[]{:S(2)}) collective-permute-start(bf16[8,5,128,128]{3,2,1,0:T(8,128)(2,1)} %get-tuple-element.79), channel_id=1, source_target_pairs={{0,5},{1,4},{2,7},{3,6},{4,1},{5,0},{6,3},{7,2},{8,13},{9,12},{10,... | collective-permute-start | bytes 3932168 | tf_op jit(solution)/shard_map/ppermute | solution.py:38
  470.7 1.0 collective-permute-start.38
  473.6 5.5 collective-permute-done.35.refs_20_
  479.1 27.6 %collective-permute-done.36.refs_21_ = bf16[8,5,128,128]{3,2,1,0:T(8,128)(2,1)} collective-permute-done((bf16[8,5,128,128]{3,2,1,0:T(8,128)(2,1)}, bf16[8,5,128,128]{3,2,1,0:T(8,128)(2,1)}, u32[]{:S(2)}, u32[]{:S(2)}) %collective-permute-start.36) | collective-permute-done | bytes 1310752 | tf_op jit(solution)/shard_map/ppermute | solution.py:38
  506.7 28.1 %collective-permute-done.37.refs_22_ = bf16[8,5,128,128]{3,2,1,0:T(8,128)(2,1)} collective-permute-done((bf16[8,5,128,128]{3,2,1,0:T(8,128)(2,1)}, bf16[8,5,128,128]{3,2,1,0:T(8,128)(2,1)}, u32[]{:S(2)}, u32[]{:S(2)}) %collective-permute-start.37) | collective-permute-done | bytes 1310752 | tf_op jit(solution)/shard_map/ppermute | solution.py:38
  534.7 26.6 %collective-permute-done.38.refs_23_ = bf16[8,5,128,128]{3,2,1,0:T(8,128)(2,1)} collective-permute-done((bf16[8,5,128,128]{3,2,1,0:T(8,128)(2,1)}, bf16[8,5,128,128]{3,2,1,0:T(8,128)(2,1)}, u32[]{:S(2)}, u32[]{:S(2)}) %collective-permute-start.38) | collective-permute-done | bytes 1310752 | tf_op jit(solution)/shard_map/ppermute | solution.py:38
  561.3 8.3 %place.1 = bf16[24,13,128,128]{3,2,1,0:T(8,128)(2,1)} custom-call(s32[24]{0:T(128)} %add.470.x_lane_ref, s32[24]{0:T(128)} %get-tuple-element.137.x_slot_ref, s32[24]{0:T(128)} %get-tuple-element.120.z_lane_ref, s32[24]{0:T(128)} %get-tuple-element.118.z_slot_ref, bf16[8,2,128,128]{3,2,1,0:T(8,128)(2,1)} %get-tuple-element.52.refs_0_, ...), custom_call_target="tpu_custom_call" | custom-call | tf_op jit(solution)/shard_map/place/pallas_call | solution.py:259
  (145 shorter events, 10.3 us)
Async XLA Ops:
  0.0 58.2 %collective-permute-start = (s32[2]{0:T(128)}, s32[2]{0:T(128)S(1)}, u32[]{:S(2)}, u32[]{:S(2)}) collective-permute-start(s32[2]{0:T(128)} %listed_ref.7), channel_id=1, source_target_pairs={{0,32},{32,64},{64,96},{1,33},{33,65},{65,97},{2,34},{34,66},{66,9... | collective-permute-start | bytes 32 | tf_op jit(solution)/shard_map/ppermute | solution.py:21
  4.2 117.7 %collective-permute-start.28 = (bf16[2,5,256,256]{3,2,1,0:T(8,128)(2,1)}, bf16[2,5,256,256]{3,2,1,0:T(8,128)(2,1)}, u32[]{:S(2)}, u32[]{:S(2)}) collective-permute-start(bf16[2,5,256,256]{3,2,1,0:T(8,128)(2,1)} %pick.6), channel_id=1, source_target_pairs={{0,32},{32,64},{64,96},{1,33},{33,65},{65,97},{2,34},{34,66},{66,9... | collective-permute-start | bytes 3932168 | tf_op jit(solution)/shard_map/ppermute | solution.py:21
  7.0 61.6 %collective-permute-start.15 = (bf16[3,2,256,256]{3,2,1,0:T(8,128)(2,1)S(1)}, bf16[3,2,256,256]{3,2,1,0:T(8,128)(2,1)}, u32[]{:S(2)}, u32[]{:S(2)}) collective-permute-start(bf16[3,2,256,256]{3,2,1,0:T(8,128)(2,1)S(1)} %get-tuple-element.124), channel_id=1, source_target_pairs={{0,2},{1,3},{2,4},{3,5},{4,6},{5,7},{6,0},{7,1},{8,10},{9,11},{10,... | collective-permute-start | bytes 2359304 | tf_op jit(solution)/shard_map/ppermute | solution.py:38
  11.4 38.5 %collective-permute-start.16 = (bf16[2,2,256,256]{3,2,1,0:T(8,128)(2,1)}, bf16[2,2,256,256]{3,2,1,0:T(8,128)(2,1)}, u32[]{:S(2)}, u32[]{:S(2)}) collective-permute-start(bf16[2,2,256,256]{3,2,1,0:T(8,128)(2,1)} %pick.5), channel_id=1, source_target_pairs={{0,32},{32,64},{64,96},{1,33},{33,65},{65,97},{2,34},{34,66},{66,9... | collective-permute-start | bytes 1572872 | tf_op jit(solution)/shard_map/ppermute | solution.py:21
  15.2 52.2 %collective-permute-start.3 = (bf16[2,2,256,256]{3,2,1,0:T(8,128)(2,1)}, bf16[2,2,256,256]{3,2,1,0:T(8,128)(2,1)}, u32[]{:S(2)}, u32[]{:S(2)}) collective-permute-start(bf16[2,2,256,256]{3,2,1,0:T(8,128)(2,1)} %pick.4), channel_id=1, source_target_pairs={{0,32},{32,64},{64,96},{1,33},{33,65},{65,97},{2,34},{34,66},{66,9... | collective-permute-start | bytes 1572872 | tf_op jit(solution)/shard_map/ppermute | solution.py:21
  49.9 20.4 %collective-permute-start.17 = (bf16[2,2,256,256]{3,2,1,0:T(8,128)(2,1)}, bf16[2,2,256,256]{3,2,1,0:T(8,128)(2,1)}, u32[]{:S(2)}, u32[]{:S(2)}) collective-permute-start(bf16[2,2,256,256]{3,2,1,0:T(8,128)(2,1)} %collective-permute-done.16.near_ref), channel_id=1, source_target_pairs={{0,2},{1,3},{2,4},{3,5},{4,6},{5,7},{6,0},{7,1},{8,10},{9,11},{10,... | collective-permute-start | bytes 1572872 | tf_op jit(solution)/shard_map/ppermute | solution.py:38
  58.2 12.1 %copy-start.18 = (f32[6144]{0:T(1024)}, f32[6144]{0:T(1024)S(1)}, u32[]{:S(2)}) copy-start(f32[6144]{0:T(1024)S(1)} %fusion.33.taps_ref) | copy-start | bytes 73732
  58.2 3.6 collective-permute-start.1
  61.9 3.6 collective-permute-start.14
  65.4 34.1 %collective-permute-start.40 = (bf16[2,4,256,256]{3,2,1,0:T(8,128)(2,1)}, bf16[2,4,256,256]{3,2,1,0:T(8,128)(2,1)S(1)}, u32[]{:S(2)}, u32[]{:S(2)}) collective-permute-start(bf16[2,4,256,256]{3,2,1,0:T(8,128)(2,1)} %pick.7), channel_id=1, source_target_pairs={{0,32},{32,64},{64,96},{1,33},{33,65},{65,97},{2,34},{34,66},{66,9... | collective-permute-start | bytes 3145736 | tf_op jit(solution)/shard_map/ppermute | solution.py:21
  67.4 30.5 %collective-permute-start.2 = (bf16[3,2,256,256]{3,2,1,0:T(8,128)(2,1)S(1)}, bf16[3,2,256,256]{3,2,1,0:T(8,128)(2,1)}, u32[]{:S(2)}, u32[]{:S(2)}) collective-permute-start(bf16[3,2,256,256]{3,2,1,0:T(8,128)(2,1)S(1)} %get-tuple-element.125), channel_id=1, source_target_pairs={{0,8},{1,9},{2,10},{3,11},{4,12},{5,13},{6,14},{7,15},{8,16},{9,17... | collective-permute-start | bytes 2359304 | tf_op jit(solution)/shard_map/ppermute | solution.py:38
  68.6 33.4 %collective-permute-start.4 = (bf16[2,2,256,256]{3,2,1,0:T(8,128)(2,1)}, bf16[2,2,256,256]{3,2,1,0:T(8,128)(2,1)}, u32[]{:S(2)}, u32[]{:S(2)}) collective-permute-start(bf16[2,2,256,256]{3,2,1,0:T(8,128)(2,1)} %collective-permute-done.3.near_ref), channel_id=1, source_target_pairs={{0,8},{1,9},{2,10},{3,11},{4,12},{5,13},{6,14},{7,15},{8,16},{9,17... | collective-permute-start | bytes 1572872 | tf_op jit(solution)/shard_map/ppermute | solution.py:38
  86.7 35.3 %collective-permute-start.18 = (bf16[16,2,128,128]{3,2,1,0:T(8,128)(2,1)}, bf16[16,2,128,128]{3,2,1,0:T(8,128)(2,1)}, u32[]{:S(2)}, u32[]{:S(2)}) collective-permute-start(bf16[16,2,128,128]{3,2,1,0:T(8,128)(2,1)} %get-tuple-element.61), channel_id=1, source_target_pairs={{0,2},{1,3},{2,4},{3,5},{4,6},{5,7},{6,0},{7,1},{8,10},{9,11},{10,... | collective-permute-start | bytes 3145736 | tf_op jit(solution)/shard_map/ppermute | solution.py:38
  97.8 24.3 %collective-permute-start.19 = (bf16[16,2,128,128]{3,2,1,0:T(8,128)(2,1)}, bf16[16,2,128,128]{3,2,1,0:T(8,128)(2,1)}, u32[]{:S(2)}, u32[]{:S(2)}) collective-permute-start(bf16[16,2,128,128]{3,2,1,0:T(8,128)(2,1)} %get-tuple-element.62), channel_id=1, source_target_pairs={{0,6},{1,7},{2,0},{3,1},{4,2},{5,3},{6,4},{7,5},{8,14},{9,15},{10,... | collective-permute-start | bytes 3145736 | tf_op jit(solution)/shard_map/ppermute | solution.py:38
  100.5 54.8 %collective-permute-start.27 = (bf16[3,5,256,256]{3,2,1,0:T(8,128)(2,1)S(1)}, bf16[3,5,256,256]{3,2,1,0:T(8,128)(2,1)}, u32[]{:S(2)}, u32[]{:S(2)}) collective-permute-start(bf16[3,5,256,256]{3,2,1,0:T(8,128)(2,1)S(1)} %slice.28), channel_id=1, source_target_pairs={{0,8},{1,9},{2,10},{3,11},{4,12},{5,13},{6,14},{7,15},{8,16},{9,17... | collective-permute-start | bytes 5898248 | tf_op jit(solution)/shard_map/ppermute | solution.py:38
  102.0 53.3 %collective-permute-start.39 = (bf16[3,4,256,256]{3,2,1,0:T(8,128)(2,1)S(1)}, bf16[3,4,256,256]{3,2,1,0:T(8,128)(2,1)}, u32[]{:S(2)}, u32[]{:S(2)}) collective-permute-start(bf16[3,4,256,256]{3,2,1,0:T(8,128)(2,1)S(1)} %slice.29), channel_id=1, source_target_pairs={{0,2},{1,3},{2,4},{3,5},{4,6},{5,7},{6,0},{7,1},{8,10},{9,11},{10,... | collective-permute-start | bytes 4718600 | tf_op jit(solution)/shard_map/ppermute | solution.py:38
  121.9 50.1 %collective-permute-start.41 = (bf16[2,4,256,256]{3,2,1,0:T(8,128)(2,1)}, bf16[2,4,256,256]{3,2,1,0:T(8,128)(2,1)}, u32[]{:S(2)}, u32[]{:S(2)}) collective-permute-start(bf16[2,4,256,256]{3,2,1,0:T(8,128)(2,1)} %copy-done.17), channel_id=1, source_target_pairs={{0,2},{1,3},{2,4},{3,5},{4,6},{5,7},{6,0},{7,1},{8,10},{9,11},{10,... | collective-permute-start | bytes 3145736 | tf_op jit(solution)/shard_map/ppermute | solution.py:38
  122.0 50.0 %collective-permute-start.5 = (bf16[16,2,128,128]{3,2,1,0:T(8,128)(2,1)}, bf16[16,2,128,128]{3,2,1,0:T(8,128)(2,1)}, u32[]{:S(2)}, u32[]{:S(2)}) collective-permute-start(bf16[16,2,128,128]{3,2,1,0:T(8,128)(2,1)} %get-tuple-element.50), channel_id=1, source_target_pairs={{0,8},{1,9},{2,10},{3,11},{4,12},{5,13},{6,14},{7,15},{8,16},{9,17... | collective-permute-start | bytes 3145736 | tf_op jit(solution)/shard_map/ppermute | solution.py:38
  122.1 49.9 %collective-permute-start.6 = (bf16[16,2,128,128]{3,2,1,0:T(8,128)(2,1)}, bf16[16,2,128,128]{3,2,1,0:T(8,128)(2,1)}, u32[]{:S(2)}, u32[]{:S(2)}) collective-permute-start(bf16[16,2,128,128]{3,2,1,0:T(8,128)(2,1)} %get-tuple-element.51), channel_id=1, source_target_pairs={{0,24},{1,25},{2,26},{3,27},{4,28},{5,29},{6,30},{7,31},{8,0},{9,1... | collective-permute-start | bytes 3145736 | tf_op jit(solution)/shard_map/ppermute | solution.py:38
  155.3 41.4 %collective-permute-start.29 = (bf16[2,5,256,256]{3,2,1,0:T(8,128)(2,1)}, bf16[2,5,256,256]{3,2,1,0:T(8,128)(2,1)S(1)}, u32[]{:S(2)}, u32[]{:S(2)}) collective-permute-start(bf16[2,5,256,256]{3,2,1,0:T(8,128)(2,1)} %collective-permute-done.28.near_ref), channel_id=1, source_target_pairs={{0,8},{1,9},{2,10},{3,11},{4,12},{5,13},{6,14},{7,15},{8,16},{9,17... | collective-permute-start | bytes 3932168 | tf_op jit(solution)/shard_map/ppermute | solution.py:38
  155.3 55.2 %collective-permute-start.20 = (bf16[8,2,128,128]{3,2,1,0:T(8,128)(2,1)}, bf16[8,2,128,128]{3,2,1,0:T(8,128)(2,1)S(1)}, u32[]{:S(2)}, u32[]{:S(2)}) collective-permute-start(bf16[8,2,128,128]{3,2,1,0:T(8,128)(2,1)} %get-tuple-element.64), channel_id=1, source_target_pairs={{0,1},{1,0},{2,3},{3,2},{4,5},{5,4},{6,7},{7,6},{8,9},{9,8},{10,11... | collective-permute-start | bytes 1572872 | tf_op jit(solution)/shard_map/ppermute | solution.py:38
  172.0 38.5 %collective-permute-start.21 = (bf16[8,2,128,128]{3,2,1,0:T(8,128)(2,1)}, bf16[8,2,128,128]{3,2,1,0:T(8,128)(2,1)S(1)}, u32[]{:S(2)}, u32[]{:S(2)}) collective-permute-start(bf16[8,2,128,128]{3,2,1,0:T(8,128)(2,1)} %get-tuple-element.65), channel_id=1, source_target_pairs={{0,8},{1,9},{2,10},{3,11},{4,12},{5,13},{6,14},{7,15},{8,16},{9,17... | collective-permute-start | bytes 1572872 | tf_op jit(solution)/shard_map/ppermute | solution.py:38
  172.0 44.8 %collective-permute-start.22 = (bf16[8,2,128,128]{3,2,1,0:T(8,128)(2,1)}, bf16[8,2,128,128]{3,2,1,0:T(8,128)(2,1)S(1)}, u32[]{:S(2)}, u32[]{:S(2)}) collective-permute-start(bf16[8,2,128,128]{3,2,1,0:T(8,128)(2,1)} %get-tuple-element.66), channel_id=1, source_target_pairs={{0,9},{1,8},{2,11},{3,10},{4,13},{5,12},{6,15},{7,14},{8,17},{9,16... | collective-permute-start | bytes 1572872 | tf_op jit(solution)/shard_map/ppermute | solution.py:38
  172.1 63.2 %collective-permute-start.23 = (bf16[8,2,128,128]{3,2,1,0:T(8,128)(2,1)}, bf16[8,2,128,128]{3,2,1,0:T(8,128)(2,1)S(1)}, u32[]{:S(2)}, u32[]{:S(2)}) collective-permute-start(bf16[8,2,128,128]{3,2,1,0:T(8,128)(2,1)} %get-tuple-element.67), channel_id=1, source_target_pairs={{0,16},{1,17},{2,18},{3,19},{4,20},{5,21},{6,22},{7,23},{8,24},{9,... | collective-permute-start | bytes 1572872 | tf_op jit(solution)/shard_map/ppermute | solution.py:38
  196.8 13.8 %copy-start.16 = (bf16[2,5,256,256]{3,2,1,0:T(8,128)(2,1)}, bf16[2,5,256,256]{3,2,1,0:T(8,128)(2,1)S(1)}, u32[]{:S(2)}) copy-start(bf16[2,5,256,256]{3,2,1,0:T(8,128)(2,1)S(1)} %collective-permute-done.29.near_beyond_ref) | copy-start | bytes 3932164
  196.8 116.3 %collective-permute-start.42 = (bf16[16,4,128,128]{3,2,1,0:T(8,128)(2,1)}, bf16[16,4,128,128]{3,2,1,0:T(8,128)(2,1)}, u32[]{:S(2)}, u32[]{:S(2)}) collective-permute-start(bf16[16,4,128,128]{3,2,1,0:T(8,128)(2,1)} %get-tuple-element.83), channel_id=1, source_target_pairs={{0,2},{1,3},{2,4},{3,5},{4,6},{5,7},{6,0},{7,1},{8,10},{9,11},{10,... | collective-permute-start | bytes 6291464 | tf_op jit(solution)/shard_map/ppermute | solution.py:38
  210.5 52.2 %copy-start.6 = (bf16[8,2,128,128]{3,2,1,0:T(8,128)(2,1)}, bf16[8,2,128,128]{3,2,1,0:T(8,128)(2,1)S(1)}, u32[]{:S(2)}) copy-start(bf16[8,2,128,128]{3,2,1,0:T(8,128)(2,1)S(1)} %collective-permute-done.20.refs_9_) | copy-start | bytes 1572868
  210.5 103.8 %collective-permute-start.43 = (bf16[16,4,128,128]{3,2,1,0:T(8,128)(2,1)}, bf16[16,4,128,128]{3,2,1,0:T(8,128)(2,1)}, u32[]{:S(2)}, u32[]{:S(2)}) collective-permute-start(bf16[16,4,128,128]{3,2,1,0:T(8,128)(2,1)} %get-tuple-element.84), channel_id=1, source_target_pairs={{0,6},{1,7},{2,0},{3,1},{4,2},{5,3},{6,4},{7,5},{8,14},{9,15},{10,... | collective-permute-start | bytes 6291464 | tf_op jit(solution)/shard_map/ppermute | solution.py:38
  210.6 52.2 %copy-start.7 = (bf16[8,2,128,128]{3,2,1,0:T(8,128)(2,1)}, bf16[8,2,128,128]{3,2,1,0:T(8,128)(2,1)S(1)}, u32[]{:S(2)}) copy-start(bf16[8,2,128,128]{3,2,1,0:T(8,128)(2,1)S(1)} %collective-permute-done.21.refs_10_) | copy-start | bytes 1572868
  210.6 52.2 %collective-permute-start.24 = (bf16[8,2,128,128]{3,2,1,0:T(8,128)(2,1)}, bf16[8,2,128,128]{3,2,1,0:T(8,128)(2,1)S(1)}, u32[]{:S(2)}, u32[]{:S(2)}) collective-permute-start(bf16[8,2,128,128]{3,2,1,0:T(8,128)(2,1)} %get-tuple-element.68), channel_id=1, source_target_pairs={{0,17},{1,16},{2,19},{3,18},{4,21},{5,20},{6,23},{7,22},{8,25},{9,... | collective-permute-start | bytes 1572872 | tf_op jit(solution)/shard_map/ppermute | solution.py:38
  216.9 45.9 %copy-start.8 = (bf16[8,2,128,128]{3,2,1,0:T(8,128)(2,1)}, bf16[8,2,128,128]{3,2,1,0:T(8,128)(2,1)S(1)}, u32[]{:S(2)}) copy-start(bf16[8,2,128,128]{3,2,1,0:T(8,128)(2,1)S(1)} %collective-permute-done.22.refs_11_) | copy-start | bytes 1572868
  216.9 50.6 %collective-permute-start.25 = (bf16[8,2,128,128]{3,2,1,0:T(8,128)(2,1)}, bf16[8,2,128,128]{3,2,1,0:T(8,128)(2,1)}, u32[]{:S(2)}, u32[]{:S(2)}) collective-permute-start(bf16[8,2,128,128]{3,2,1,0:T(8,128)(2,1)} %get-tuple-element.69), channel_id=1, source_target_pairs={{0,24},{1,25},{2,26},{3,27},{4,28},{5,29},{6,30},{7,31},{8,0},{9,1... | collective-permute-start | bytes 1572872 | tf_op jit(solution)/shard_map/ppermute | solution.py:38
  235.2 27.5 %copy-start.9 = (bf16[8,2,128,128]{3,2,1,0:T(8,128)(2,1)}, bf16[8,2,128,128]{3,2,1,0:T(8,128)(2,1)S(1)}, u32[]{:S(2)}) copy-start(bf16[8,2,128,128]{3,2,1,0:T(8,128)(2,1)S(1)} %collective-permute-done.23.refs_12_) | copy-start | bytes 1572868
  235.2 32.3 %collective-permute-start.26 = (bf16[8,2,128,128]{3,2,1,0:T(8,128)(2,1)}, bf16[8,2,128,128]{3,2,1,0:T(8,128)(2,1)}, u32[]{:S(2)}, u32[]{:S(2)}) collective-permute-start(bf16[8,2,128,128]{3,2,1,0:T(8,128)(2,1)} %get-tuple-element.70), channel_id=1, source_target_pairs={{0,25},{1,24},{2,27},{3,26},{4,29},{5,28},{6,31},{7,30},{8,1},{9,0... | collective-permute-start | bytes 1572872 | tf_op jit(solution)/shard_map/ppermute | solution.py:38
  263.6 64.9 %collective-permute-start.30 = (bf16[16,5,128,128]{3,2,1,0:T(8,128)(2,1)}, bf16[16,5,128,128]{3,2,1,0:T(8,128)(2,1)S(1)}, u32[]{:S(2)}, u32[]{:S(2)}) collective-permute-start(bf16[16,5,128,128]{3,2,1,0:T(8,128)(2,1)} %get-tuple-element.72), channel_id=1, source_target_pairs={{0,8},{1,9},{2,10},{3,11},{4,12},{5,13},{6,14},{7,15},{8,16},{9,17... | collective-permute-start | bytes 7864328 | tf_op jit(solution)/shard_map/ppermute | solution.py:38
  267.4 13.3 %collective-permute-start.10 = (bf16[8,2,128,128]{3,2,1,0:T(8,128)(2,1)}, bf16[8,2,128,128]{3,2,1,0:T(8,128)(2,1)S(1)}, u32[]{:S(2)}, u32[]{:S(2)}) collective-permute-start(bf16[8,2,128,128]{3,2,1,0:T(8,128)(2,1)} %get-tuple-element.56), channel_id=1, source_target_pairs={{0,4},{1,5},{2,6},{3,7},{4,0},{5,1},{6,2},{7,3},{8,12},{9,13},{10,... | collective-permute-start | bytes 1572872 | tf_op jit(solution)/shard_map/ppermute | solution.py:38
  267.5 61.5 %collective-permute-start.31 = (bf16[16,5,128,128]{3,2,1,0:T(8,128)(2,1)}, bf16[16,5,128,128]{3,2,1,0:T(8,128)(2,1)}, u32[]{:S(2)}, u32[]{:S(2)}) collective-permute-start(bf16[16,5,128,128]{3,2,1,0:T(8,128)(2,1)} %get-tuple-element.73), channel_id=1, source_target_pairs={{0,24},{1,25},{2,26},{3,27},{4,28},{5,29},{6,30},{7,31},{8,0},{9,1... | collective-permute-start | bytes 7864328 | tf_op jit(solution)/shard_map/ppermute | solution.py:38
  280.8 40.2 %copy-start.11 = (bf16[8,2,128,128]{3,2,1,0:T(8,128)(2,1)}, bf16[8,2,128,128]{3,2,1,0:T(8,128)(2,1)S(1)}, u32[]{:S(2)}) copy-start(bf16[8,2,128,128]{3,2,1,0:T(8,128)(2,1)S(1)} %collective-permute-done.10.refs_4_) | copy-start | bytes 1572868
  280.8 14.6 %collective-permute-start.11 = (bf16[8,2,128,128]{3,2,1,0:T(8,128)(2,1)}, bf16[8,2,128,128]{3,2,1,0:T(8,128)(2,1)}, u32[]{:S(2)}, u32[]{:S(2)}) collective-permute-start(bf16[8,2,128,128]{3,2,1,0:T(8,128)(2,1)} %get-tuple-element.57), channel_id=1, source_target_pairs={{0,5},{1,4},{2,7},{3,6},{4,1},{5,0},{6,3},{7,2},{8,13},{9,12},{10,... | collective-permute-start | bytes 1572872 | tf_op jit(solution)/shard_map/ppermute | solution.py:38
  295.4 16.3 %collective-permute-start.12 = (bf16[8,2,128,128]{3,2,1,0:T(8,128)(2,1)}, bf16[8,2,128,128]{3,2,1,0:T(8,128)(2,1)}, u32[]{:S(2)}, u32[]{:S(2)}) collective-permute-start(bf16[8,2,128,128]{3,2,1,0:T(8,128)(2,1)} %get-tuple-element.58), channel_id=1, source_target_pairs={{0,6},{1,7},{2,0},{3,1},{4,2},{5,3},{6,4},{7,5},{8,14},{9,15},{10,... | collective-permute-start | bytes 1572872 | tf_op jit(solution)/shard_map/ppermute | solution.py:38
  311.7 14.0 %collective-permute-start.13 = (bf16[8,2,128,128]{3,2,1,0:T(8,128)(2,1)}, bf16[8,2,128,128]{3,2,1,0:T(8,128)(2,1)}, u32[]{:S(2)}, u32[]{:S(2)}) collective-permute-start(bf16[8,2,128,128]{3,2,1,0:T(8,128)(2,1)} %get-tuple-element.59), channel_id=1, source_target_pairs={{0,7},{1,6},{2,1},{3,0},{4,3},{5,2},{6,5},{7,4},{8,15},{9,14},{10,... | collective-permute-start | bytes 1572872 | tf_op jit(solution)/shard_map/ppermute | solution.py:38
  313.0 12.8 %collective-permute-start.7 = (bf16[8,2,128,128]{3,2,1,0:T(8,128)(2,1)}, bf16[8,2,128,128]{3,2,1,0:T(8,128)(2,1)}, u32[]{:S(2)}, u32[]{:S(2)}) collective-permute-start(bf16[8,2,128,128]{3,2,1,0:T(8,128)(2,1)} %get-tuple-element.53), channel_id=1, source_target_pairs={{0,1},{1,0},{2,3},{3,2},{4,5},{5,4},{6,7},{7,6},{8,9},{9,8},{10,11... | collective-permute-start | bytes 1572872 | tf_op jit(solution)/shard_map/ppermute | solution.py:38
  314.3 14.2 %collective-permute-start.8 = (bf16[8,2,128,128]{3,2,1,0:T(8,128)(2,1)}, bf16[8,2,128,128]{3,2,1,0:T(8,128)(2,1)}, u32[]{:S(2)}, u32[]{:S(2)}) collective-permute-start(bf16[8,2,128,128]{3,2,1,0:T(8,128)(2,1)} %get-tuple-element.54), channel_id=1, source_target_pairs={{0,2},{1,3},{2,4},{3,5},{4,6},{5,7},{6,0},{7,1},{8,10},{9,11},{10,... | collective-permute-start | bytes 1572872 | tf_op jit(solution)/shard_map/ppermute | solution.py:38
  325.7 18.8 %collective-permute-start.44 = (bf16[8,4,128,128]{3,2,1,0:T(8,128)(2,1)}, bf16[8,4,128,128]{3,2,1,0:T(8,128)(2,1)}, u32[]{:S(2)}, u32[]{:S(2)}) collective-permute-start(bf16[8,4,128,128]{3,2,1,0:T(8,128)(2,1)} %get-tuple-element.86), channel_id=1, source_target_pairs={{0,1},{1,0},{2,3},{3,2},{4,5},{5,4},{6,7},{7,6},{8,9},{9,8},{10,11... | collective-permute-start | bytes 3145736 | tf_op jit(solution)/shard_map/ppermute | solution.py:38
  325.8 26.3 %collective-permute-start.45 = (bf16[8,4,128,128]{3,2,1,0:T(8,128)(2,1)}, bf16[8,4,128,128]{3,2,1,0:T(8,128)(2,1)}, u32[]{:S(2)}, u32[]{:S(2)}) collective-permute-start(bf16[8,4,128,128]{3,2,1,0:T(8,128)(2,1)} %get-tuple-element.87), channel_id=1, source_target_pairs={{0,8},{1,9},{2,10},{3,11},{4,12},{5,13},{6,14},{7,15},{8,16},{9,17... | collective-permute-start | bytes 3145736 | tf_op jit(solution)/shard_map/ppermute | solution.py:38
  328.5 45.0 %collective-permute-start.46 = (bf16[8,4,128,128]{3,2,1,0:T(8,128)(2,1)}, bf16[8,4,128,128]{3,2,1,0:T(8,128)(2,1)}, u32[]{:S(2)}, u32[]{:S(2)}) collective-permute-start(bf16[8,4,128,128]{3,2,1,0:T(8,128)(2,1)} %get-tuple-element.88), channel_id=1, source_target_pairs={{0,9},{1,8},{2,11},{3,10},{4,13},{5,12},{6,15},{7,14},{8,17},{9,16... | collective-permute-start | bytes 3145736 | tf_op jit(solution)/shard_map/ppermute | solution.py:38
  328.5 69.3 %collective-permute-start.47 = (bf16[8,4,128,128]{3,2,1,0:T(8,128)(2,1)}, bf16[8,4,128,128]{3,2,1,0:T(8,128)(2,1)}, u32[]{:S(2)}, u32[]{:S(2)}) collective-permute-start(bf16[8,4,128,128]{3,2,1,0:T(8,128)(2,1)} %get-tuple-element.89), channel_id=1, source_target_pairs={{0,16},{1,17},{2,18},{3,19},{4,20},{5,21},{6,22},{7,23},{8,24},{9,... | collective-permute-start | bytes 3145736 | tf_op jit(solution)/shard_map/ppermute | solution.py:38
  329.0 15.5 %collective-permute-start.9 = (bf16[8,2,128,128]{3,2,1,0:T(8,128)(2,1)}, bf16[8,2,128,128]{3,2,1,0:T(8,128)(2,1)S(1)}, u32[]{:S(2)}, u32[]{:S(2)}) collective-permute-start(bf16[8,2,128,128]{3,2,1,0:T(8,128)(2,1)} %get-tuple-element.55), channel_id=1, source_target_pairs={{0,3},{1,2},{2,5},{3,4},{4,7},{5,6},{6,1},{7,0},{8,11},{9,10},{10,... | collective-permute-start | bytes 1572872 | tf_op jit(solution)/shard_map/ppermute | solution.py:38
  344.5 216.8 %copy-start.12 = (bf16[8,2,128,128]{3,2,1,0:T(8,128)(2,1)}, bf16[8,2,128,128]{3,2,1,0:T(8,128)(2,1)S(1)}, u32[]{:S(2)}) copy-start(bf16[8,2,128,128]{3,2,1,0:T(8,128)(2,1)S(1)} %collective-permute-done.9.refs_3_) | copy-start | bytes 1572868
  344.5 126.2 %collective-permute-start.32 = (bf16[8,5,128,128]{3,2,1,0:T(8,128)(2,1)}, bf16[8,5,128,128]{3,2,1,0:T(8,128)(2,1)S(1)}, u32[]{:S(2)}, u32[]{:S(2)}) collective-permute-start(bf16[8,5,128,128]{3,2,1,0:T(8,128)(2,1)} %get-tuple-element.75), channel_id=1, source_target_pairs={{0,1},{1,0},{2,3},{3,2},{4,5},{5,4},{6,7},{7,6},{8,9},{9,8},{10,11... | collective-permute-start | bytes 3932168 | tf_op jit(solution)/shard_map/ppermute | solution.py:38
  344.5 126.2 %collective-permute-start.33 = (bf16[8,5,128,128]{3,2,1,0:T(8,128)(2,1)}, bf16[8,5,128,128]{3,2,1,0:T(8,128)(2,1)S(1)}, u32[]{:S(2)}, u32[]{:S(2)}) collective-permute-start(bf16[8,5,128,128]{3,2,1,0:T(8,128)(2,1)} %get-tuple-element.76), channel_id=1, source_target_pairs={{0,2},{1,3},{2,4},{3,5},{4,6},{5,7},{6,0},{7,1},{8,10},{9,11},{10,... | collective-permute-start | bytes 3932168 | tf_op jit(solution)/shard_map/ppermute | solution.py:38
  352.1 66.1 %collective-permute-start.48 = (bf16[8,4,128,128]{3,2,1,0:T(8,128)(2,1)}, bf16[8,4,128,128]{3,2,1,0:T(8,128)(2,1)S(1)}, u32[]{:S(2)}, u32[]{:S(2)}) collective-permute-start(bf16[8,4,128,128]{3,2,1,0:T(8,128)(2,1)} %get-tuple-element.90), channel_id=1, source_target_pairs={{0,17},{1,16},{2,19},{3,18},{4,21},{5,20},{6,23},{7,22},{8,25},{9,... | collective-permute-start | bytes 3145736 | tf_op jit(solution)/shard_map/ppermute | solution.py:38
  373.5 47.1 %collective-permute-start.49 = (bf16[8,4,128,128]{3,2,1,0:T(8,128)(2,1)}, bf16[8,4,128,128]{3,2,1,0:T(8,128)(2,1)S(1)}, u32[]{:S(2)}, u32[]{:S(2)}) collective-permute-start(bf16[8,4,128,128]{3,2,1,0:T(8,128)(2,1)} %get-tuple-element.91), channel_id=1, source_target_pairs={{0,24},{1,25},{2,26},{3,27},{4,28},{5,29},{6,30},{7,31},{8,0},{9,1... | collective-permute-start | bytes 3145736 | tf_op jit(solution)/shard_map/ppermute | solution.py:38
  397.8 51.2 %collective-permute-start.50 = (bf16[8,4,128,128]{3,2,1,0:T(8,128)(2,1)}, bf16[8,4,128,128]{3,2,1,0:T(8,128)(2,1)S(1)}, u32[]{:S(2)}, u32[]{:S(2)}) collective-permute-start(bf16[8,4,128,128]{3,2,1,0:T(8,128)(2,1)} %get-tuple-element.92), channel_id=1, source_target_pairs={{0,25},{1,24},{2,27},{3,26},{4,29},{5,28},{6,31},{7,30},{8,1},{9,0... | collective-permute-start | bytes 3145736 | tf_op jit(solution)/shard_map/ppermute | solution.py:38
  418.3 52.4 %copy-start.3 = (bf16[8,4,128,128]{3,2,1,0:T(8,128)(2,1)}, bf16[8,4,128,128]{3,2,1,0:T(8,128)(2,1)S(1)}, u32[]{:S(2)}) copy-start(bf16[8,4,128,128]{3,2,1,0:T(8,128)(2,1)S(1)} %collective-permute-done.48.refs_29_) | copy-start | bytes 3145732
  418.3 55.3 %collective-permute-start.34 = (bf16[8,5,128,128]{3,2,1,0:T(8,128)(2,1)}, bf16[8,5,128,128]{3,2,1,0:T(8,128)(2,1)}, u32[]{:S(2)}, u32[]{:S(2)}) collective-permute-start(bf16[8,5,128,128]{3,2,1,0:T(8,128)(2,1)} %get-tuple-element.77), channel_id=1, source_target_pairs={{0,3},{1,2},{2,5},{3,4},{4,7},{5,6},{6,1},{7,0},{8,11},{9,10},{10,... | collective-permute-start | bytes 3932168 | tf_op jit(solution)/shard_map/ppermute | solution.py:38
  420.6 50.1 %copy-start.4 = (bf16[8,4,128,128]{3,2,1,0:T(8,128)(2,1)}, bf16[8,4,128,128]{3,2,1,0:T(8,128)(2,1)S(1)}, u32[]{:S(2)}) copy-start(bf16[8,4,128,128]{3,2,1,0:T(8,128)(2,1)S(1)} %collective-permute-done.49.refs_30_) | copy-start | bytes 3145732
  420.6 58.5 %collective-permute-start.35 = (bf16[8,5,128,128]{3,2,1,0:T(8,128)(2,1)}, bf16[8,5,128,128]{3,2,1,0:T(8,128)(2,1)}, u32[]{:S(2)}, u32[]{:S(2)}) collective-permute-start(bf16[8,5,128,128]{3,2,1,0:T(8,128)(2,1)} %get-tuple-element.78), channel_id=1, source_target_pairs={{0,4},{1,5},{2,6},{3,7},{4,0},{5,1},{6,2},{7,3},{8,12},{9,13},{10,... | collective-permute-start | bytes 3932168 | tf_op jit(solution)/shard_map/ppermute | solution.py:38
  449.0 21.7 %copy-start.5 = (bf16[8,4,128,128]{3,2,1,0:T(8,128)(2,1)}, bf16[8,4,128,128]{3,2,1,0:T(8,128)(2,1)S(1)}, u32[]{:S(2)}) copy-start(bf16[8,4,128,128]{3,2,1,0:T(8,128)(2,1)S(1)} %collective-permute-done.50.refs_31_) | copy-start | bytes 3145732
  449.0 57.6 %collective-permute-start.36 = (bf16[8,5,128,128]{3,2,1,0:T(8,128)(2,1)}, bf16[8,5,128,128]{3,2,1,0:T(8,128)(2,1)}, u32[]{:S(2)}, u32[]{:S(2)}) collective-permute-start(bf16[8,5,128,128]{3,2,1,0:T(8,128)(2,1)} %get-tuple-element.79), channel_id=1, source_target_pairs={{0,5},{1,4},{2,7},{3,6},{4,1},{5,0},{6,3},{7,2},{8,13},{9,12},{10,... | collective-permute-start | bytes 3932168 | tf_op jit(solution)/shard_map/ppermute | solution.py:38
  470.7 90.7 %copy-start.1 = (bf16[8,5,128,128]{3,2,1,0:T(8,128)(2,1)}, bf16[8,5,128,128]{3,2,1,0:T(8,128)(2,1)S(1)}, u32[]{:S(2)}) copy-start(bf16[8,5,128,128]{3,2,1,0:T(8,128)(2,1)S(1)} %collective-permute-done.32.refs_17_) | copy-start | bytes 3932164
  470.7 64.1 %collective-permute-start.37 = (bf16[8,5,128,128]{3,2,1,0:T(8,128)(2,1)}, bf16[8,5,128,128]{3,2,1,0:T(8,128)(2,1)}, u32[]{:S(2)}, u32[]{:S(2)}) collective-permute-start(bf16[8,5,128,128]{3,2,1,0:T(8,128)(2,1)} %get-tuple-element.80), channel_id=1, source_target_pairs={{0,6},{1,7},{2,0},{3,1},{4,2},{5,3},{6,4},{7,5},{8,14},{9,15},{10,... | collective-permute-start | bytes 3932168 | tf_op jit(solution)/shard_map/ppermute | solution.py:38
  470.7 90.6 %copy-start.2 = (bf16[8,5,128,128]{3,2,1,0:T(8,128)(2,1)}, bf16[8,5,128,128]{3,2,1,0:T(8,128)(2,1)S(1)}, u32[]{:S(2)}) copy-start(bf16[8,5,128,128]{3,2,1,0:T(8,128)(2,1)S(1)} %collective-permute-done.33.refs_18_) | copy-start | bytes 3932164
  470.7 90.6 %collective-permute-start.38 = (bf16[8,5,128,128]{3,2,1,0:T(8,128)(2,1)}, bf16[8,5,128,128]{3,2,1,0:T(8,128)(2,1)}, u32[]{:S(2)}, u32[]{:S(2)}) collective-permute-start(bf16[8,5,128,128]{3,2,1,0:T(8,128)(2,1)} %get-tuple-element.81), channel_id=1, source_target_pairs={{0,7},{1,6},{2,1},{3,0},{4,3},{5,2},{6,5},{7,4},{8,15},{9,14},{10,... | collective-permute-start | bytes 3932168 | tf_op jit(solution)/shard_map/ppermute | solution.py:38
  (6 other events, 19.7 us)

commit v5 on v4

--- a/solution.py
+++ b/solution.py
@@ -8,7 +8,7 @@
 from jax.sharding import PartitionSpec as P
 
 
-CHUNKS = (("x", 2), ("z", 2), ("x", 5), ("z", 4))
+CHUNKS = (("x", 3), ("z", 3), ("x", 4), ("z", 3))
 RING = 4
 LANES = 2 * RING
 ABREAST = 4
@@ -28,14 +28,18 @@
     return jnp.where(mag <= 1.0, near, jnp.where(mag < 2.0, far, jnp.zeros_like(mag)))
 
 
-def hop(value, along, steps, cross=0):
+def ring_pairs(along, steps, cross):
     pairs = []
     for x in range(RING):
         for z in range(RING):
             for core in range(2):
                 to_x, to_z = ((x + steps) % RING, z) if along == "x" else (x, (z + steps) % RING)
                 pairs.append(((x * RING + z) * 2 + core, (to_x * RING + to_z) * 2 + (core ^ cross)))
-    return lax.ppermute(value, "tile", pairs)
+    return pairs
+
+
+def hop(value, along, steps, cross=0):
+    return lax.ppermute(value, "tile", ring_pairs(along, steps, cross))
 
 
 def pick_kernel(first, bands, listed_ref, tiles_ref, picked_ref, held, in_sem, out_sem):
@@ -283,12 +287,26 @@
         parts.append((axis, first, bands))
         first += bands
 
+    def next_zone(value, along, steps):
+        pairs = []
+        zones = lax.axis_size("zone")
+        for zone in range(zones - 1):
+            for source, target in ring_pairs(along, steps, 0):
+                pairs.append((zone * tile_count + source, (zone + 1) * tile_count + target))
+        return lax.ppermute(value, ("zone", "tile"), pairs)
+
+    near_list = passed_along(seam_list, "zone", 1)
+    near_list_by = {axis: next_zone(seam_list, axis, 1) for axis in ("x", "z")}
+    list_by = {axis: hop(seam_list, axis, 1) for axis in ("x", "z")}
+
     nears, beyonds, nears_beyond = [], [], []
-    for axis, first, bands in parts:
+    for part, (axis, first, bands) in enumerate(parts):
         nears.append(passed_along(pick(seam_list, tiles, first, bands), "zone", 1))
         beyonds.append(hop(tiles[:, first : first + bands], axis, 1))
-        nears_beyond.append(hop(nears[-1], axis, 1))
-    near_list = passed_along(seam_list, "zone", 1)
+        if part == 0:
+            nears_beyond.append(hop(nears[0], axis, 1))
+        else:
+            nears_beyond.append(passed_along(pick(list_by[axis], beyonds[part], 0, bands), "zone", 1))
 
     def coordinates(device):
         return device // (2 * RING), (device // 2) % RING, device % 2
@@ -337,7 +355,7 @@
     taps = jnp.concatenate([cubic_weight(step - fractions[:, axis]) for axis in range(2) for step in STEPS])
     flat_offsets = offsets.reshape(-1)
     zone_flag = zone_index[None].astype(jnp.int32)
-    listed_by = {axis: jnp.concatenate([near_list, hop(near_list, axis, 1), zone_flag]) for axis in ("x", "z")}
+    listed_by = {axis: jnp.concatenate([near_list, near_list_by[axis], zone_flag]) for axis in ("x", "z")}
 
     arrays = []
     for part, (axis, first, bands) in enumerate(parts):

time: 575 us -> 665 us (1.16); the launches traced: 570 us -> 651 us
  waiting for transfers between devices: 298 us -> 418 us
  starting transfers between devices: 130 us -> 75.7 us
  Pallas kernels: 126 us -> 134 us
    ppermute x46 -> x45, waiting for transfers between devices: 267 us -> 357 us  [the longest x43 357 us: hop(): return lax.ppermute(value, 'tile', ring_pairs(along, steps, cross))]
    ppermute x46 -> x45, starting transfers between devices: 124 us -> 65.1 us  [the longest x43 62.5 us: hop(): return lax.ppermute(value, 'tile', ring_pairs(along, steps, cross))]
    ppermute x5 -> x8, waiting for transfers between devices: 30.8 us -> 60.4 us  [passed_along(): lax.ppermute(value, axis, [(source, source + steps) for source in range(i...]
    pallas_call x4 -> x7, Pallas kernels: 10.6 us -> 18.5 us  [pick(): pl.pallas_call(functools.partial(pick_kernel, first, bands), out_shape=ja...]
  transfers between devices with their start and end apart: 51 -> 53, of which waited for: 21 -> 21; matrix products, arithmetic and copies ran while one was open for 2% -> 3% of each run, Pallas kernels for 21% -> 19%
where the time goes in v5:
time: 665 us; the launch traced here: 651 us
  waiting for transfers between devices  418 us (63%)
  Pallas kernels  134 us (20%)
  starting transfers between devices  75.7 us (11%)
  local copies, waits for them, and re-layouts  11.8 us (2%)
  other arithmetic  11 us (2%)
    ppermute x43, waiting for transfers between devices, hop(): return lax.ppermute(value, 'tile', ring_pairs(along, steps, cross))  357 us
    pallas_call x4, Pallas kernels, render(): pl.pallas_call(functools.partial(render_kernel, local_count, first, bands...  83.8 us
    ppermute x43, starting transfers between devices, hop(): return lax.ppermute(value, 'tile', ring_pairs(along, steps, cross))  62.5 us
    ppermute x8, waiting for transfers between devices, passed_along(): lax.ppermute(value, axis, [(source, source + steps) for source in range(i...  60.4 us
    pallas_call x4, Pallas kernels, pack(): pl.pallas_call(pack_kernel, out_shape=[jax.ShapeDtypeStruct(shape, stay.d...  23.6 us
    pallas_call x7, Pallas kernels, pick(): pl.pallas_call(functools.partial(pick_kernel, first, bands), out_shape=ja...  18.5 us
  transfers between devices with their start and end apart: 53, of which 21 were waited for; matrix products, arithmetic and copies ran while one was open for 3% of the time, Pallas kernels for 19%

profile of v5, /device:TPU:60, one launch (start us, length us, event | category | flops | bytes accessed | tf_op | source)
XLA Modules:
  0.0 651.3 jit_solution(15994663895108065338)
XLA Ops:
  0.0 1.9 collective-permute-start.17
  3.2 1.3 collective-permute-start.1
  4.5 2.6 pick.7
  7.1 1.3 collective-permute-start.3
  8.4 1.5 slice.28
  15.0 3.9 fusion.49
  18.9 1.3 collective-permute-start
  20.2 1.7 collective-permute-start.41
  22.0 8.7 %collective-permute-done = s32[2]{0:T(128)S(1)} collective-permute-done((s32[2]{0:T(128)S(1)}, s32[2]{0:T(128)S(1)}, u32[]{:S(2)}, u32[]{:S(2)}) %collective-permute-start) | collective-permute-done | bytes 40 | tf_op jit(solution)/shard_map/ppermute | solution.py:21
  32.4 1.8 select_reduce_fusion
  34.3 2.6 pick.8
  36.9 2.6 pick.12
  39.5 2.7 pick.10
  44.0 1.3 fusion.27
  45.3 1.3 fusion.30
  46.6 1.3 fusion.33.taps_ref
  47.9 1.3 add_add_fusion.1
  50.7 2.6 pick.13
  53.3 19.7 %collective-permute-done.15.tiles_ref.beyond_ref = bf16[3,3,256,256]{3,2,1,0:T(8,128)(2,1)} collective-permute-done((bf16[3,3,256,256]{3,2,1,0:T(8,128)(2,1)}, bf16[3,3,256,256]{3,2,1,0:T(8,128)(2,1)}, u32[]{:S(2)}, u32[]{:S(2)}) %collective-permute-start.15) | collective-permute-done | bytes 1179680 | tf_op jit(solution)/shard_map/ppermute | solution.py:42
  74.3 2.6 pick.9
  76.9 11.2 %collective-permute-done.30.listed_ref = s32[2]{0:T(128)S(1)} collective-permute-done((s32[2]{0:T(128)}, s32[2]{0:T(128)S(1)}, u32[]{:S(2)}, u32[]{:S(2)}) %collective-permute-start.30) | collective-permute-done | bytes 40 | tf_op jit(solution)/shard_map/ppermute | solution.py:42
  88.1 1.3 collective-permute-start.16
  89.4 1.6 collective-permute-start.29
  91.0 2.8 pick.11
  93.8 1.3 collective-permute-start.43
  95.2 1.3 collective-permute-start.18
  96.5 21.0 %render.4 = (bf16[32,3,128,128]{3,2,1,0:T(8,128)(2,1)}, bf16[16,3,128,128]{3,2,1,0:T(8,128)(2,1)}, bf16[16,3,128,128]{3,2,1,0:T(8,128)(2,1)}) custom-call(s32[1]{0:T(128)} %bitcast.1.count_ref, s32[64]{0:T(128)} %get-tuple-element.127.blocks_ref, s32[64]{0:T(128)} %get-tuple-element.128.into_ref, s32[64]{0:T(128)} %get-tuple-element.129.side_ref, ...), custom_call_target="tpu_custom_call" | custom-call | flops 14495514624 | bytes 2359296 | tf_op jit(solution)/shard_map/render/pallas_call | solution.py:169
  117.5 51.7 %collective-permute-done.18.near_beyond_ref = bf16[2,3,256,256]{3,2,1,0:T(8,128)(2,1)S(1)} collective-permute-done((bf16[2,3,256,256]{3,2,1,0:T(8,128)(2,1)S(1)}, bf16[2,3,256,256]{3,2,1,0:T(8,128)(2,1)S(1)}, u32[]{:S(2)}, u32[]{:S(2)}) %collective-permute-start.18) | collective-permute-done | bytes 786464 | tf_op jit(solution)/shard_map/ppermute | solution.py:21
  171.0 19.4 %render.5 = (bf16[32,3,128,128]{3,2,1,0:T(8,128)(2,1)}, bf16[16,3,128,128]{3,2,1,0:T(8,128)(2,1)}, bf16[16,3,128,128]{3,2,1,0:T(8,128)(2,1)}) custom-call(s32[1]{0:T(128)} %bitcast.3.count_ref, s32[64]{0:T(128)} %get-tuple-element.95.blocks_ref, s32[64]{0:T(128)} %get-tuple-element.94.into_ref, s32[64]{0:T(128)} %get-tuple-element.93.side_ref, ...), custom_call_target="tpu_custom_call" | custom-call | flops 14495514624 | bytes 2359296 | tf_op jit(solution)/shard_map/render/pallas_call | solution.py:169
  190.4 1.3 collective-permute-start.31
  191.7 12.0 %collective-permute-start.19 = (bf16[16,3,128,128]{3,2,1,0:T(8,128)(2,1)}, bf16[16,3,128,128]{3,2,1,0:T(8,128)(2,1)}, u32[]{:S(2)}, u32[]{:S(2)}) collective-permute-start(bf16[16,3,128,128]{3,2,1,0:T(8,128)(2,1)} %get-tuple-element.61), channel_id=1, source_target_pairs={{0,2},{1,3},{2,4},{3,5},{4,6},{5,7},{6,0},{7,1},{8,10},{9,11},{10,... | collective-permute-start | bytes 4718600 | tf_op jit(solution)/shard_map/ppermute | solution.py:42
  203.7 19.4 %render.7 = (bf16[32,3,128,128]{3,2,1,0:T(8,128)(2,1)}, bf16[16,3,128,128]{3,2,1,0:T(8,128)(2,1)}, bf16[16,3,128,128]{3,2,1,0:T(8,128)(2,1)}) custom-call(s32[1]{0:T(128)} %bitcast.3.count_ref, s32[64]{0:T(128)} %get-tuple-element.95.blocks_ref, s32[64]{0:T(128)} %get-tuple-element.94.into_ref, s32[64]{0:T(128)} %get-tuple-element.93.side_ref, ...), custom_call_target="tpu_custom_call" | custom-call | flops 14495514624 | bytes 2359296 | tf_op jit(solution)/shard_map/render/pallas_call | solution.py:169
  224.4 11.4 %collective-permute-start.44 = (bf16[16,3,128,128]{3,2,1,0:T(8,128)(2,1)}, bf16[16,3,128,128]{3,2,1,0:T(8,128)(2,1)S(1)}, u32[]{:S(2)}, u32[]{:S(2)}) collective-permute-start(bf16[16,3,128,128]{3,2,1,0:T(8,128)(2,1)} %get-tuple-element.83), channel_id=1, source_target_pairs={{0,2},{1,3},{2,4},{3,5},{4,6},{5,7},{6,0},{7,1},{8,10},{9,11},{10,... | collective-permute-start | bytes 4718600 | tf_op jit(solution)/shard_map/ppermute | solution.py:42
  236.9 5.7 pack.4
  242.7 2.1 collective-permute-start.8
  244.8 25.3 %collective-permute-done.20.down_ref = bf16[16,3,128,128]{3,2,1,0:T(8,128)(2,1)} collective-permute-done((bf16[16,3,128,128]{3,2,1,0:T(8,128)(2,1)}, bf16[16,3,128,128]{3,2,1,0:T(8,128)(2,1)}, u32[]{:S(2)}, u32[]{:S(2)}) %collective-permute-start.20) | collective-permute-done | bytes 1572896 | tf_op jit(solution)/shard_map/ppermute | solution.py:42
  271.0 3.7 collective-permute-start.10
  274.7 28.2 %collective-permute-done.45.down_ref = bf16[16,3,128,128]{3,2,1,0:T(8,128)(2,1)S(1)} collective-permute-done((bf16[16,3,128,128]{3,2,1,0:T(8,128)(2,1)}, bf16[16,3,128,128]{3,2,1,0:T(8,128)(2,1)S(1)}, u32[]{:S(2)}, u32[]{:S(2)}) %collective-permute-start.45) | collective-permute-done | bytes 1572896 | tf_op jit(solution)/shard_map/ppermute | solution.py:42
  303.0 4.7 collective-permute-start.13
  307.7 24.1 %render.6 = (bf16[32,4,128,128]{3,2,1,0:T(8,128)(2,1)}, bf16[16,4,128,128]{3,2,1,0:T(8,128)(2,1)}, bf16[16,4,128,128]{3,2,1,0:T(8,128)(2,1)}) custom-call(s32[1]{0:T(128)} %bitcast.1.count_ref, s32[64]{0:T(128)} %get-tuple-element.127.blocks_ref, s32[64]{0:T(128)} %get-tuple-element.128.into_ref, s32[64]{0:T(128)} %get-tuple-element.129.side_ref, ...), custom_call_target="tpu_custom_call" | custom-call | flops 19327352832 | bytes 3145728 | tf_op jit(solution)/shard_map/render/pallas_call | solution.py:169
  331.8 4.9 collective-permute-done.9.refs_3_
  336.7 2.0 collective-permute-start.33
  338.8 5.7 pack.5
  344.6 8.1 %collective-permute-done.12.refs_6_ = bf16[8,3,128,128]{3,2,1,0:T(8,128)(2,1)} collective-permute-done((bf16[8,3,128,128]{3,2,1,0:T(8,128)(2,1)}, bf16[8,3,128,128]{3,2,1,0:T(8,128)(2,1)}, u32[]{:S(2)}, u32[]{:S(2)}) %collective-permute-start.12) | collective-permute-done | bytes 786464 | tf_op jit(solution)/shard_map/ppermute | solution.py:42
  352.7 16.9 %collective-permute-done.13.refs_7_ = bf16[8,3,128,128]{3,2,1,0:T(8,128)(2,1)} collective-permute-done((bf16[8,3,128,128]{3,2,1,0:T(8,128)(2,1)}, bf16[8,3,128,128]{3,2,1,0:T(8,128)(2,1)}, u32[]{:S(2)}, u32[]{:S(2)}) %collective-permute-start.13) | collective-permute-done | bytes 786464 | tf_op jit(solution)/shard_map/ppermute | solution.py:42
  369.5 32.9 %collective-permute-done.22.refs_10_ = bf16[8,3,128,128]{3,2,1,0:T(8,128)(2,1)} collective-permute-done((bf16[8,3,128,128]{3,2,1,0:T(8,128)(2,1)}, bf16[8,3,128,128]{3,2,1,0:T(8,128)(2,1)}, u32[]{:S(2)}, u32[]{:S(2)}) %collective-permute-start.22) | collective-permute-done | bytes 786464 | tf_op jit(solution)/shard_map/ppermute | solution.py:42
  402.4 45.5 %collective-permute-done.23.refs_11_ = bf16[8,3,128,128]{3,2,1,0:T(8,128)(2,1)} collective-permute-done((bf16[8,3,128,128]{3,2,1,0:T(8,128)(2,1)}, bf16[8,3,128,128]{3,2,1,0:T(8,128)(2,1)}, u32[]{:S(2)}, u32[]{:S(2)}) %collective-permute-start.23) | collective-permute-done | bytes 786464 | tf_op jit(solution)/shard_map/ppermute | solution.py:42
  448.0 2.1 collective-permute-start.26
  450.0 5.7 pack.7
  456.1 12.1 %collective-permute-done.26.refs_14_ = bf16[8,3,128,128]{3,2,1,0:T(8,128)(2,1)} collective-permute-done((bf16[8,3,128,128]{3,2,1,0:T(8,128)(2,1)}, bf16[8,3,128,128]{3,2,1,0:T(8,128)(2,1)}, u32[]{:S(2)}, u32[]{:S(2)}) %collective-permute-start.26) | collective-permute-done | bytes 786464 | tf_op jit(solution)/shard_map/ppermute | solution.py:42
  469.4 3.3 collective-permute-start.49
  472.7 6.6 %pack.6 = (bf16[8,4,128,128]{3,2,1,0:T(8,128)(2,1)}, bf16[8,4,128,128]{3,2,1,0:T(8,128)(2,1)}, bf16[8,4,128,128]{3,2,1,0:T(8,128)(2,1)}, bf16[8,4,128,128]{3,2,1...) custom-call(bf16[32,4,128,128]{3,2,1,0:T(8,128)(2,1)} %get-tuple-ele, ...), custom_call_target="tpu_custom_call" | custom-call | tf_op jit(solution)/shard_map/pack/pallas_call | solution.py:210
  479.4 7.5 %collective-permute-done.27.refs_15_ = bf16[8,3,128,128]{3,2,1,0:T(8,128)(2,1)} collective-permute-done((bf16[8,3,128,128]{3,2,1,0:T(8,128)(2,1)}, bf16[8,3,128,128]{3,2,1,0:T(8,128)(2,1)}, u32[]{:S(2)}, u32[]{:S(2)}) %collective-permute-start.27) | collective-permute-done | bytes 786464 | tf_op jit(solution)/shard_map/ppermute | solution.py:42
  486.9 4.6 collective-permute-start.35
  491.5 48.5 %collective-permute-done.48.refs_27_ = bf16[8,3,128,128]{3,2,1,0:T(8,128)(2,1)} collective-permute-done((bf16[8,3,128,128]{3,2,1,0:T(8,128)(2,1)}, bf16[8,3,128,128]{3,2,1,0:T(8,128)(2,1)}, u32[]{:S(2)}, u32[]{:S(2)}) %collective-permute-start.48) | collective-permute-done | bytes 786464 | tf_op jit(solution)/shard_map/ppermute | solution.py:42
  540.1 1.5 collective-permute-start.36
  541.6 18.5 %collective-permute-done.51.refs_30_ = bf16[8,3,128,128]{3,2,1,0:T(8,128)(2,1)S(1)} collective-permute-done((bf16[8,3,128,128]{3,2,1,0:T(8,128)(2,1)}, bf16[8,3,128,128]{3,2,1,0:T(8,128)(2,1)S(1)}, u32[]{:S(2)}, u32[]{:S(2)}) %collective-permute-start.51) | collective-permute-done | bytes 786464 | tf_op jit(solution)/shard_map/ppermute | solution.py:42
  560.2 2.2 collective-permute-start.39
  562.5 2.0 collective-permute-start.40
  566.2 21.7 %collective-permute-done.37.refs_20_ = bf16[8,4,128,128]{3,2,1,0:T(8,128)(2,1)} collective-permute-done((bf16[8,4,128,128]{3,2,1,0:T(8,128)(2,1)}, bf16[8,4,128,128]{3,2,1,0:T(8,128)(2,1)}, u32[]{:S(2)}, u32[]{:S(2)}) %collective-permute-start.37) | collective-permute-done | bytes 1048608 | tf_op jit(solution)/shard_map/ppermute | solution.py:42
  588.0 10.6 %collective-permute-done.38.refs_21_ = bf16[8,4,128,128]{3,2,1,0:T(8,128)(2,1)} collective-permute-done((bf16[8,4,128,128]{3,2,1,0:T(8,128)(2,1)}, bf16[8,4,128,128]{3,2,1,0:T(8,128)(2,1)}, u32[]{:S(2)}, u32[]{:S(2)}) %collective-permute-start.38) | collective-permute-done | bytes 1048608 | tf_op jit(solution)/shard_map/ppermute | solution.py:42
  598.5 22.5 %collective-permute-done.39.refs_22_ = bf16[8,4,128,128]{3,2,1,0:T(8,128)(2,1)} collective-permute-done((bf16[8,4,128,128]{3,2,1,0:T(8,128)(2,1)}, bf16[8,4,128,128]{3,2,1,0:T(8,128)(2,1)}, u32[]{:S(2)}, u32[]{:S(2)}) %collective-permute-start.39) | collective-permute-done | bytes 1048608 | tf_op jit(solution)/shard_map/ppermute | solution.py:42
  621.0 21.8 %collective-permute-done.40.refs_23_ = bf16[8,4,128,128]{3,2,1,0:T(8,128)(2,1)} collective-permute-done((bf16[8,4,128,128]{3,2,1,0:T(8,128)(2,1)}, bf16[8,4,128,128]{3,2,1,0:T(8,128)(2,1)}, u32[]{:S(2)}, u32[]{:S(2)}) %collective-permute-start.40) | collective-permute-done | bytes 1048608 | tf_op jit(solution)/shard_map/ppermute | solution.py:42
  642.8 8.3 %place.1 = bf16[24,13,128,128]{3,2,1,0:T(8,128)(2,1)} custom-call(s32[24]{0:T(128)} %add.470.x_lane_ref, s32[24]{0:T(128)} %get-tuple-element.138.x_slot_ref, s32[24]{0:T(128)} %get-tuple-element.120.z_lane_ref, s32[24]{0:T(128)} %get-tuple-element.118.z_slot_ref, bf16[8,3,128,128]{3,2,1,0:T(8,128)(2,1)} %get-tuple-element.52.refs_0_, ...), custom_call_target="tpu_custom_call" | custom-call | tf_op jit(solution)/shard_map/place/pallas_call | solution.py:263
  (161 shorter events, 21.4 us)
Async XLA Ops:
  0.0 18.9 %collective-permute-start.17 = (s32[2]{0:T(128)}, s32[2]{0:T(128)S(1)}, u32[]{:S(2)}, u32[]{:S(2)}) collective-permute-start(s32[2]{0:T(128)} %listed_ref.7), channel_id=1, source_target_pairs={{0,2},{1,3},{2,4},{3,5},{4,6},{5,7},{6,0},{7,1},{8,10},{9,11},{10,... | collective-permute-start | bytes 32 | tf_op jit(solution)/shard_map/ppermute | solution.py:42
  1.9 18.2 %collective-permute-start.14 = (s32[2]{0:T(128)}, s32[2]{0:T(128)S(1)}, u32[]{:S(2)}, u32[]{:S(2)}) collective-permute-start(s32[2]{0:T(128)} %listed_ref.7), channel_id=1, source_target_pairs={{0,34},{1,35},{2,36},{3,37},{4,38},{5,39},{6,32},{7,33},{8,42},{9,... | collective-permute-start | bytes 32 | tf_op jit(solution)/shard_map/ppermute | solution.py:296
  3.2 18.7 %collective-permute-start.1 = (s32[2]{0:T(128)}, s32[2]{0:T(128)S(1)}, u32[]{:S(2)}, u32[]{:S(2)}) collective-permute-start(s32[2]{0:T(128)} %listed_ref.7), channel_id=1, source_target_pairs={{0,40},{1,41},{2,42},{3,43},{4,44},{5,45},{6,46},{7,47},{8,48},{9,... | collective-permute-start | bytes 32 | tf_op jit(solution)/shard_map/ppermute | solution.py:296
  7.1 24.8 %collective-permute-start.3 = (bf16[2,3,256,256]{3,2,1,0:T(8,128)(2,1)}, bf16[2,3,256,256]{3,2,1,0:T(8,128)(2,1)}, u32[]{:S(2)}, u32[]{:S(2)}) collective-permute-start(bf16[2,3,256,256]{3,2,1,0:T(8,128)(2,1)} %pick.7), channel_id=1, source_target_pairs={{0,32},{32,64},{64,96},{1,33},{33,65},{65,97},{2,34},{34,66},{66,9... | collective-permute-start | bytes 2359304 | tf_op jit(solution)/shard_map/ppermute | solution.py:21
  9.9 79.5 %collective-permute-start.28 = (bf16[3,4,256,256]{3,2,1,0:T(8,128)(2,1)S(1)}, bf16[3,4,256,256]{3,2,1,0:T(8,128)(2,1)S(1)}, u32[]{:S(2)}, u32[]{:S(2)}) collective-permute-start(bf16[3,4,256,256]{3,2,1,0:T(8,128)(2,1)S(1)} %slice.28), channel_id=1, source_target_pairs={{0,8},{1,9},{2,10},{3,11},{4,12},{5,13},{6,14},{7,15},{8,16},{9,17... | collective-permute-start | bytes 4718600 | tf_op jit(solution)/shard_map/ppermute | solution.py:42
  18.9 18.0 %copy-start.17 = (s32[2]{0:T(128)}, s32[2]{0:T(128)S(1)}, u32[]{:S(2)}) copy-start(s32[2]{0:T(128)S(1)} %collective-permute-done.17.listed_ref) | copy-start | bytes 28
  18.9 11.8 %collective-permute-start = (s32[2]{0:T(128)S(1)}, s32[2]{0:T(128)S(1)}, u32[]{:S(2)}, u32[]{:S(2)}) collective-permute-start(s32[2]{0:T(128)S(1)} %copy-done.14), channel_id=1, source_target_pairs={{0,32},{32,64},{64,96},{1,33},{33,65},{65,97},{2,34},{34,66},{66,9... | collective-permute-start | bytes 32 | tf_op jit(solution)/shard_map/ppermute | solution.py:21
  20.2 16.7 %copy-start.18 = (s32[2]{0:T(128)}, s32[2]{0:T(128)S(1)}, u32[]{:S(2)}) copy-start(s32[2]{0:T(128)S(1)} %collective-permute-done.14) | copy-start | bytes 28
  20.2 29.2 %collective-permute-start.41 = (bf16[3,3,256,256]{3,2,1,0:T(8,128)(2,1)}, bf16[3,3,256,256]{3,2,1,0:T(8,128)(2,1)}, u32[]{:S(2)}, u32[]{:S(2)}) collective-permute-start(bf16[3,3,256,256]{3,2,1,0:T(8,128)(2,1)} %get-tuple-element.124), channel_id=1, source_target_pairs={{0,2},{1,3},{2,4},{3,5},{4,6},{5,7},{6,0},{7,1},{8,10},{9,11},{10,... | collective-permute-start | bytes 3538952 | tf_op jit(solution)/shard_map/ppermute | solution.py:42
  21.9 15.0 %copy-start.19 = (s32[2]{0:T(128)}, s32[2]{0:T(128)S(1)}, u32[]{:S(2)}) copy-start(s32[2]{0:T(128)S(1)} %collective-permute-done.1) | copy-start | bytes 28
  21.9 51.1 %collective-permute-start.15 = (bf16[3,3,256,256]{3,2,1,0:T(8,128)(2,1)}, bf16[3,3,256,256]{3,2,1,0:T(8,128)(2,1)}, u32[]{:S(2)}, u32[]{:S(2)}) collective-permute-start(bf16[3,3,256,256]{3,2,1,0:T(8,128)(2,1)} %get-tuple-element.125), channel_id=1, source_target_pairs={{0,2},{1,3},{2,4},{3,5},{4,6},{5,7},{6,0},{7,1},{8,10},{9,11},{10,... | collective-permute-start | bytes 3538952 | tf_op jit(solution)/shard_map/ppermute | solution.py:42
  30.7 6.3 copy-start.20
  30.7 63.2 %collective-permute-start.2 = (bf16[3,3,256,256]{3,2,1,0:T(8,128)(2,1)}, bf16[3,3,256,256]{3,2,1,0:T(8,128)(2,1)}, u32[]{:S(2)}, u32[]{:S(2)}) collective-permute-start(bf16[3,3,256,256]{3,2,1,0:T(8,128)(2,1)} %get-tuple-element.126), channel_id=1, source_target_pairs={{0,8},{1,9},{2,10},{3,11},{4,12},{5,13},{6,14},{7,15},{8,16},{9,17... | collective-permute-start | bytes 3538952 | tf_op jit(solution)/shard_map/ppermute | solution.py:42
  31.9 63.3 %collective-permute-start.4 = (bf16[2,3,256,256]{3,2,1,0:T(8,128)(2,1)}, bf16[2,3,256,256]{3,2,1,0:T(8,128)(2,1)}, u32[]{:S(2)}, u32[]{:S(2)}) collective-permute-start(bf16[2,3,256,256]{3,2,1,0:T(8,128)(2,1)} %collective-permute-done.3.near_ref), channel_id=1, source_target_pairs={{0,8},{1,9},{2,10},{3,11},{4,12},{5,13},{6,14},{7,15},{8,16},{9,17... | collective-permute-start | bytes 2359304 | tf_op jit(solution)/shard_map/ppermute | solution.py:42
  49.4 38.7 %collective-permute-start.30 = (s32[2]{0:T(128)}, s32[2]{0:T(128)S(1)}, u32[]{:S(2)}, u32[]{:S(2)}) collective-permute-start(s32[2]{0:T(128)} %listed_ref.7), channel_id=1, source_target_pairs={{0,8},{1,9},{2,10},{3,11},{4,12},{5,13},{6,14},{7,15},{8,16},{9,17... | collective-permute-start | bytes 32 | tf_op jit(solution)/shard_map/ppermute | solution.py:42
  73.0 117.4 %collective-permute-start.42 = (bf16[2,3,256,256]{3,2,1,0:T(8,128)(2,1)}, bf16[2,3,256,256]{3,2,1,0:T(8,128)(2,1)}, u32[]{:S(2)}, u32[]{:S(2)}) collective-permute-start(bf16[2,3,256,256]{3,2,1,0:T(8,128)(2,1)} %pick.12), channel_id=1, source_target_pairs={{0,32},{32,64},{64,96},{1,33},{33,65},{65,97},{2,34},{34,66},{66,9... | collective-permute-start | bytes 2359304 | tf_op jit(solution)/shard_map/ppermute | solution.py:21
  88.1 29.4 %collective-permute-start.16 = (bf16[2,3,256,256]{3,2,1,0:T(8,128)(2,1)}, bf16[2,3,256,256]{3,2,1,0:T(8,128)(2,1)}, u32[]{:S(2)}, u32[]{:S(2)}) collective-permute-start(bf16[2,3,256,256]{3,2,1,0:T(8,128)(2,1)} %pick.8), channel_id=1, source_target_pairs={{0,32},{32,64},{64,96},{1,33},{33,65},{65,97},{2,34},{34,66},{66,9... | collective-permute-start | bytes 2359304 | tf_op jit(solution)/shard_map/ppermute | solution.py:21
  89.4 133.7 %collective-permute-start.29 = (bf16[2,4,256,256]{3,2,1,0:T(8,128)(2,1)}, bf16[2,4,256,256]{3,2,1,0:T(8,128)(2,1)}, u32[]{:S(2)}, u32[]{:S(2)}) collective-permute-start(bf16[2,4,256,256]{3,2,1,0:T(8,128)(2,1)} %pick.10), channel_id=1, source_target_pairs={{0,32},{32,64},{64,96},{1,33},{33,65},{65,97},{2,34},{34,66},{66,9... | collective-permute-start | bytes 3145736 | tf_op jit(solution)/shard_map/ppermute | solution.py:21
  93.8 97.8 %collective-permute-start.43 = (bf16[2,3,256,256]{3,2,1,0:T(8,128)(2,1)}, bf16[2,3,256,256]{3,2,1,0:T(8,128)(2,1)}, u32[]{:S(2)}, u32[]{:S(2)}) collective-permute-start(bf16[2,3,256,256]{3,2,1,0:T(8,128)(2,1)} %pick.13), channel_id=1, source_target_pairs={{0,32},{32,64},{64,96},{1,33},{33,65},{65,97},{2,34},{34,66},{66,9... | collective-permute-start | bytes 2359304 | tf_op jit(solution)/shard_map/ppermute | solution.py:21
  95.2 74.1 %collective-permute-start.18 = (bf16[2,3,256,256]{3,2,1,0:T(8,128)(2,1)S(1)}, bf16[2,3,256,256]{3,2,1,0:T(8,128)(2,1)S(1)}, u32[]{:S(2)}, u32[]{:S(2)}) collective-permute-start(bf16[2,3,256,256]{3,2,1,0:T(8,128)(2,1)S(1)} %copy-done.9), channel_id=1, source_target_pairs={{0,32},{32,64},{64,96},{1,33},{33,65},{65,97},{2,34},{34,66},{66,9... | collective-permute-start | bytes 2359304 | tf_op jit(solution)/shard_map/ppermute | solution.py:21
  117.5 105.7 %collective-permute-start.5 = (bf16[16,3,128,128]{3,2,1,0:T(8,128)(2,1)}, bf16[16,3,128,128]{3,2,1,0:T(8,128)(2,1)S(1)}, u32[]{:S(2)}, u32[]{:S(2)}) collective-permute-start(bf16[16,3,128,128]{3,2,1,0:T(8,128)(2,1)} %get-tuple-element.50), channel_id=1, source_target_pairs={{0,8},{1,9},{2,10},{3,11},{4,12},{5,13},{6,14},{7,15},{8,16},{9,17... | collective-permute-start | bytes 4718600 | tf_op jit(solution)/shard_map/ppermute | solution.py:42
  170.2 65.6 %collective-permute-start.6 = (bf16[16,3,128,128]{3,2,1,0:T(8,128)(2,1)}, bf16[16,3,128,128]{3,2,1,0:T(8,128)(2,1)S(1)}, u32[]{:S(2)}, u32[]{:S(2)}) collective-permute-start(bf16[16,3,128,128]{3,2,1,0:T(8,128)(2,1)} %get-tuple-element.51), channel_id=1, source_target_pairs={{0,24},{1,25},{2,26},{3,27},{4,28},{5,29},{6,30},{7,31},{8,0},{9,1... | collective-permute-start | bytes 4718600 | tf_op jit(solution)/shard_map/ppermute | solution.py:42
  190.4 52.2 %collective-permute-start.31 = (bf16[2,4,256,256]{3,2,1,0:T(8,128)(2,1)}, bf16[2,4,256,256]{3,2,1,0:T(8,128)(2,1)}, u32[]{:S(2)}, u32[]{:S(2)}) collective-permute-start(bf16[2,4,256,256]{3,2,1,0:T(8,128)(2,1)} %pick.11), channel_id=1, source_target_pairs={{0,32},{32,64},{64,96},{1,33},{33,65},{65,97},{2,34},{34,66},{66,9... | collective-permute-start | bytes 3145736 | tf_op jit(solution)/shard_map/ppermute | solution.py:21
  191.7 51.0 %collective-permute-start.19 = (bf16[16,3,128,128]{3,2,1,0:T(8,128)(2,1)}, bf16[16,3,128,128]{3,2,1,0:T(8,128)(2,1)}, u32[]{:S(2)}, u32[]{:S(2)}) collective-permute-start(bf16[16,3,128,128]{3,2,1,0:T(8,128)(2,1)} %get-tuple-element.61), channel_id=1, source_target_pairs={{0,2},{1,3},{2,4},{3,5},{4,6},{5,7},{6,0},{7,1},{8,10},{9,11},{10,... | collective-permute-start | bytes 4718600 | tf_op jit(solution)/shard_map/ppermute | solution.py:42
  223.1 47.0 %collective-permute-start.20 = (bf16[16,3,128,128]{3,2,1,0:T(8,128)(2,1)}, bf16[16,3,128,128]{3,2,1,0:T(8,128)(2,1)}, u32[]{:S(2)}, u32[]{:S(2)}) collective-permute-start(bf16[16,3,128,128]{3,2,1,0:T(8,128)(2,1)} %get-tuple-element.62), channel_id=1, source_target_pairs={{0,6},{1,7},{2,0},{3,1},{4,2},{5,3},{6,4},{7,5},{8,14},{9,15},{10,... | collective-permute-start | bytes 4718600 | tf_op jit(solution)/shard_map/ppermute | solution.py:42
  224.4 46.6 %collective-permute-start.44 = (bf16[16,3,128,128]{3,2,1,0:T(8,128)(2,1)}, bf16[16,3,128,128]{3,2,1,0:T(8,128)(2,1)S(1)}, u32[]{:S(2)}, u32[]{:S(2)}) collective-permute-start(bf16[16,3,128,128]{3,2,1,0:T(8,128)(2,1)} %get-tuple-element.83), channel_id=1, source_target_pairs={{0,2},{1,3},{2,4},{3,5},{4,6},{5,7},{6,0},{7,1},{8,10},{9,11},{10,... | collective-permute-start | bytes 4718600 | tf_op jit(solution)/shard_map/ppermute | solution.py:42
  236.9 65.9 %collective-permute-start.45 = (bf16[16,3,128,128]{3,2,1,0:T(8,128)(2,1)}, bf16[16,3,128,128]{3,2,1,0:T(8,128)(2,1)S(1)}, u32[]{:S(2)}, u32[]{:S(2)}) collective-permute-start(bf16[16,3,128,128]{3,2,1,0:T(8,128)(2,1)} %get-tuple-element.84), channel_id=1, source_target_pairs={{0,6},{1,7},{2,0},{3,1},{4,2},{5,3},{6,4},{7,5},{8,14},{9,15},{10,... | collective-permute-start | bytes 4718600 | tf_op jit(solution)/shard_map/ppermute | solution.py:42
  242.6 60.2 %collective-permute-start.7 = (bf16[8,3,128,128]{3,2,1,0:T(8,128)(2,1)}, bf16[8,3,128,128]{3,2,1,0:T(8,128)(2,1)}, u32[]{:S(2)}, u32[]{:S(2)}) collective-permute-start(bf16[8,3,128,128]{3,2,1,0:T(8,128)(2,1)} %get-tuple-element.53), channel_id=1, source_target_pairs={{0,1},{1,0},{2,3},{3,2},{4,5},{5,4},{6,7},{7,6},{8,9},{9,8},{10,11... | collective-permute-start | bytes 2359304 | tf_op jit(solution)/shard_map/ppermute | solution.py:42
  242.7 60.2 %collective-permute-start.8 = (bf16[8,3,128,128]{3,2,1,0:T(8,128)(2,1)}, bf16[8,3,128,128]{3,2,1,0:T(8,128)(2,1)}, u32[]{:S(2)}, u32[]{:S(2)}) collective-permute-start(bf16[8,3,128,128]{3,2,1,0:T(8,128)(2,1)} %get-tuple-element.54), channel_id=1, source_target_pairs={{0,2},{1,3},{2,4},{3,5},{4,6},{5,7},{6,0},{7,1},{8,10},{9,11},{10,... | collective-permute-start | bytes 2359304 | tf_op jit(solution)/shard_map/ppermute | solution.py:42
  270.2 66.6 %collective-permute-start.9 = (bf16[8,3,128,128]{3,2,1,0:T(8,128)(2,1)}, bf16[8,3,128,128]{3,2,1,0:T(8,128)(2,1)}, u32[]{:S(2)}, u32[]{:S(2)}) collective-permute-start(bf16[8,3,128,128]{3,2,1,0:T(8,128)(2,1)} %get-tuple-element.55), channel_id=1, source_target_pairs={{0,3},{1,2},{2,5},{3,4},{4,7},{5,6},{6,1},{7,0},{8,11},{9,10},{10,... | collective-permute-start | bytes 2359304 | tf_op jit(solution)/shard_map/ppermute | solution.py:42
  271.0 60.8 %copy-start.2 = (bf16[16,3,128,128]{3,2,1,0:T(8,128)(2,1)}, bf16[16,3,128,128]{3,2,1,0:T(8,128)(2,1)S(1)}, u32[]{:S(2)}) copy-start(bf16[16,3,128,128]{3,2,1,0:T(8,128)(2,1)S(1)} %collective-permute-done.44.up_ref) | copy-start | bytes 4718596
  271.0 65.8 %collective-permute-start.10 = (bf16[8,3,128,128]{3,2,1,0:T(8,128)(2,1)}, bf16[8,3,128,128]{3,2,1,0:T(8,128)(2,1)}, u32[]{:S(2)}, u32[]{:S(2)}) collective-permute-start(bf16[8,3,128,128]{3,2,1,0:T(8,128)(2,1)} %get-tuple-element.56), channel_id=1, source_target_pairs={{0,4},{1,5},{2,6},{3,7},{4,0},{5,1},{6,2},{7,3},{8,12},{9,13},{10,... | collective-permute-start | bytes 2359304 | tf_op jit(solution)/shard_map/ppermute | solution.py:42
  302.9 28.9 %copy-start.3 = (bf16[16,3,128,128]{3,2,1,0:T(8,128)(2,1)}, bf16[16,3,128,128]{3,2,1,0:T(8,128)(2,1)S(1)}, u32[]{:S(2)}) copy-start(bf16[16,3,128,128]{3,2,1,0:T(8,128)(2,1)S(1)} %collective-permute-done.45.down_ref) | copy-start | bytes 4718596
  302.9 41.6 %collective-permute-start.11 = (bf16[8,3,128,128]{3,2,1,0:T(8,128)(2,1)}, bf16[8,3,128,128]{3,2,1,0:T(8,128)(2,1)}, u32[]{:S(2)}, u32[]{:S(2)}) collective-permute-start(bf16[8,3,128,128]{3,2,1,0:T(8,128)(2,1)} %get-tuple-element.57), channel_id=1, source_target_pairs={{0,5},{1,4},{2,7},{3,6},{4,1},{5,0},{6,3},{7,2},{8,13},{9,12},{10,... | collective-permute-start | bytes 2359304 | tf_op jit(solution)/shard_map/ppermute | solution.py:42
  302.9 49.8 %collective-permute-start.12 = (bf16[8,3,128,128]{3,2,1,0:T(8,128)(2,1)}, bf16[8,3,128,128]{3,2,1,0:T(8,128)(2,1)}, u32[]{:S(2)}, u32[]{:S(2)}) collective-permute-start(bf16[8,3,128,128]{3,2,1,0:T(8,128)(2,1)} %get-tuple-element.58), channel_id=1, source_target_pairs={{0,6},{1,7},{2,0},{3,1},{4,2},{5,3},{6,4},{7,5},{8,14},{9,15},{10,... | collective-permute-start | bytes 2359304 | tf_op jit(solution)/shard_map/ppermute | solution.py:42
  303.0 66.6 %collective-permute-start.13 = (bf16[8,3,128,128]{3,2,1,0:T(8,128)(2,1)}, bf16[8,3,128,128]{3,2,1,0:T(8,128)(2,1)}, u32[]{:S(2)}, u32[]{:S(2)}) collective-permute-start(bf16[8,3,128,128]{3,2,1,0:T(8,128)(2,1)} %get-tuple-element.59), channel_id=1, source_target_pairs={{0,7},{1,6},{2,1},{3,0},{4,3},{5,2},{6,5},{7,4},{8,15},{9,14},{10,... | collective-permute-start | bytes 2359304 | tf_op jit(solution)/shard_map/ppermute | solution.py:42
  336.7 131.5 %collective-permute-start.32 = (bf16[16,4,128,128]{3,2,1,0:T(8,128)(2,1)}, bf16[16,4,128,128]{3,2,1,0:T(8,128)(2,1)S(1)}, u32[]{:S(2)}, u32[]{:S(2)}) collective-permute-start(bf16[16,4,128,128]{3,2,1,0:T(8,128)(2,1)} %get-tuple-element.72), channel_id=1, source_target_pairs={{0,8},{1,9},{2,10},{3,11},{4,12},{5,13},{6,14},{7,15},{8,16},{9,17... | collective-permute-start | bytes 6291464 | tf_op jit(solution)/shard_map/ppermute | solution.py:42
  336.7 132.6 %collective-permute-start.33 = (bf16[16,4,128,128]{3,2,1,0:T(8,128)(2,1)}, bf16[16,4,128,128]{3,2,1,0:T(8,128)(2,1)}, u32[]{:S(2)}, u32[]{:S(2)}) collective-permute-start(bf16[16,4,128,128]{3,2,1,0:T(8,128)(2,1)} %get-tuple-element.73), channel_id=1, source_target_pairs={{0,24},{1,25},{2,26},{3,27},{4,28},{5,29},{6,30},{7,31},{8,0},{9,1... | collective-permute-start | bytes 6291464 | tf_op jit(solution)/shard_map/ppermute | solution.py:42
  344.5 25.1 %collective-permute-start.21 = (bf16[8,3,128,128]{3,2,1,0:T(8,128)(2,1)}, bf16[8,3,128,128]{3,2,1,0:T(8,128)(2,1)}, u32[]{:S(2)}, u32[]{:S(2)}) collective-permute-start(bf16[8,3,128,128]{3,2,1,0:T(8,128)(2,1)} %get-tuple-element.64), channel_id=1, source_target_pairs={{0,1},{1,0},{2,3},{3,2},{4,5},{5,4},{6,7},{7,6},{8,9},{9,8},{10,11... | collective-permute-start | bytes 2359304 | tf_op jit(solution)/shard_map/ppermute | solution.py:42
  352.7 49.8 %collective-permute-start.22 = (bf16[8,3,128,128]{3,2,1,0:T(8,128)(2,1)}, bf16[8,3,128,128]{3,2,1,0:T(8,128)(2,1)}, u32[]{:S(2)}, u32[]{:S(2)}) collective-permute-start(bf16[8,3,128,128]{3,2,1,0:T(8,128)(2,1)} %get-tuple-element.65), channel_id=1, source_target_pairs={{0,8},{1,9},{2,10},{3,11},{4,12},{5,13},{6,14},{7,15},{8,16},{9,17... | collective-permute-start | bytes 2359304 | tf_op jit(solution)/shard_map/ppermute | solution.py:42
  369.5 78.4 %collective-permute-start.23 = (bf16[8,3,128,128]{3,2,1,0:T(8,128)(2,1)}, bf16[8,3,128,128]{3,2,1,0:T(8,128)(2,1)}, u32[]{:S(2)}, u32[]{:S(2)}) collective-permute-start(bf16[8,3,128,128]{3,2,1,0:T(8,128)(2,1)} %get-tuple-element.66), channel_id=1, source_target_pairs={{0,9},{1,8},{2,11},{3,10},{4,13},{5,12},{6,15},{7,14},{8,17},{9,16... | collective-permute-start | bytes 2359304 | tf_op jit(solution)/shard_map/ppermute | solution.py:42
  369.5 86.1 %collective-permute-start.24 = (bf16[8,3,128,128]{3,2,1,0:T(8,128)(2,1)}, bf16[8,3,128,128]{3,2,1,0:T(8,128)(2,1)S(1)}, u32[]{:S(2)}, u32[]{:S(2)}) collective-permute-start(bf16[8,3,128,128]{3,2,1,0:T(8,128)(2,1)} %get-tuple-element.67), channel_id=1, source_target_pairs={{0,16},{1,17},{2,18},{3,19},{4,20},{5,21},{6,22},{7,23},{8,24},{9,... | collective-permute-start | bytes 2359304 | tf_op jit(solution)/shard_map/ppermute | solution.py:42
  402.4 53.4 %collective-permute-start.25 = (bf16[8,3,128,128]{3,2,1,0:T(8,128)(2,1)}, bf16[8,3,128,128]{3,2,1,0:T(8,128)(2,1)}, u32[]{:S(2)}, u32[]{:S(2)}) collective-permute-start(bf16[8,3,128,128]{3,2,1,0:T(8,128)(2,1)} %get-tuple-element.68), channel_id=1, source_target_pairs={{0,17},{1,16},{2,19},{3,18},{4,21},{5,20},{6,23},{7,22},{8,25},{9,... | collective-permute-start | bytes 2359304 | tf_op jit(solution)/shard_map/ppermute | solution.py:42
  448.0 20.3 %collective-permute-start.26 = (bf16[8,3,128,128]{3,2,1,0:T(8,128)(2,1)}, bf16[8,3,128,128]{3,2,1,0:T(8,128)(2,1)}, u32[]{:S(2)}, u32[]{:S(2)}) collective-permute-start(bf16[8,3,128,128]{3,2,1,0:T(8,128)(2,1)} %get-tuple-element.69), channel_id=1, source_target_pairs={{0,24},{1,25},{2,26},{3,27},{4,28},{5,29},{6,30},{7,31},{8,0},{9,1... | collective-permute-start | bytes 2359304 | tf_op jit(solution)/shard_map/ppermute | solution.py:42
  455.7 84.4 %copy-start.10 = (bf16[8,3,128,128]{3,2,1,0:T(8,128)(2,1)}, bf16[8,3,128,128]{3,2,1,0:T(8,128)(2,1)S(1)}, u32[]{:S(2)}) copy-start(bf16[8,3,128,128]{3,2,1,0:T(8,128)(2,1)S(1)} %collective-permute-done.24.refs_12_) | copy-start | bytes 2359300
  455.7 31.2 %collective-permute-start.27 = (bf16[8,3,128,128]{3,2,1,0:T(8,128)(2,1)}, bf16[8,3,128,128]{3,2,1,0:T(8,128)(2,1)}, u32[]{:S(2)}, u32[]{:S(2)}) collective-permute-start(bf16[8,3,128,128]{3,2,1,0:T(8,128)(2,1)} %get-tuple-element.70), channel_id=1, source_target_pairs={{0,25},{1,24},{2,27},{3,26},{4,29},{5,28},{6,31},{7,30},{8,1},{9,0... | collective-permute-start | bytes 2359304 | tf_op jit(solution)/shard_map/ppermute | solution.py:42
  455.8 31.1 %collective-permute-start.46 = (bf16[8,3,128,128]{3,2,1,0:T(8,128)(2,1)}, bf16[8,3,128,128]{3,2,1,0:T(8,128)(2,1)}, u32[]{:S(2)}, u32[]{:S(2)}) collective-permute-start(bf16[8,3,128,128]{3,2,1,0:T(8,128)(2,1)} %get-tuple-element.86), channel_id=1, source_target_pairs={{0,1},{1,0},{2,3},{3,2},{4,5},{5,4},{6,7},{7,6},{8,9},{9,8},{10,11... | collective-permute-start | bytes 2359304 | tf_op jit(solution)/shard_map/ppermute | solution.py:42
  468.3 23.2 %collective-permute-start.47 = (bf16[8,3,128,128]{3,2,1,0:T(8,128)(2,1)}, bf16[8,3,128,128]{3,2,1,0:T(8,128)(2,1)}, u32[]{:S(2)}, u32[]{:S(2)}) collective-permute-start(bf16[8,3,128,128]{3,2,1,0:T(8,128)(2,1)} %get-tuple-element.87), channel_id=1, source_target_pairs={{0,8},{1,9},{2,10},{3,11},{4,12},{5,13},{6,14},{7,15},{8,16},{9,17... | collective-permute-start | bytes 2359304 | tf_op jit(solution)/shard_map/ppermute | solution.py:42
  468.3 71.7 %collective-permute-start.48 = (bf16[8,3,128,128]{3,2,1,0:T(8,128)(2,1)}, bf16[8,3,128,128]{3,2,1,0:T(8,128)(2,1)}, u32[]{:S(2)}, u32[]{:S(2)}) collective-permute-start(bf16[8,3,128,128]{3,2,1,0:T(8,128)(2,1)} %get-tuple-element.88), channel_id=1, source_target_pairs={{0,9},{1,8},{2,11},{3,10},{4,13},{5,12},{6,15},{7,14},{8,17},{9,16... | collective-permute-start | bytes 2359304 | tf_op jit(solution)/shard_map/ppermute | solution.py:42
  469.4 70.6 %collective-permute-start.49 = (bf16[8,3,128,128]{3,2,1,0:T(8,128)(2,1)}, bf16[8,3,128,128]{3,2,1,0:T(8,128)(2,1)}, u32[]{:S(2)}, u32[]{:S(2)}) collective-permute-start(bf16[8,3,128,128]{3,2,1,0:T(8,128)(2,1)} %get-tuple-element.89), channel_id=1, source_target_pairs={{0,16},{1,17},{2,18},{3,19},{4,20},{5,21},{6,22},{7,23},{8,24},{9,... | collective-permute-start | bytes 2359304 | tf_op jit(solution)/shard_map/ppermute | solution.py:42
  486.9 73.3 %collective-permute-start.34 = (bf16[8,4,128,128]{3,2,1,0:T(8,128)(2,1)}, bf16[8,4,128,128]{3,2,1,0:T(8,128)(2,1)S(1)}, u32[]{:S(2)}, u32[]{:S(2)}) collective-permute-start(bf16[8,4,128,128]{3,2,1,0:T(8,128)(2,1)} %get-tuple-element.75), channel_id=1, source_target_pairs={{0,1},{1,0},{2,3},{3,2},{4,5},{5,4},{6,7},{7,6},{8,9},{9,8},{10,11... | collective-permute-start | bytes 3145736 | tf_op jit(solution)/shard_map/ppermute | solution.py:42
  486.9 75.5 %collective-permute-start.35 = (bf16[8,4,128,128]{3,2,1,0:T(8,128)(2,1)}, bf16[8,4,128,128]{3,2,1,0:T(8,128)(2,1)S(1)}, u32[]{:S(2)}, u32[]{:S(2)}) collective-permute-start(bf16[8,4,128,128]{3,2,1,0:T(8,128)(2,1)} %get-tuple-element.76), channel_id=1, source_target_pairs={{0,2},{1,3},{2,4},{3,5},{4,6},{5,7},{6,0},{7,1},{8,10},{9,11},{10,... | collective-permute-start | bytes 3145736 | tf_op jit(solution)/shard_map/ppermute | solution.py:42
  491.5 48.5 %collective-permute-start.50 = (bf16[8,3,128,128]{3,2,1,0:T(8,128)(2,1)}, bf16[8,3,128,128]{3,2,1,0:T(8,128)(2,1)S(1)}, u32[]{:S(2)}, u32[]{:S(2)}) collective-permute-start(bf16[8,3,128,128]{3,2,1,0:T(8,128)(2,1)} %get-tuple-element.90), channel_id=1, source_target_pairs={{0,17},{1,16},{2,19},{3,18},{4,21},{5,20},{6,23},{7,22},{8,25},{9,... | collective-permute-start | bytes 2359304 | tf_op jit(solution)/shard_map/ppermute | solution.py:42
  540.0 20.1 %collective-permute-start.51 = (bf16[8,3,128,128]{3,2,1,0:T(8,128)(2,1)}, bf16[8,3,128,128]{3,2,1,0:T(8,128)(2,1)S(1)}, u32[]{:S(2)}, u32[]{:S(2)}) collective-permute-start(bf16[8,3,128,128]{3,2,1,0:T(8,128)(2,1)} %get-tuple-element.91), channel_id=1, source_target_pairs={{0,24},{1,25},{2,26},{3,27},{4,28},{5,29},{6,30},{7,31},{8,0},{9,1... | collective-permute-start | bytes 2359304 | tf_op jit(solution)/shard_map/ppermute | solution.py:42
  540.0 20.1 %collective-permute-start.52 = (bf16[8,3,128,128]{3,2,1,0:T(8,128)(2,1)}, bf16[8,3,128,128]{3,2,1,0:T(8,128)(2,1)S(1)}, u32[]{:S(2)}, u32[]{:S(2)}) collective-permute-start(bf16[8,3,128,128]{3,2,1,0:T(8,128)(2,1)} %get-tuple-element.92), channel_id=1, source_target_pairs={{0,25},{1,24},{2,27},{3,26},{4,29},{5,28},{6,31},{7,30},{8,1},{9,0... | collective-permute-start | bytes 2359304 | tf_op jit(solution)/shard_map/ppermute | solution.py:42
  540.0 22.4 %copy-start.11 = (bf16[8,3,128,128]{3,2,1,0:T(8,128)(2,1)}, bf16[8,3,128,128]{3,2,1,0:T(8,128)(2,1)S(1)}, u32[]{:S(2)}) copy-start(bf16[8,3,128,128]{3,2,1,0:T(8,128)(2,1)S(1)} %collective-permute-done.50.refs_29_) | copy-start | bytes 2359300
  540.1 26.2 %collective-permute-start.36 = (bf16[8,4,128,128]{3,2,1,0:T(8,128)(2,1)}, bf16[8,4,128,128]{3,2,1,0:T(8,128)(2,1)S(1)}, u32[]{:S(2)}, u32[]{:S(2)}) collective-permute-start(bf16[8,4,128,128]{3,2,1,0:T(8,128)(2,1)} %get-tuple-element.77), channel_id=1, source_target_pairs={{0,3},{1,2},{2,5},{3,4},{4,7},{5,6},{6,1},{7,0},{8,11},{9,10},{10,... | collective-permute-start | bytes 3145736 | tf_op jit(solution)/shard_map/ppermute | solution.py:42
  560.1 27.9 %collective-permute-start.37 = (bf16[8,4,128,128]{3,2,1,0:T(8,128)(2,1)}, bf16[8,4,128,128]{3,2,1,0:T(8,128)(2,1)}, u32[]{:S(2)}, u32[]{:S(2)}) collective-permute-start(bf16[8,4,128,128]{3,2,1,0:T(8,128)(2,1)} %get-tuple-element.78), channel_id=1, source_target_pairs={{0,4},{1,5},{2,6},{3,7},{4,0},{5,1},{6,2},{7,3},{8,12},{9,13},{10,... | collective-permute-start | bytes 3145736 | tf_op jit(solution)/shard_map/ppermute | solution.py:42
  560.1 38.5 %collective-permute-start.38 = (bf16[8,4,128,128]{3,2,1,0:T(8,128)(2,1)}, bf16[8,4,128,128]{3,2,1,0:T(8,128)(2,1)}, u32[]{:S(2)}, u32[]{:S(2)}) collective-permute-start(bf16[8,4,128,128]{3,2,1,0:T(8,128)(2,1)} %get-tuple-element.79), channel_id=1, source_target_pairs={{0,5},{1,4},{2,7},{3,6},{4,1},{5,0},{6,3},{7,2},{8,13},{9,12},{10,... | collective-permute-start | bytes 3145736 | tf_op jit(solution)/shard_map/ppermute | solution.py:42
  560.2 82.6 %copy-start.6 = (bf16[8,4,128,128]{3,2,1,0:T(8,128)(2,1)}, bf16[8,4,128,128]{3,2,1,0:T(8,128)(2,1)S(1)}, u32[]{:S(2)}) copy-start(bf16[8,4,128,128]{3,2,1,0:T(8,128)(2,1)S(1)} %collective-permute-done.34.refs_17_) | copy-start | bytes 3145732
  560.2 60.8 %collective-permute-start.39 = (bf16[8,4,128,128]{3,2,1,0:T(8,128)(2,1)}, bf16[8,4,128,128]{3,2,1,0:T(8,128)(2,1)}, u32[]{:S(2)}, u32[]{:S(2)}) collective-permute-start(bf16[8,4,128,128]{3,2,1,0:T(8,128)(2,1)} %get-tuple-element.80), channel_id=1, source_target_pairs={{0,6},{1,7},{2,0},{3,1},{4,2},{5,3},{6,4},{7,5},{8,14},{9,15},{10,... | collective-permute-start | bytes 3145736 | tf_op jit(solution)/shard_map/ppermute | solution.py:42
  562.4 80.4 %copy-start.7 = (bf16[8,4,128,128]{3,2,1,0:T(8,128)(2,1)}, bf16[8,4,128,128]{3,2,1,0:T(8,128)(2,1)S(1)}, u32[]{:S(2)}) copy-start(bf16[8,4,128,128]{3,2,1,0:T(8,128)(2,1)S(1)} %collective-permute-done.35.refs_18_) | copy-start | bytes 3145732
  562.5 80.3 %collective-permute-start.40 = (bf16[8,4,128,128]{3,2,1,0:T(8,128)(2,1)}, bf16[8,4,128,128]{3,2,1,0:T(8,128)(2,1)}, u32[]{:S(2)}, u32[]{:S(2)}) collective-permute-start(bf16[8,4,128,128]{3,2,1,0:T(8,128)(2,1)} %get-tuple-element.81), channel_id=1, source_target_pairs={{0,7},{1,6},{2,1},{3,0},{4,3},{5,2},{6,5},{7,4},{8,15},{9,14},{10,... | collective-permute-start | bytes 3145736 | tf_op jit(solution)/shard_map/ppermute | solution.py:42
  566.2 76.6 %copy-start.8 = (bf16[8,4,128,128]{3,2,1,0:T(8,128)(2,1)}, bf16[8,4,128,128]{3,2,1,0:T(8,128)(2,1)S(1)}, u32[]{:S(2)}) copy-start(bf16[8,4,128,128]{3,2,1,0:T(8,128)(2,1)S(1)} %collective-permute-done.36.refs_19_) | copy-start | bytes 3145732
  (13 other events, 42.7 us)

commit v6 on v5

--- a/solution.py
+++ b/solution.py
@@ -8,7 +8,8 @@
 from jax.sharding import PartitionSpec as P
 
 
-CHUNKS = (("x", 3), ("z", 3), ("x", 4), ("z", 3))
+EARLY = 3
+CHUNKS = (("x", 5), ("z", 5))
 RING = 4
 LANES = 2 * RING
 ABREAST = 4
@@ -73,18 +74,140 @@
     )(listed, tiles)
 
 
+def render_early_kernel(
+    local_count, first, bands, seams, range_ref, blocks_ref, slots_ref, source_ref, offsets_ref, taps_ref, blend_ref,
+    listed_ref, tiles_ref, *refs,
+):
+    if seams:
+        near_ref, _, out_ref, held, beside, row_lag, col_lag, done, in_sem, out_sem = refs
+        load_near = pltpu.make_async_copy(near_ref, beside, in_sem.at[1])
+        load_near.start()
+        start, stop = range_ref[0], range_ref[1]
+    else:
+        out_ref, held, row_lag, col_lag, done, in_sem, out_sem = refs
+        start, stop = 0, range_ref[0]
+    load = pltpu.make_async_copy(tiles_ref.at[:, pl.ds(first, bands)], held, in_sem.at[0])
+    load.start()
+    height, width = held.shape[2], held.shape[3]
+    row_lag[...] = lax.broadcasted_iota(jnp.int32, row_lag.shape, 1) - 2 * lax.broadcasted_iota(jnp.int32, row_lag.shape, 0)
+    col_lag[...] = lax.broadcasted_iota(jnp.int32, col_lag.shape, 0) - 2 * lax.broadcasted_iota(jnp.int32, col_lag.shape, 1)
+    load.wait()
+    if seams:
+        load_near.wait()
+
+    def store(index):
+        way = lax.rem(index - start, 2 * ABREAST)
+        return pltpu.make_async_copy(done.at[way], out_ref.at[slots_ref[index]], out_sem.at[way])
+
+    def kernel_matrix(lag_ref, block, axis):
+        lag = lag_ref[...] - offsets_ref[2 * block + axis]
+        kernel = jnp.zeros(lag.shape, jnp.float32)
+        for place, step in enumerate(STEPS):
+            kernel = jnp.where(lag == step, taps_ref[(len(STEPS) * axis + place) * source_ref.shape[0] + block], kernel)
+        return kernel.astype(jnp.bfloat16)
+
+    def render_one(index):
+        block = blocks_ref[index]
+        tile = lax.rem(source_ref[block], local_count)
+        row_kernel = kernel_matrix(row_lag, block, 0)
+        col_kernel = kernel_matrix(col_lag, block, 1)
+        if seams:
+            place = jnp.where(listed_ref[1] == tile, 1, 0)
+            weight = blend_ref[block]
+            mixed = (1.0 - weight) * held[tile].astype(jnp.float32) + weight * beside[place].astype(jnp.float32)
+            mixed = mixed.astype(jnp.bfloat16)
+        else:
+            mixed = held[tile]
+        mixed = mixed.reshape(bands * height, width)
+        across = jnp.dot(mixed, col_kernel, preferred_element_type=jnp.float32).astype(jnp.bfloat16)
+        beside_each = jnp.concatenate([across[b * height : (b + 1) * height] for b in range(bands)], axis=1)
+        return jnp.dot(row_kernel, beside_each, preferred_element_type=jnp.float32).astype(jnp.bfloat16)
+
+    def some(turn, carry):
+        begin = start + turn * ABREAST
+        for ahead in range(ABREAST):
+
+            @pl.when(turn >= 2)
+            def _():
+                store(begin + ahead - 2 * ABREAST).wait()
+
+        results = [render_one(jnp.minimum(begin + ahead, stop - 1)) for ahead in range(ABREAST)]
+        for ahead in range(ABREAST):
+            way = lax.rem(turn, 2) * ABREAST + ahead
+            for b in range(bands):
+                done[way, b] = results[ahead][:, b * (width // 2) : (b + 1) * (width // 2)]
+        for ahead in range(ABREAST):
+
+            @pl.when(begin + ahead < stop)
+            def _():
+                store(begin + ahead).start()
+
+        return carry
+
+    turns = lax.div(stop - start + ABREAST - 1, ABREAST)
+    lax.fori_loop(0, turns, some, 0)
+
+    def drain(index, carry):
+        store(index).wait()
+        return carry
+
+    lax.fori_loop(start + jnp.maximum(turns - 2, 0) * ABREAST, stop, drain, 0)
+
+
+def render_early(scalars, tiles, first, bands, slots, near=None, begun=None):
+    local_count, _, height, width = tiles.shape
+    block = (bands, height // 2, width // 2)
+    seams = near is not None
+    arrays = (tiles, near, begun) if seams else (tiles,)
+    flops = 12 * bands * (2 * height * width * width // 2 + height * width * height // 2)
+    return pl.pallas_call(
+        functools.partial(render_early_kernel, local_count, first, bands, seams),
+        out_shape=jax.ShapeDtypeStruct((slots,) + block, jnp.bfloat16),
+        in_specs=[pl.BlockSpec(memory_space=pltpu.SMEM)] * len(scalars)
+        + [pl.BlockSpec(memory_space=pl.ANY)] * len(arrays),
+        out_specs=pl.BlockSpec(memory_space=pl.ANY),
+        scratch_shapes=[pltpu.VMEM((local_count, bands, height, width), jnp.bfloat16)]
+        + ([pltpu.VMEM(near.shape, jnp.bfloat16)] if seams else [])
+        + [
+            pltpu.VMEM((height // 2, height), jnp.int32),
+            pltpu.VMEM((width, width // 2), jnp.int32),
+            pltpu.VMEM((2 * ABREAST,) + block, jnp.bfloat16),
+            pltpu.SemaphoreType.DMA((2,)),
+            pltpu.SemaphoreType.DMA((2 * ABREAST,)),
+        ],
+        input_output_aliases={len(scalars) + 2: 0} if seams else {},
+        cost_estimate=pl.CostEstimate(flops=8 * flops, bytes_accessed=12 * bands * height * width // 2, transcendentals=0),
+        name="early_seams" if seams else "early",
+    )(*scalars, *arrays)
+
+
+def swap(outgoing, capacity):
+    slots = outgoing.shape[0]
+    pairs = outgoing.reshape((slots // capacity, capacity) + outgoing.shape[1:])
+    return lax.all_to_all(pairs, "tile", split_axis=0, concat_axis=0, tiled=True).reshape(outgoing.shape)
+
+
 def render_kernel(
-    local_count, first, bands, count_ref, blocks_ref, into_ref, side_ref, source_ref, offsets_ref, taps_ref, blend_ref,
-    listed_ref, tiles_ref, beyond_ref, near_ref, near_beyond_ref, stay_ref, up_ref, down_ref,
-    held, beside, row_lag, col_lag, done, in_sem, out_sem,
+    local_count, first, bands, seams, range_ref, blocks_ref, into_ref, side_ref, source_ref, offsets_ref, taps_ref,
+    blend_ref, listed_ref, tiles_ref, beyond_ref, *refs,
 ):
-    seams = near_ref.shape[0]
-    loads = (
+    if seams:
+        near_ref, near_beyond_ref, _, _, _, stay_ref, up_ref, down_ref, held, beside = refs[:10]
+        start, stop = range_ref[0], range_ref[1]
+    else:
+        stay_ref, up_ref, down_ref, held = refs[:4]
+        start, stop = 0, range_ref[0]
+    row_lag, col_lag, done, in_sem, out_sem = refs[-5:]
+    loads = [
         pltpu.make_async_copy(tiles_ref.at[:, pl.ds(first, bands)], held.at[pl.ds(0, local_count)], in_sem.at[0]),
         pltpu.make_async_copy(beyond_ref, held.at[pl.ds(local_count, local_count)], in_sem.at[1]),
-        pltpu.make_async_copy(near_ref, beside.at[pl.ds(0, seams)], in_sem.at[2]),
-        pltpu.make_async_copy(near_beyond_ref, beside.at[pl.ds(seams, seams)], in_sem.at[3]),
-    )
+    ]
+    if seams:
+        listed = near_ref.shape[0]
+        loads += [
+            pltpu.make_async_copy(near_ref, beside.at[pl.ds(0, listed)], in_sem.at[2]),
+            pltpu.make_async_copy(near_beyond_ref, beside.at[pl.ds(listed, listed)], in_sem.at[3]),
+        ]
     for load in loads:
         load.start()
     height, width = held.shape[2], held.shape[3]
@@ -92,7 +215,6 @@
     col_lag[...] = lax.broadcasted_iota(jnp.int32, col_lag.shape, 0) - 2 * lax.broadcasted_iota(jnp.int32, col_lag.shape, 1)
     for load in loads:
         load.wait()
-    count = count_ref[0]
 
     def start_store(index, way):
         into = into_ref[index]
@@ -117,21 +239,20 @@
         block = blocks_ref[index]
         side = side_ref[index]
         tile = lax.rem(source_ref[block], local_count)
-        second = listed_ref[seams * side + 1] == tile
-        flagged = (second | (listed_ref[seams * side] == tile)) & (listed_ref[2 * seams] > 0)
-        place = seams * side + jnp.where(second, 1, 0)
-        weight = jnp.where(flagged, blend_ref[block], 0.0)
         row_kernel = kernel_matrix(row_lag, block, 0)
         col_kernel = kernel_matrix(col_lag, block, 1)
-        primary = held[local_count * side + tile].astype(jnp.float32)
-        mixed = (1.0 - weight) * primary + weight * beside[place].astype(jnp.float32)
+        mixed = held[local_count * side + tile]
+        if seams:
+            place = listed * side + jnp.where(listed_ref[listed * side + 1] == tile, 1, 0)
+            weight = blend_ref[block]
+            mixed = (1.0 - weight) * mixed.astype(jnp.float32) + weight * beside[place].astype(jnp.float32)
         mixed = mixed.astype(jnp.bfloat16).reshape(bands * height, width)
         across = jnp.dot(mixed, col_kernel, preferred_element_type=jnp.float32).astype(jnp.bfloat16)
         beside_each = jnp.concatenate([across[b * height : (b + 1) * height] for b in range(bands)], axis=1)
         return jnp.dot(row_kernel, beside_each, preferred_element_type=jnp.float32).astype(jnp.bfloat16)
 
     def some(turn, carry):
-        begin = turn * ABREAST
+        begin = start + turn * ABREAST
         half = lax.rem(turn, 2) * ABREAST
         for ahead in range(ABREAST):
 
@@ -139,50 +260,54 @@
             def _():
                 wait_store(half + ahead)
 
-        results = [render_one(jnp.minimum(begin + ahead, count - 1)) for ahead in range(ABREAST)]
+        results = [render_one(jnp.minimum(begin + ahead, stop - 1)) for ahead in range(ABREAST)]
         for ahead in range(ABREAST):
             for b in range(bands):
                 done[half + ahead, b] = results[ahead][:, b * (width // 2) : (b + 1) * (width // 2)]
         for ahead in range(ABREAST):
 
-            @pl.when(begin + ahead < count)
+            @pl.when(begin + ahead < stop)
             def _():
                 start_store(begin + ahead, half + ahead)
 
         return carry
 
-    turns = lax.div(count + ABREAST - 1, ABREAST)
+    turns = lax.div(stop - start + ABREAST - 1, ABREAST)
     lax.fori_loop(0, turns, some, 0)
 
     def drain(index, carry):
         wait_store(lax.rem(index, 2 * ABREAST))
         return carry
 
-    lax.fori_loop(jnp.maximum(turns - 2, 0) * ABREAST, count, drain, 0)
-
-
-def render(scalars, tiles, beyond, near, near_beyond, first):
+    lax.fori_loop(jnp.maximum(turns - 2, 0) * ABREAST, stop - start, drain, 0)
+
+
+def render(scalars, tiles, beyond, first, near=None, near_beyond=None, begun=()):
     local_count, _, height, width = tiles.shape
     bands = beyond.shape[1]
     block = (bands, height // 2, width // 2)
-    flops = 24 * bands * (2 * height * width * width // 2 + height * width * height // 2)
+    seams = near is not None
+    arrays = (tiles, beyond) + ((near, near_beyond) if seams else ()) + tuple(begun)
+    flops = 12 * bands * (2 * height * width * width // 2 + height * width * height // 2)
     return pl.pallas_call(
-        functools.partial(render_kernel, local_count, first, bands),
+        functools.partial(render_kernel, local_count, first, bands, seams),
         out_shape=[jax.ShapeDtypeStruct((slots,) + block, jnp.bfloat16) for slots in (4 * LANES, 2 * LANES, 2 * LANES)],
-        in_specs=[pl.BlockSpec(memory_space=pltpu.SMEM)] * len(scalars) + [pl.BlockSpec(memory_space=pl.ANY)] * 4,
+        in_specs=[pl.BlockSpec(memory_space=pltpu.SMEM)] * len(scalars)
+        + [pl.BlockSpec(memory_space=pl.ANY)] * len(arrays),
         out_specs=[pl.BlockSpec(memory_space=pl.ANY)] * 3,
-        scratch_shapes=[
-            pltpu.VMEM((2 * local_count, bands, height, width), jnp.bfloat16),
-            pltpu.VMEM((2 * near.shape[0], bands, height, width), jnp.bfloat16),
+        scratch_shapes=[pltpu.VMEM((2 * local_count, bands, height, width), jnp.bfloat16)]
+        + ([pltpu.VMEM((2 * near.shape[0], bands, height, width), jnp.bfloat16)] if seams else [])
+        + [
             pltpu.VMEM((height // 2, height), jnp.int32),
             pltpu.VMEM((width, width // 2), jnp.int32),
             pltpu.VMEM((2 * ABREAST,) + block, jnp.bfloat16),
             pltpu.SemaphoreType.DMA((4,)),
             pltpu.SemaphoreType.DMA((2 * ABREAST,)),
         ],
-        cost_estimate=pl.CostEstimate(flops=8 * flops, bytes_accessed=24 * bands * height * width // 2, transcendentals=0),
-        name="render",
-    )(*scalars, tiles, beyond, near, near_beyond)
+        input_output_aliases={len(scalars) + 4 + number: number for number in range(3)} if seams else {},
+        cost_estimate=pl.CostEstimate(flops=8 * flops, bytes_accessed=12 * bands * height * width // 2, transcendentals=0),
+        name="late_seams" if seams else "late",
+    )(*scalars, *arrays)
 
 
 def pack_kernel(stay_ref, up_ref, down_ref, *refs):
@@ -221,11 +346,18 @@
     )(stay, up, down)
 
 
-def place_kernel(parts, x_lane_ref, x_slot_ref, z_lane_ref, z_slot_ref, *refs):
+def place_kernel(parts, taken_ref, early_ref, x_lane_ref, x_slot_ref, z_lane_ref, z_slot_ref, *refs):
     arrays, (out_ref, held, in_sem, out_sem) = refs[: LANES * len(parts)], refs[LANES * len(parts) :]
+    early = early_ref.shape[1]
     count = out_ref.shape[0]
 
+    def take_early(index):
+        return pltpu.make_async_copy(
+            early_ref.at[taken_ref[index]], held.at[index, pl.ds(0, early)], in_sem.at[len(parts), index]
+        )
+
     def take(index, carry):
+        take_early(index).start()
         for number, (axis, first, bands) in enumerate(parts):
             lane_ref, slot_ref = (x_lane_ref, x_slot_ref) if axis == "x" else (z_lane_ref, z_slot_ref)
             for lane in range(LANES):
@@ -243,6 +375,7 @@
     lax.fori_loop(0, count, take, 0)
 
     def put(index, carry):
+        take_early(index).wait()
         for number, (axis, first, bands) in enumerate(parts):
             pltpu.make_async_copy(
                 arrays[LANES * number].at[0], held.at[index, pl.ds(first, bands)], in_sem.at[number, index]
@@ -259,19 +392,21 @@
     lax.fori_loop(0, count, finish, 0)
 
 
-def place(parts, taken, arrays, shape):
+def place(parts, taken, early, picks, arrays, shape):
     return pl.pallas_call(
         functools.partial(place_kernel, parts),
         out_shape=jax.ShapeDtypeStruct(shape, jnp.bfloat16),
-        in_specs=[pl.BlockSpec(memory_space=pltpu.SMEM)] * 4 + [pl.BlockSpec(memory_space=pl.ANY)] * len(arrays),
+        in_specs=[pl.BlockSpec(memory_space=pltpu.SMEM), pl.BlockSpec(memory_space=pl.ANY)]
+        + [pl.BlockSpec(memory_space=pltpu.SMEM)] * 4
+        + [pl.BlockSpec(memory_space=pl.ANY)] * len(arrays),
         out_specs=pl.BlockSpec(memory_space=pl.ANY),
         scratch_shapes=[
             pltpu.VMEM(shape, jnp.bfloat16),
-            pltpu.SemaphoreType.DMA((len(parts), shape[0])),
+            pltpu.SemaphoreType.DMA((len(parts) + 1, shape[0])),
             pltpu.SemaphoreType.DMA((shape[0],)),
         ],
         name="place",
-    )(*taken, *arrays)
+    )(taken, early, *picks, *arrays)
 
 
 def local(tiles, seam_list, source, offsets, fractions, blend):
@@ -282,7 +417,7 @@
     per_owner = source.shape[0] // tile_count
     slots = 8 * LANES
 
-    parts, first = [], 0
+    parts, first = [], EARLY
     for axis, bands in CHUNKS:
         parts.append((axis, first, bands))
         first += bands
@@ -299,14 +434,12 @@
     near_list_by = {axis: next_zone(seam_list, axis, 1) for axis in ("x", "z")}
     list_by = {axis: hop(seam_list, axis, 1) for axis in ("x", "z")}
 
+    near_early = passed_along(pick(seam_list, tiles, 0, EARLY), "zone", 1)
     nears, beyonds, nears_beyond = [], [], []
     for part, (axis, first, bands) in enumerate(parts):
         nears.append(passed_along(pick(seam_list, tiles, first, bands), "zone", 1))
         beyonds.append(hop(tiles[:, first : first + bands], axis, 1))
-        if part == 0:
-            nears_beyond.append(hop(nears[0], axis, 1))
-        else:
-            nears_beyond.append(passed_along(pick(list_by[axis], beyonds[part], 0, bands), "zone", 1))
+        nears_beyond.append(passed_along(pick(list_by[axis], beyonds[part], 0, bands), "zone", 1))
 
     def coordinates(device):
         return device // (2 * RING), (device // 2) % RING, device % 2
@@ -326,47 +459,76 @@
     own_rank = jnp.sum(((own_src[:, None] == own_src[None, :]) & earlier).astype(jnp.int32), axis=1)
     from_x, from_z, from_core = coordinates(own_src)
 
-    def lists(my_p, my_q, src_p, src_q, own_p, own_q):
+    tile_of = (source % local_count).reshape(tile_count, per_owner)
+    in_next = zone_index > 0
+
+    def in_list(device_list):
+        return jnp.any(tile_of[:, :, None] == device_list[None, None, :], axis=2) & in_next
+
+    def line(plain, flagged, values):
+        def place_in_line(members):
+            within = jnp.sum((members[:, None, :] & earlier[None]).astype(jnp.int32), axis=2)
+            each = jnp.sum(members.astype(jnp.int32), axis=1)
+            return within + jnp.sum(jnp.where(owners_ahead, each[None, :], 0), axis=1)[:, None], jnp.sum(each)
+
+        plain_turn, plain_count = place_in_line(plain)
+        seam_turn, seam_count = place_in_line(flagged)
+        turn = jnp.where(plain, plain_turn, jnp.where(flagged, plain_count + seam_turn, -1))
+        hit = turn[None] == jnp.arange(slots, dtype=jnp.int32)[:, None, None]
+        listed = tuple(jnp.sum(jnp.where(hit, value[None], 0), axis=(1, 2)) for value in values)
+        return (jnp.stack([plain_count, plain_count + seam_count]),) + listed
+
+    taps = jnp.concatenate([cubic_weight(step - fractions[:, axis]) for axis in range(2) for step in STEPS])
+    flat_offsets = offsets.reshape(-1)
+    mine = src_device == myself
+    flags = in_list(near_list)
+    early_list = line(mine & ~flags, mine & flags, (block_ids, 2 * owner_ids[:, None] + rank))
+    scalars = early_list + (source, flat_offsets, taps, blend, near_list)
+    outgoing = render_early(scalars, tiles, 0, EARLY, slots)
+    outgoing = render_early(scalars, tiles, 0, EARLY, slots, near_early, outgoing)
+    early = swap(outgoing, 2)
+    outgoing, src_device, rank, block_ids, own_src = lax.optimization_barrier(
+        (outgoing, src_device, rank, block_ids, own_src)
+    )
+    src_x, src_z, src_core = coordinates(src_device)
+    from_x, from_z, from_core = coordinates(own_src)
+
+    def lists(my_p, my_q, src_p, src_q, own_p, own_q, lists_by_side):
         behind = (my_p - src_p) & (RING - 1)
         ahead = (own_p - my_p) & (RING - 1)
         mine = (src_core == my_core) & (src_q == my_q)
         mine = mine & (((behind == 0) & ((ahead == 0) | (ahead == 3))) | ((behind == 1) & ((ahead == 0) | (ahead == 1))))
         lane = 2 * ((own_q - my_q) & (RING - 1)) + (own_core != my_core).astype(jnp.int32)
         slot = jnp.where(ahead == 0, 4 * lane + 2 * behind + rank, 2 * lane + rank)
-        within = jnp.sum((mine[:, None, :] & earlier[None]).astype(jnp.int32), axis=2)
-        each = jnp.sum(mine.astype(jnp.int32), axis=1)
-        turn = within + jnp.sum(jnp.where(owners_ahead, each[None, :], 0), axis=1)[:, None]
-        hit = mine[None] & (turn[None] == jnp.arange(slots, dtype=jnp.int32)[:, None, None])
-
-        def listed(values):
-            return jnp.sum(jnp.where(hit, values[None], 0), axis=(1, 2))
-
-        return jnp.sum(each)[None], listed(block_ids), listed(64 * ahead + slot), listed(behind)
+        flags = jnp.where(behind == 0, in_list(lists_by_side[0]), in_list(lists_by_side[1]))
+        return line(mine & ~flags, mine & flags, (block_ids, 64 * ahead + slot, behind))
 
     def taken(my_p, my_q, src_p, src_q):
         lane = 2 * ((my_q - src_q) & (RING - 1)) + (from_core != my_core).astype(jnp.int32)
         return lane, 2 * ((my_p - src_p) & (RING - 1)) + own_rank
 
     by_axis = {
-        "x": lists(my_x, my_z, src_x, src_z, own_x, own_z),
-        "z": lists(my_z, my_x, src_z, src_x, own_z, own_x),
+        "x": lists(my_x, my_z, src_x, src_z, own_x, own_z, (near_list, near_list_by["x"])),
+        "z": lists(my_z, my_x, src_z, src_x, own_z, own_x, (near_list, near_list_by["z"])),
     }
     picks = taken(my_x, my_z, from_x, from_z) + taken(my_z, my_x, from_z, from_x)
-    taps = jnp.concatenate([cubic_weight(step - fractions[:, axis]) for axis in range(2) for step in STEPS])
-    flat_offsets = offsets.reshape(-1)
-    zone_flag = zone_index[None].astype(jnp.int32)
-    listed_by = {axis: jnp.concatenate([near_list, near_list_by[axis], zone_flag]) for axis in ("x", "z")}
-
+    listed_by = {axis: jnp.concatenate([near_list, near_list_by[axis]]) for axis in ("x", "z")}
+
+    begun = []
+    for part, (axis, first, bands) in enumerate(parts):
+        scalars = by_axis[axis] + (source, flat_offsets, taps, blend, listed_by[axis])
+        begun.append(render(scalars, tiles, beyonds[part], first))
     arrays = []
     for part, (axis, first, bands) in enumerate(parts):
         scalars = by_axis[axis] + (source, flat_offsets, taps, blend, listed_by[axis])
-        stay, up, down = render(scalars, tiles, beyonds[part], nears[part], nears_beyond[part], first)
+        stay, up, down = render(scalars, tiles, beyonds[part], first, nears[part], nears_beyond[part], begun[part])
         came_up, came_down = hop(up, axis, 1), hop(down, axis, -1)
         packed = pack(stay, came_up, came_down)
         other = "z" if axis == "x" else "x"
         arrays += [packed[0]] + [hop(packed[lane], other, lane // 2, lane % 2) for lane in range(1, LANES)]
     shape = (per_owner, band_count, height // 2, width // 2)
-    return place(tuple(parts), picks, arrays, shape)
+    own_taken = 2 * own_src + own_rank
+    return place(tuple(parts), own_taken, early, picks, arrays, shape)
 
 
 def solution(mesh):

time: 665 us -> 563 us (0.85); the launches traced: 651 us -> 561 us
  waiting for transfers between devices: 418 us -> 282 us
  starting transfers between devices: 75.7 us -> 115 us
    ppermute x43 -> x22, waiting for transfers between devices: 357 us -> 258 us  [hop(): return lax.ppermute(value, 'tile', ring_pairs(along, steps, cross))]
    ppermute x8 -> x6, waiting for transfers between devices: 60.4 us -> 24.9 us  [passed_along(): lax.ppermute(value, axis, [(source, source + steps) for source in range(i...]
    pallas_call x0 -> x2, Pallas kernels: none -> 34.3 us  [render_early(): pl.pallas_call(functools.partial(render_early_kernel, local_count, first,...]
    ppermute x43 -> x22, starting transfers between devices: 62.5 us -> 94.5 us  [hop(): return lax.ppermute(value, 'tile', ring_pairs(along, steps, cross))]
    pallas_call x4, Pallas kernels: 83.8 us -> 59.9 us  [render(): pl.pallas_call(functools.partial(render_kernel, local_count, first, bands...]
    all_to_all x0 -> x1, starting transfers between devices: none -> 10 us  [swap(): lax.all_to_all(pairs, 'tile', split_axis=0, concat_axis=0, tiled=True)]
    pallas_call x4 -> x2, Pallas kernels: 23.6 us -> 16.5 us  [pack(): pl.pallas_call(pack_kernel, out_shape=[jax.ShapeDtypeStruct(shape, stay.d...]
    pallas_call x7 -> x5, Pallas kernels: 18.5 us -> 14.2 us  [pick(): pl.pallas_call(functools.partial(pick_kernel, first, bands), out_shape=ja...]
  transfers between devices with their start and end apart: 53 -> 31, of which waited for: 21 -> 11; matrix products, arithmetic and copies ran while one was open for 3% -> 4% of each run, Pallas kernels for 19% -> 22%
where the time goes in v6:
time: 563 us; the launch traced here: 561 us
  waiting for transfers between devices  282 us (50%)
  Pallas kernels  134 us (24%)
  starting transfers between devices  115 us (20%)
  other arithmetic  16.6 us (3%)
  local copies, waits for them, and re-layouts  8.97 us (2%)
    ppermute x22, waiting for transfers between devices, hop(): return lax.ppermute(value, 'tile', ring_pairs(along, steps, cross))  258 us
    ppermute x22, starting transfers between devices, hop(): return lax.ppermute(value, 'tile', ring_pairs(along, steps, cross))  94.5 us
    pallas_call x4, Pallas kernels, render(): pl.pallas_call(functools.partial(render_kernel, local_count, first, bands...  59.9 us
    pallas_call x2, Pallas kernels, render_early(): pl.pallas_call(functools.partial(render_early_kernel, local_count, first,...  34.3 us
    ppermute x6, waiting for transfers between devices, passed_along(): lax.ppermute(value, axis, [(source, source + steps) for source in range(i...  24.9 us
    pallas_call x2, Pallas kernels, pack(): pl.pallas_call(pack_kernel, out_shape=[jax.ShapeDtypeStruct(shape, stay.d...  16.5 us
    pallas_call x5, Pallas kernels, pick(): pl.pallas_call(functools.partial(pick_kernel, first, bands), out_shape=ja...  14.2 us
  transfers between devices with their start and end apart: 31, of which 11 were waited for; matrix products, arithmetic and copies ran while one was open for 4% of the time, Pallas kernels for 22%

profile of v6, /device:TPU:60, one launch (start us, length us, event | category | flops | bytes accessed | tf_op | source)
XLA Modules:
  0.0 561.5 jit_solution(15460640542047473818)
XLA Ops:
  0.0 1.3 collective-permute-start
  1.3 1.3 collective-permute-start.16
  2.6 1.3 collective-permute-start.2
  3.9 2.0 collective-permute-start.19
  5.9 1.2 collective-permute-start.5
  7.1 0.7 add_select_fusion.4
  7.8 0.7 broadcast_compare_fusion.3
  8.6 2.6 pick.5
  11.2 4.4 fusion.42
  15.7 2.9 pick.8
  18.6 3.0 pick.6
  22.2 0.8 reshape.346.offsets_ref
  23.3 1.3 collective-permute-start.1
  24.6 1.7 collective-permute-start.17
  26.3 1.3 collective-permute-start.18
  28.1 0.7 convert_reduce_fusion.18
  29.0 0.6 select_select_fusion.2
  31.1 1.0 select_reduce_fusion.6
  32.7 1.2 pad_add_fusion.range_ref
  33.8 13.0 %early.1.refs_1_ = bf16[64,3,128,128]{3,2,1,0:T(8,128)(2,1)} custom-call(s32[2]{0:T(128)} %pad_add_fusion.range_ref, s32[64]{0:T(128)} %get-tuple-element.76.blocks_ref, s32[64]{0:T(128)} %get-tuple-element.75.slots_ref, s32[768]{0:T(1024)} %source_ref.11, s32[1536]{0:T(1024)} %reshape.346.offsets_ref, f32[6144]{0:T(1024)} %copy-done.12, f32[768]{0:T(1024)} %blend_ref.11, ...), custom_call_target="tpu_custom_call" | custom-call | flops 7247757312 | bytes 1179648 | tf_op jit(solution)/shard_map/early/pallas_call | solution.py:163
  46.8 1.1 collective-permute-done.1.refs_0_
  48.5 21.3 %early_seams.1 = bf16[64,3,128,128]{3,2,1,0:T(8,128)(2,1)} custom-call(s32[2]{0:T(128)} %pad_add_fusion.range_ref, s32[64]{0:T(128)} %get-tuple-element.76.blocks_ref, s32[64]{0:T(128)} %get-tuple-element.75.slots_ref, s32[768]{0:T(1024)} %source_ref.11, s32[1536]{0:T(1024)} %reshape.346.offsets_ref, ...), custom_call_target="tpu_custom_call", output_to_operand_aliasing={{}: (10, {})} | custom-call | flops 7247757312 | bytes 1179648 | tf_op jit(solution)/shard_map/early_seams/pallas_call | solution.py:163
  69.9 0.7 convert_reduce_fusion.9
  70.7 0.7 convert_reduce_fusion.13
  71.7 0.7 convert_reduce_fusion.7
  72.7 0.6 select_select_fusion.1
  75.0 0.7 select_select_fusion
  77.1 1.2 pad_add_fusion.3.range_ref
  78.4 1.2 pad_add_fusion.1.range_ref
  79.6 1.6 select_reduce_fusion
  81.2 1.3 collective-permute-start.4
  82.5 1.3 copy-done.1
  83.8 3.0 pick.9
  86.8 1.3 collective-permute-start.20
  88.1 2.9 collective-permute-done.3.tiles_ref.beyond_ref
  91.0 2.8 pick.7
  93.8 1.3 collective-permute-start.6
  95.1 12.9 %late.3 = (bf16[32,5,128,128]{3,2,1,0:T(8,128)(2,1)}, bf16[16,5,128,128]{3,2,1,0:T(8,128)(2,1)}, bf16[16,5,128,128]{3,2,1,0:T(8,128)(2,1)}) custom-call(s32[2]{0:T(128)} %pad_add_fusion.3.range_ref, s32[64]{0:T(128)} %get-tuple-element.71.blocks_ref, s32[64]{0:T(128)} %get-tuple-element.70.into_ref, s32[64]{0:T(128)} %get-tuple-element.69.side_ref, ...), custom_call_target="tpu_custom_call" | custom-call | flops 12079595520 | bytes 1966080 | tf_op jit(solution)/shard_map/late/pallas_call | solution.py:292
  108.0 12.9 %late.2 = (bf16[32,5,128,128]{3,2,1,0:T(8,128)(2,1)}, bf16[16,5,128,128]{3,2,1,0:T(8,128)(2,1)}, bf16[16,5,128,128]{3,2,1,0:T(8,128)(2,1)}) custom-call(s32[2]{0:T(128)} %pad_add_fusion.1.range_ref, s32[64]{0:T(128)} %get-tuple-element.72.blocks_ref, s32[64]{0:T(128)} %get-tuple-element.74.into_ref, s32[64]{0:T(128)} %get-tuple-element.73.side_ref, ...), custom_call_target="tpu_custom_call" | custom-call | flops 12079595520 | bytes 1966080 | tf_op jit(solution)/shard_map/late/pallas_call | solution.py:292
  121.0 23.7 %collective-permute-done.20.refs_1_ = bf16[2,5,256,256]{3,2,1,0:T(8,128)(2,1)} collective-permute-done((bf16[2,5,256,256]{3,2,1,0:T(8,128)(2,1)}, bf16[2,5,256,256]{3,2,1,0:T(8,128)(2,1)}, u32[]{:S(2)}, u32[]{:S(2)}) %collective-permute-start.20) | collective-permute-done | bytes 1310752 | tf_op jit(solution)/shard_map/ppermute | solution.py:22
  144.7 16.0 %late_seams.3 = (bf16[32,5,128,128]{3,2,1,0:T(8,128)(2,1)}, bf16[16,5,128,128]{3,2,1,0:T(8,128)(2,1)}, bf16[16,5,128,128]{3,2,1,0:T(8,128)(2,1)}) custom-call(s32[2]{0:T(128)} %pad_add_fusion.3.range_ref, s32[64]{0:T(128)} %get-tuple-element.71.blocks_ref, ...), custom_call_target="tpu_custom_call", output_to_operand_aliasing={{0}: (13, {}), {1}: (14, {}), {2}: (15, {})} | custom-call | flops 12079595520 | bytes 1966080 | tf_op jit(solution)/shard_map/late_seams/pallas_call | solution.py:292
  160.7 15.0 %collective-permute-start.21 = (bf16[16,5,128,128]{3,2,1,0:T(8,128)(2,1)}, bf16[16,5,128,128]{3,2,1,0:T(8,128)(2,1)}, u32[]{:S(2)}, u32[]{:S(2)}) collective-permute-start(bf16[16,5,128,128]{3,2,1,0:T(8,128)(2,1)} %get-tuple-element.59), channel_id=1, source_target_pairs={{0,2},{1,3},{2,4},{3,5},{4,6},{5,7},{6,0},{7,1},{8,10},{9,11},{10,... | collective-permute-start | bytes 7864328 | tf_op jit(solution)/shard_map/ppermute | solution.py:43
  175.7 1.1 copy-done.11
  176.7 18.1 %late_seams.2 = (bf16[32,5,128,128]{3,2,1,0:T(8,128)(2,1)}, bf16[16,5,128,128]{3,2,1,0:T(8,128)(2,1)}, bf16[16,5,128,128]{3,2,1,0:T(8,128)(2,1)}) custom-call(s32[2]{0:T(128)} %pad_add_fusion.1.range_ref, s32[64]{0:T(128)} %get-tuple-element.72.blocks_ref, ...), custom_call_target="tpu_custom_call", output_to_operand_aliasing={{0}: (13, {}), {1}: (14, {}), {2}: (15, {})} | custom-call | flops 12079595520 | bytes 1966080 | tf_op jit(solution)/shard_map/late_seams/pallas_call | solution.py:292
  194.9 10.0 %all-to-all-start = ((bf16[32,2,3,128,128]{4,3,2,1,0:T(8,128)(2,1)}), bf16[32,2,3,128,128]{4,3,2,1,0:T(8,128)(2,1)}, u32[]{:S(2)}, u32[]{:S(2)}) async-start(bf16[32,2,3,128,128]{4,3,2,1,0:T(8,128)(2,1)} %bitcast.10), calls=%async_computation | async-start | bytes 12582912 | tf_op jit(solution)/shard_map/all_to_all | solution.py:187
  205.0 0.6 collective-permute-start.8
  205.6 62.4 %collective-permute-done.21.up_ref = bf16[16,5,128,128]{3,2,1,0:T(8,128)(2,1)} collective-permute-done((bf16[16,5,128,128]{3,2,1,0:T(8,128)(2,1)}, bf16[16,5,128,128]{3,2,1,0:T(8,128)(2,1)}, u32[]{:S(2)}, u32[]{:S(2)}) %collective-permute-start.21) | collective-permute-done | bytes 2621472 | tf_op jit(solution)/shard_map/ppermute | solution.py:43
  268.0 8.3 %pack.3 = (bf16[8,5,128,128]{3,2,1,0:T(8,128)(2,1)}, bf16[8,5,128,128]{3,2,1,0:T(8,128)(2,1)}, bf16[8,5,128,128]{3,2,1,0:T(8,128)(2,1)}, bf16[8,5,128,128]{3,2,1...) custom-call(bf16[32,5,128,128]{3,2,1,0:T(8,128)(2,1)} %get-tuple-ele, ...), custom_call_target="tpu_custom_call" | custom-call | tf_op jit(solution)/shard_map/pack/pallas_call | solution.py:335
  276.6 3.1 collective-permute-start.26
  279.7 53.5 %collective-permute-done.8.down_ref = bf16[16,5,128,128]{3,2,1,0:T(8,128)(2,1)} collective-permute-done((bf16[16,5,128,128]{3,2,1,0:T(8,128)(2,1)}, bf16[16,5,128,128]{3,2,1,0:T(8,128)(2,1)}, u32[]{:S(2)}, u32[]{:S(2)}) %collective-permute-start.8) | collective-permute-done | bytes 2621472 | tf_op jit(solution)/shard_map/ppermute | solution.py:43
  333.2 8.1 %collective-permute-start.27 = (bf16[8,5,128,128]{3,2,1,0:T(8,128)(2,1)}, bf16[8,5,128,128]{3,2,1,0:T(8,128)(2,1)}, u32[]{:S(2)}, u32[]{:S(2)}) collective-permute-start(bf16[8,5,128,128]{3,2,1,0:T(8,128)(2,1)} %get-tuple-element.66), channel_id=1, source_target_pairs={{0,17},{1,16},{2,19},{3,18},{4,21},{5,20},{6,23},{7,22},{8,25},{9,... | collective-permute-start | bytes 3932168 | tf_op jit(solution)/shard_map/ppermute | solution.py:43
  341.3 8.3 %pack.2 = (bf16[8,5,128,128]{3,2,1,0:T(8,128)(2,1)}, bf16[8,5,128,128]{3,2,1,0:T(8,128)(2,1)}, bf16[8,5,128,128]{3,2,1,0:T(8,128)(2,1)}, bf16[8,5,128,128]{3,2,1...) custom-call(bf16[32,5,128,128]{3,2,1,0:T(8,128)(2,1)} %get-tuple-ele, ...), custom_call_target="tpu_custom_call" | custom-call | tf_op jit(solution)/shard_map/pack/pallas_call | solution.py:335
  349.7 4.3 collective-permute-done.24.refs_10_
  354.0 28.1 %collective-permute-done.25.refs_11_ = bf16[8,5,128,128]{3,2,1,0:T(8,128)(2,1)} collective-permute-done((bf16[8,5,128,128]{3,2,1,0:T(8,128)(2,1)}, bf16[8,5,128,128]{3,2,1,0:T(8,128)(2,1)}, u32[]{:S(2)}, u32[]{:S(2)}) %collective-permute-start.25) | collective-permute-done | bytes 1310752 | tf_op jit(solution)/shard_map/ppermute | solution.py:43
  382.1 48.4 %collective-permute-start.10 = (bf16[8,5,128,128]{3,2,1,0:T(8,128)(2,1)}, bf16[8,5,128,128]{3,2,1,0:T(8,128)(2,1)}, u32[]{:S(2)}, u32[]{:S(2)}) collective-permute-start(bf16[8,5,128,128]{3,2,1,0:T(8,128)(2,1)} %get-tuple-element.49), channel_id=1, source_target_pairs={{0,2},{1,3},{2,4},{3,5},{4,6},{5,7},{6,0},{7,1},{8,10},{9,11},{10,... | collective-permute-start | bytes 3932168 | tf_op jit(solution)/shard_map/ppermute | solution.py:43
  430.5 4.8 collective-permute-start.11
  435.3 3.0 collective-permute-start.13
  438.4 6.0 %collective-permute-done.29.refs_15_ = bf16[8,5,128,128]{3,2,1,0:T(8,128)(2,1)S(1)} collective-permute-done((bf16[8,5,128,128]{3,2,1,0:T(8,128)(2,1)}, bf16[8,5,128,128]{3,2,1,0:T(8,128)(2,1)S(1)}, u32[]{:S(2)}, u32[]{:S(2)}) %collective-permute-start.29) | collective-permute-done | bytes 1310752 | tf_op jit(solution)/shard_map/ppermute | solution.py:43
  444.4 1.3 collective-permute-start.14
  445.7 10.0 %collective-permute-done.10.refs_2_ = bf16[8,5,128,128]{3,2,1,0:T(8,128)(2,1)} collective-permute-done((bf16[8,5,128,128]{3,2,1,0:T(8,128)(2,1)}, bf16[8,5,128,128]{3,2,1,0:T(8,128)(2,1)}, u32[]{:S(2)}, u32[]{:S(2)}) %collective-permute-start.10) | collective-permute-done | bytes 1310752 | tf_op jit(solution)/shard_map/ppermute | solution.py:43
  455.7 84.3 %collective-permute-done.11.refs_3_ = bf16[8,5,128,128]{3,2,1,0:T(8,128)(2,1)} collective-permute-done((bf16[8,5,128,128]{3,2,1,0:T(8,128)(2,1)}, bf16[8,5,128,128]{3,2,1,0:T(8,128)(2,1)}, u32[]{:S(2)}, u32[]{:S(2)}) %collective-permute-start.11) | collective-permute-done | bytes 1310752 | tf_op jit(solution)/shard_map/ppermute | solution.py:43
  540.0 4.4 collective-permute-start.9
  546.3 6.0 %collective-permute-done.15.refs_7_ = bf16[8,5,128,128]{3,2,1,0:T(8,128)(2,1)} collective-permute-done((bf16[8,5,128,128]{3,2,1,0:T(8,128)(2,1)}, bf16[8,5,128,128]{3,2,1,0:T(8,128)(2,1)}, u32[]{:S(2)}, u32[]{:S(2)}) %collective-permute-start.15) | collective-permute-done | bytes 1310752 | tf_op jit(solution)/shard_map/ppermute | solution.py:43
  552.3 9.0 %place.1 = bf16[24,13,128,128]{3,2,1,0:T(8,128)(2,1)} custom-call(s32[24]{0:T(128)} %get-tuple-element.139.taken_ref, bf16[64,3,128,128]{3,2,1,0:T(8,128)(2,1)} %bitcast.4.early_ref, s32[24]{0:T(128)} %add.474.x_lane_ref, s32[24]{0:T(128)} %get-tuple-element.142.x_slot_ref, s32[24]{0:T(128)} %get-tuple-element.119.z_lane_ref, ...), custom_call_target="tpu_custom_call" | custom-call | tf_op jit(solution)/shard_map/place/pallas_call | solution.py:396
  (108 shorter events, 6.5 us)
Async XLA Ops:
  0.0 23.2 %collective-permute-start = (s32[2]{0:T(128)}, s32[2]{0:T(128)S(1)}, u32[]{:S(2)}, u32[]{:S(2)}) collective-permute-start(s32[2]{0:T(128)} %listed_ref.5), channel_id=1, source_target_pairs={{0,32},{32,64},{64,96},{1,33},{33,65},{65,97},{2,34},{34,66},{66,9... | collective-permute-start | bytes 32 | tf_op jit(solution)/shard_map/ppermute | solution.py:22
  1.3 23.3 %collective-permute-start.16 = (s32[2]{0:T(128)}, s32[2]{0:T(128)S(1)}, u32[]{:S(2)}, u32[]{:S(2)}) collective-permute-start(s32[2]{0:T(128)} %listed_ref.5), channel_id=1, source_target_pairs={{0,34},{1,35},{2,36},{3,37},{4,38},{5,39},{6,32},{7,33},{8,42},{9,... | collective-permute-start | bytes 32 | tf_op jit(solution)/shard_map/ppermute | solution.py:431
  2.6 23.7 %collective-permute-start.2 = (s32[2]{0:T(128)}, s32[2]{0:T(128)S(1)}, u32[]{:S(2)}, u32[]{:S(2)}) collective-permute-start(s32[2]{0:T(128)} %listed_ref.5), channel_id=1, source_target_pairs={{0,40},{1,41},{2,42},{3,43},{4,44},{5,45},{6,46},{7,47},{8,48},{9,... | collective-permute-start | bytes 32 | tf_op jit(solution)/shard_map/ppermute | solution.py:431
  3.9 77.3 %collective-permute-start.19 = (s32[2]{0:T(128)}, s32[2]{0:T(128)S(1)}, u32[]{:S(2)}, u32[]{:S(2)}) collective-permute-start(s32[2]{0:T(128)} %listed_ref.5), channel_id=1, source_target_pairs={{0,2},{1,3},{2,4},{3,5},{4,6},{5,7},{6,0},{7,1},{8,10},{9,11},{10,... | collective-permute-start | bytes 32 | tf_op jit(solution)/shard_map/ppermute | solution.py:43
  5.9 82.2 %collective-permute-start.5 = (s32[2]{0:T(128)}, s32[2]{0:T(128)S(1)}, u32[]{:S(2)}, u32[]{:S(2)}) collective-permute-start(s32[2]{0:T(128)} %listed_ref.5), channel_id=1, source_target_pairs={{0,8},{1,9},{2,10},{3,11},{4,12},{5,13},{6,14},{7,15},{8,16},{9,17... | collective-permute-start | bytes 32 | tf_op jit(solution)/shard_map/ppermute | solution.py:43
  18.5 3.4 copy-start.6
  18.6 3.5 copy-start.7
  18.6 4.7 copy-start.5
  23.2 10.6 %copy-start.12 = (f32[6144]{0:T(1024)}, f32[6144]{0:T(1024)S(1)}, u32[]{:S(2)}) copy-start(f32[6144]{0:T(1024)S(1)} %fusion.28.taps_ref) | copy-start | bytes 73732
  23.2 10.6 %copy-start.8 = (s32[2]{0:T(128)}, s32[2]{0:T(128)S(1)}, u32[]{:S(2)}) copy-start(s32[2]{0:T(128)S(1)} %collective-permute-done.listed_ref) | copy-start | bytes 28
  23.3 24.7 %collective-permute-start.1 = (bf16[2,3,256,256]{3,2,1,0:T(8,128)(2,1)S(1)}, bf16[2,3,256,256]{3,2,1,0:T(8,128)(2,1)}, u32[]{:S(2)}, u32[]{:S(2)}) collective-permute-start(bf16[2,3,256,256]{3,2,1,0:T(8,128)(2,1)S(1)} %copy-done.5), channel_id=1, source_target_pairs={{0,32},{32,64},{64,96},{1,33},{33,65},{65,97},{2,34},{34,66},{66,9... | collective-permute-start | bytes 2359304 | tf_op jit(solution)/shard_map/ppermute | solution.py:22
  24.6 58.0 %collective-permute-start.17 = (bf16[3,5,256,256]{3,2,1,0:T(8,128)(2,1)}, bf16[3,5,256,256]{3,2,1,0:T(8,128)(2,1)S(1)}, u32[]{:S(2)}, u32[]{:S(2)}) collective-permute-start(bf16[3,5,256,256]{3,2,1,0:T(8,128)(2,1)} %get-tuple-element.130), channel_id=1, source_target_pairs={{0,2},{1,3},{2,4},{3,5},{4,6},{5,7},{6,0},{7,1},{8,10},{9,11},{10,... | collective-permute-start | bytes 5898248 | tf_op jit(solution)/shard_map/ppermute | solution.py:43
  26.3 94.7 %collective-permute-start.18 = (bf16[2,5,256,256]{3,2,1,0:T(8,128)(2,1)}, bf16[2,5,256,256]{3,2,1,0:T(8,128)(2,1)}, u32[]{:S(2)}, u32[]{:S(2)}) collective-permute-start(bf16[2,5,256,256]{3,2,1,0:T(8,128)(2,1)} %pick.8), channel_id=1, source_target_pairs={{0,32},{32,64},{64,96},{1,33},{33,65},{65,97},{2,34},{34,66},{66,9... | collective-permute-start | bytes 3932168 | tf_op jit(solution)/shard_map/ppermute | solution.py:22
  48.0 33.2 %copy-start.4 = (bf16[2,5,256,256]{3,2,1,0:T(8,128)(2,1)S(1)}, bf16[2,5,256,256]{3,2,1,0:T(8,128)(2,1)}, u32[]{:S(2)}) copy-start(bf16[2,5,256,256]{3,2,1,0:T(8,128)(2,1)} %pick.6) | copy-start | bytes 3932164
  48.0 43.0 %collective-permute-start.3 = (bf16[3,5,256,256]{3,2,1,0:T(8,128)(2,1)}, bf16[3,5,256,256]{3,2,1,0:T(8,128)(2,1)}, u32[]{:S(2)}, u32[]{:S(2)}) collective-permute-start(bf16[3,5,256,256]{3,2,1,0:T(8,128)(2,1)} %get-tuple-element.131), channel_id=1, source_target_pairs={{0,8},{1,9},{2,10},{3,11},{4,12},{5,13},{6,14},{7,15},{8,16},{9,17... | collective-permute-start | bytes 5898248 | tf_op jit(solution)/shard_map/ppermute | solution.py:43
  81.2 1.3 copy-start.10
  81.2 94.4 %collective-permute-start.4 = (bf16[2,5,256,256]{3,2,1,0:T(8,128)(2,1)S(1)}, bf16[2,5,256,256]{3,2,1,0:T(8,128)(2,1)}, u32[]{:S(2)}, u32[]{:S(2)}) collective-permute-start(bf16[2,5,256,256]{3,2,1,0:T(8,128)(2,1)S(1)} %copy-done.4), channel_id=1, source_target_pairs={{0,32},{32,64},{64,96},{1,33},{33,65},{65,97},{2,34},{34,66},{66,9... | collective-permute-start | bytes 3932168 | tf_op jit(solution)/shard_map/ppermute | solution.py:22
  82.5 1.3 copy-start.1
  86.8 57.9 %collective-permute-start.20 = (bf16[2,5,256,256]{3,2,1,0:T(8,128)(2,1)}, bf16[2,5,256,256]{3,2,1,0:T(8,128)(2,1)}, u32[]{:S(2)}, u32[]{:S(2)}) collective-permute-start(bf16[2,5,256,256]{3,2,1,0:T(8,128)(2,1)} %pick.9), channel_id=1, source_target_pairs={{0,32},{32,64},{64,96},{1,33},{33,65},{65,97},{2,34},{34,66},{66,9... | collective-permute-start | bytes 3932168 | tf_op jit(solution)/shard_map/ppermute | solution.py:22
  88.1 2.9 copy-start.9
  93.8 81.8 %collective-permute-start.6 = (bf16[2,5,256,256]{3,2,1,0:T(8,128)(2,1)}, bf16[2,5,256,256]{3,2,1,0:T(8,128)(2,1)S(1)}, u32[]{:S(2)}, u32[]{:S(2)}) collective-permute-start(bf16[2,5,256,256]{3,2,1,0:T(8,128)(2,1)} %pick.7), channel_id=1, source_target_pairs={{0,32},{32,64},{64,96},{1,33},{33,65},{65,97},{2,34},{34,66},{66,9... | collective-permute-start | bytes 3932168 | tf_op jit(solution)/shard_map/ppermute | solution.py:22
  160.7 107.4 %collective-permute-start.21 = (bf16[16,5,128,128]{3,2,1,0:T(8,128)(2,1)}, bf16[16,5,128,128]{3,2,1,0:T(8,128)(2,1)}, u32[]{:S(2)}, u32[]{:S(2)}) collective-permute-start(bf16[16,5,128,128]{3,2,1,0:T(8,128)(2,1)} %get-tuple-element.59), channel_id=1, source_target_pairs={{0,2},{1,3},{2,4},{3,5},{4,6},{5,7},{6,0},{7,1},{8,10},{9,11},{10,... | collective-permute-start | bytes 7864328 | tf_op jit(solution)/shard_map/ppermute | solution.py:43
  175.7 92.4 %collective-permute-start.22 = (bf16[16,5,128,128]{3,2,1,0:T(8,128)(2,1)}, bf16[16,5,128,128]{3,2,1,0:T(8,128)(2,1)}, u32[]{:S(2)}, u32[]{:S(2)}) collective-permute-start(bf16[16,5,128,128]{3,2,1,0:T(8,128)(2,1)} %get-tuple-element.60), channel_id=1, source_target_pairs={{0,6},{1,7},{2,0},{3,1},{4,2},{5,3},{6,4},{7,5},{8,14},{9,15},{10,... | collective-permute-start | bytes 7864328 | tf_op jit(solution)/shard_map/ppermute | solution.py:43
  175.7 1.1 copy-start.11
  194.8 81.7 %collective-permute-start.7 = (bf16[16,5,128,128]{3,2,1,0:T(8,128)(2,1)}, bf16[16,5,128,128]{3,2,1,0:T(8,128)(2,1)S(1)}, u32[]{:S(2)}, u32[]{:S(2)}) collective-permute-start(bf16[16,5,128,128]{3,2,1,0:T(8,128)(2,1)} %get-tuple-element.45), channel_id=1, source_target_pairs={{0,8},{1,9},{2,10},{3,11},{4,12},{5,13},{6,14},{7,15},{8,16},{9,17... | collective-permute-start | bytes 7864328 | tf_op jit(solution)/shard_map/ppermute | solution.py:43
  194.9 351.3 %all-to-all-start = ((bf16[32,2,3,128,128]{4,3,2,1,0:T(8,128)(2,1)}), bf16[32,2,3,128,128]{4,3,2,1,0:T(8,128)(2,1)}, u32[]{:S(2)}, u32[]{:S(2)}) async-start(bf16[32,2,3,128,128]{4,3,2,1,0:T(8,128)(2,1)} %bitcast.10), calls=%async_computation | async-start | bytes 12582912 | tf_op jit(solution)/shard_map/all_to_all | solution.py:187
  205.0 128.3 %collective-permute-start.8 = (bf16[16,5,128,128]{3,2,1,0:T(8,128)(2,1)}, bf16[16,5,128,128]{3,2,1,0:T(8,128)(2,1)}, u32[]{:S(2)}, u32[]{:S(2)}) collective-permute-start(bf16[16,5,128,128]{3,2,1,0:T(8,128)(2,1)} %get-tuple-element.46), channel_id=1, source_target_pairs={{0,24},{1,25},{2,26},{3,27},{4,28},{5,29},{6,30},{7,31},{8,0},{9,1... | collective-permute-start | bytes 7864328 | tf_op jit(solution)/shard_map/ppermute | solution.py:43
  276.3 73.3 %collective-permute-start.23 = (bf16[8,5,128,128]{3,2,1,0:T(8,128)(2,1)}, bf16[8,5,128,128]{3,2,1,0:T(8,128)(2,1)}, u32[]{:S(2)}, u32[]{:S(2)}) collective-permute-start(bf16[8,5,128,128]{3,2,1,0:T(8,128)(2,1)} %get-tuple-element.62), channel_id=1, source_target_pairs={{0,1},{1,0},{2,3},{3,2},{4,5},{5,4},{6,7},{7,6},{8,9},{9,8},{10,11... | collective-permute-start | bytes 3932168 | tf_op jit(solution)/shard_map/ppermute | solution.py:43
  276.4 77.6 %collective-permute-start.24 = (bf16[8,5,128,128]{3,2,1,0:T(8,128)(2,1)}, bf16[8,5,128,128]{3,2,1,0:T(8,128)(2,1)}, u32[]{:S(2)}, u32[]{:S(2)}) collective-permute-start(bf16[8,5,128,128]{3,2,1,0:T(8,128)(2,1)} %get-tuple-element.63), channel_id=1, source_target_pairs={{0,8},{1,9},{2,10},{3,11},{4,12},{5,13},{6,14},{7,15},{8,16},{9,17... | collective-permute-start | bytes 3932168 | tf_op jit(solution)/shard_map/ppermute | solution.py:43
  276.5 105.6 %collective-permute-start.25 = (bf16[8,5,128,128]{3,2,1,0:T(8,128)(2,1)}, bf16[8,5,128,128]{3,2,1,0:T(8,128)(2,1)}, u32[]{:S(2)}, u32[]{:S(2)}) collective-permute-start(bf16[8,5,128,128]{3,2,1,0:T(8,128)(2,1)} %get-tuple-element.64), channel_id=1, source_target_pairs={{0,9},{1,8},{2,11},{3,10},{4,13},{5,12},{6,15},{7,14},{8,17},{9,16... | collective-permute-start | bytes 3932168 | tf_op jit(solution)/shard_map/ppermute | solution.py:43
  276.6 64.7 %copy-start = (bf16[16,5,128,128]{3,2,1,0:T(8,128)(2,1)}, bf16[16,5,128,128]{3,2,1,0:T(8,128)(2,1)S(1)}, u32[]{:S(2)}) copy-start(bf16[16,5,128,128]{3,2,1,0:T(8,128)(2,1)S(1)} %collective-permute-done.7.up_ref) | copy-start | bytes 7864324
  276.6 153.9 %collective-permute-start.26 = (bf16[8,5,128,128]{3,2,1,0:T(8,128)(2,1)}, bf16[8,5,128,128]{3,2,1,0:T(8,128)(2,1)}, u32[]{:S(2)}, u32[]{:S(2)}) collective-permute-start(bf16[8,5,128,128]{3,2,1,0:T(8,128)(2,1)} %get-tuple-element.65), channel_id=1, source_target_pairs={{0,16},{1,17},{2,18},{3,19},{4,20},{5,21},{6,22},{7,23},{8,24},{9,... | collective-permute-start | bytes 3932168 | tf_op jit(solution)/shard_map/ppermute | solution.py:43
  333.2 102.1 %collective-permute-start.27 = (bf16[8,5,128,128]{3,2,1,0:T(8,128)(2,1)}, bf16[8,5,128,128]{3,2,1,0:T(8,128)(2,1)}, u32[]{:S(2)}, u32[]{:S(2)}) collective-permute-start(bf16[8,5,128,128]{3,2,1,0:T(8,128)(2,1)} %get-tuple-element.66), channel_id=1, source_target_pairs={{0,17},{1,16},{2,19},{3,18},{4,21},{5,20},{6,23},{7,22},{8,25},{9,... | collective-permute-start | bytes 3932168 | tf_op jit(solution)/shard_map/ppermute | solution.py:43
  349.6 85.7 %collective-permute-start.28 = (bf16[8,5,128,128]{3,2,1,0:T(8,128)(2,1)}, bf16[8,5,128,128]{3,2,1,0:T(8,128)(2,1)S(1)}, u32[]{:S(2)}, u32[]{:S(2)}) collective-permute-start(bf16[8,5,128,128]{3,2,1,0:T(8,128)(2,1)} %get-tuple-element.67), channel_id=1, source_target_pairs={{0,24},{1,25},{2,26},{3,27},{4,28},{5,29},{6,30},{7,31},{8,0},{9,1... | collective-permute-start | bytes 3932168 | tf_op jit(solution)/shard_map/ppermute | solution.py:43
  354.0 90.4 %collective-permute-start.29 = (bf16[8,5,128,128]{3,2,1,0:T(8,128)(2,1)}, bf16[8,5,128,128]{3,2,1,0:T(8,128)(2,1)S(1)}, u32[]{:S(2)}, u32[]{:S(2)}) collective-permute-start(bf16[8,5,128,128]{3,2,1,0:T(8,128)(2,1)} %get-tuple-element.68), channel_id=1, source_target_pairs={{0,25},{1,24},{2,27},{3,26},{4,29},{5,28},{6,31},{7,30},{8,1},{9,0... | collective-permute-start | bytes 3932168 | tf_op jit(solution)/shard_map/ppermute | solution.py:43
  382.1 73.6 %collective-permute-start.10 = (bf16[8,5,128,128]{3,2,1,0:T(8,128)(2,1)}, bf16[8,5,128,128]{3,2,1,0:T(8,128)(2,1)}, u32[]{:S(2)}, u32[]{:S(2)}) collective-permute-start(bf16[8,5,128,128]{3,2,1,0:T(8,128)(2,1)} %get-tuple-element.49), channel_id=1, source_target_pairs={{0,2},{1,3},{2,4},{3,5},{4,6},{5,7},{6,0},{7,1},{8,10},{9,11},{10,... | collective-permute-start | bytes 3932168 | tf_op jit(solution)/shard_map/ppermute | solution.py:43
  430.5 109.5 %collective-permute-start.11 = (bf16[8,5,128,128]{3,2,1,0:T(8,128)(2,1)}, bf16[8,5,128,128]{3,2,1,0:T(8,128)(2,1)}, u32[]{:S(2)}, u32[]{:S(2)}) collective-permute-start(bf16[8,5,128,128]{3,2,1,0:T(8,128)(2,1)} %get-tuple-element.50), channel_id=1, source_target_pairs={{0,3},{1,2},{2,5},{3,4},{4,7},{5,6},{6,1},{7,0},{8,11},{9,10},{10,... | collective-permute-start | bytes 3932168 | tf_op jit(solution)/shard_map/ppermute | solution.py:43
  435.3 110.9 %collective-permute-start.12 = (bf16[8,5,128,128]{3,2,1,0:T(8,128)(2,1)}, bf16[8,5,128,128]{3,2,1,0:T(8,128)(2,1)}, u32[]{:S(2)}, u32[]{:S(2)}) collective-permute-start(bf16[8,5,128,128]{3,2,1,0:T(8,128)(2,1)} %get-tuple-element.51), channel_id=1, source_target_pairs={{0,4},{1,5},{2,6},{3,7},{4,0},{5,1},{6,2},{7,3},{8,12},{9,13},{10,... | collective-permute-start | bytes 3932168 | tf_op jit(solution)/shard_map/ppermute | solution.py:43
  435.3 116.9 %copy-start.2 = (bf16[8,5,128,128]{3,2,1,0:T(8,128)(2,1)}, bf16[8,5,128,128]{3,2,1,0:T(8,128)(2,1)S(1)}, u32[]{:S(2)}) copy-start(bf16[8,5,128,128]{3,2,1,0:T(8,128)(2,1)S(1)} %collective-permute-done.28.refs_14_) | copy-start | bytes 3932164
  435.3 110.9 %collective-permute-start.13 = (bf16[8,5,128,128]{3,2,1,0:T(8,128)(2,1)}, bf16[8,5,128,128]{3,2,1,0:T(8,128)(2,1)}, u32[]{:S(2)}, u32[]{:S(2)}) collective-permute-start(bf16[8,5,128,128]{3,2,1,0:T(8,128)(2,1)} %get-tuple-element.52), channel_id=1, source_target_pairs={{0,5},{1,4},{2,7},{3,6},{4,1},{5,0},{6,3},{7,2},{8,13},{9,12},{10,... | collective-permute-start | bytes 3932168 | tf_op jit(solution)/shard_map/ppermute | solution.py:43
  444.4 107.9 %copy-start.3 = (bf16[8,5,128,128]{3,2,1,0:T(8,128)(2,1)}, bf16[8,5,128,128]{3,2,1,0:T(8,128)(2,1)S(1)}, u32[]{:S(2)}) copy-start(bf16[8,5,128,128]{3,2,1,0:T(8,128)(2,1)S(1)} %collective-permute-done.29.refs_15_) | copy-start | bytes 3932164
  444.4 101.9 %collective-permute-start.14 = (bf16[8,5,128,128]{3,2,1,0:T(8,128)(2,1)}, bf16[8,5,128,128]{3,2,1,0:T(8,128)(2,1)}, u32[]{:S(2)}, u32[]{:S(2)}) collective-permute-start(bf16[8,5,128,128]{3,2,1,0:T(8,128)(2,1)} %get-tuple-element.53), channel_id=1, source_target_pairs={{0,6},{1,7},{2,0},{3,1},{4,2},{5,3},{6,4},{7,5},{8,14},{9,15},{10,... | collective-permute-start | bytes 3932168 | tf_op jit(solution)/shard_map/ppermute | solution.py:43
  455.7 96.5 %collective-permute-start.15 = (bf16[8,5,128,128]{3,2,1,0:T(8,128)(2,1)}, bf16[8,5,128,128]{3,2,1,0:T(8,128)(2,1)}, u32[]{:S(2)}, u32[]{:S(2)}) collective-permute-start(bf16[8,5,128,128]{3,2,1,0:T(8,128)(2,1)} %get-tuple-element.54), channel_id=1, source_target_pairs={{0,7},{1,6},{2,1},{3,0},{4,3},{5,2},{6,5},{7,4},{8,15},{9,14},{10,... | collective-permute-start | bytes 3932168 | tf_op jit(solution)/shard_map/ppermute | solution.py:43
  540.0 12.3 %collective-permute-start.9 = (bf16[8,5,128,128]{3,2,1,0:T(8,128)(2,1)}, bf16[8,5,128,128]{3,2,1,0:T(8,128)(2,1)}, u32[]{:S(2)}, u32[]{:S(2)}) collective-permute-start(bf16[8,5,128,128]{3,2,1,0:T(8,128)(2,1)} %get-tuple-element.48), channel_id=1, source_target_pairs={{0,1},{1,0},{2,3},{3,2},{4,5},{5,4},{6,7},{7,6},{8,9},{9,8},{10,11... | collective-permute-start | bytes 3932168 | tf_op jit(solution)/shard_map/ppermute | solution.py:43

commit v7 on v6

--- a/solution.py
+++ b/solution.py
@@ -9,7 +9,7 @@
 
 
 EARLY = 3
-CHUNKS = (("x", 5), ("z", 5))
+CHUNKS = (("x", 6), ("z", 4))
 RING = 4
 LANES = 2 * RING
 ABREAST = 4
@@ -422,19 +422,11 @@
         parts.append((axis, first, bands))
         first += bands
 
-    def next_zone(value, along, steps):
-        pairs = []
-        zones = lax.axis_size("zone")
-        for zone in range(zones - 1):
-            for source, target in ring_pairs(along, steps, 0):
-                pairs.append((zone * tile_count + source, (zone + 1) * tile_count + target))
-        return lax.ppermute(value, ("zone", "tile"), pairs)
-
     near_list = passed_along(seam_list, "zone", 1)
-    near_list_by = {axis: next_zone(seam_list, axis, 1) for axis in ("x", "z")}
-    list_by = {axis: hop(seam_list, axis, 1) for axis in ("x", "z")}
-
     near_early = passed_along(pick(seam_list, tiles, 0, EARLY), "zone", 1)
+    both = {axis: hop(jnp.concatenate([seam_list, near_list]), axis, 1) for axis in ("x", "z")}
+    list_by = {axis: lists[: seam_list.shape[0]] for axis, lists in both.items()}
+    near_list_by = {axis: lists[seam_list.shape[0] :] for axis, lists in both.items()}
     nears, beyonds, nears_beyond = [], [], []
     for part, (axis, first, bands) in enumerate(parts):
         nears.append(passed_along(pick(seam_list, tiles, first, bands), "zone", 1))

time: 563 us -> 608 us (1.080)
  waiting for transfers between devices: 282 us -> 382 us
  starting transfers between devices: 115 us -> 52.3 us
    ppermute x22, waiting for transfers between devices: 258 us -> 355 us  [hop(): return lax.ppermute(value, 'tile', ring_pairs(along, steps, cross))]
    ppermute x22, starting transfers between devices: 94.5 us -> 36 us  [hop(): return lax.ppermute(value, 'tile', ring_pairs(along, steps, cross))]
  transfers between devices with their start and end apart: 31 -> 29, of which waited for: 11 -> 12; matrix products, arithmetic and copies ran while one was open for 4% -> 4% of each run, Pallas kernels for 22% -> 21%
where the time goes in v7:
time: 608 us; the launch traced here: 601 us
  waiting for transfers between devices  382 us (63%)
  Pallas kernels  134 us (22%)
  starting transfers between devices  52.3 us (9%)
  other arithmetic  15.6 us (3%)
  local copies, waits for them, and re-layouts  12.7 us (2%)
    ppermute x22, waiting for transfers between devices, hop(): return lax.ppermute(value, 'tile', ring_pairs(along, steps, cross))  355 us
    pallas_call x4, Pallas kernels, render(): pl.pallas_call(functools.partial(render_kernel, local_count, first, bands...  60.2 us
    ppermute x22, starting transfers between devices, hop(): return lax.ppermute(value, 'tile', ring_pairs(along, steps, cross))  36 us
    pallas_call x2, Pallas kernels, render_early(): pl.pallas_call(functools.partial(render_early_kernel, local_count, first,...  34.3 us
    ppermute x6, waiting for transfers between devices, passed_along(): lax.ppermute(value, axis, [(source, source + steps) for source in range(i...  26.9 us
    pallas_call x2, Pallas kernels, pack(): pl.pallas_call(pack_kernel, out_shape=[jax.ShapeDtypeStruct(shape, stay.d...  16.1 us
    pallas_call x5, Pallas kernels, pick(): pl.pallas_call(functools.partial(pick_kernel, first, bands), out_shape=ja...  14.1 us
  transfers between devices with their start and end apart: 29, of which 12 were waited for; matrix products, arithmetic and copies ran while one was open for 4% of the time, Pallas kernels for 21%

profile of v7, /device:TPU:60, one launch (start us, length us, event | category | flops | bytes accessed | tf_op | source)
XLA Modules:
  0.0 601.3 jit_solution(17711400153571187596)
XLA Ops:
  0.0 1.3 collective-permute-start
  1.3 2.6 pick.5
  3.9 1.3 collective-permute-start.1
  5.2 3.3 slice.33
  8.5 1.2 collective-permute-start.3
  9.7 3.0 pick.6
  12.7 1.3 collective-permute-start.4
  14.0 2.7 slice.36
  16.6 1.9 collective-permute-start.16
  18.8 2.9 pick.8
  22.3 0.8 reshape.346.offsets_ref
  23.4 1.6 collective-permute-start.15
  25.1 27.7 %collective-permute-done.15 = s32[4]{0:T(128)S(1)} collective-permute-done((s32[4]{0:T(128)S(1)}, s32[4]{0:T(128)S(1)}, u32[]{:S(2)}, u32[]{:S(2)}) %collective-permute-start.15) | collective-permute-done | bytes 48 | tf_op jit(solution)/shard_map/ppermute | solution.py:43
  53.3 0.6 fusion.42
  53.9 7.8 %collective-permute-done.2 = s32[4]{0:T(128)S(1)} collective-permute-done((s32[4]{0:T(128)S(1)}, s32[4]{0:T(128)S(1)}, u32[]{:S(2)}, u32[]{:S(2)}) %collective-permute-start.2) | collective-permute-done | bytes 48 | tf_op jit(solution)/shard_map/ppermute | solution.py:43
  61.7 1.3 collective-permute-start.17
  63.0 0.5 fusion.43
  64.1 0.7 convert_reduce_fusion.18
  66.4 0.6 select_select_fusion.2
  67.1 1.0 select_reduce_fusion.6
  68.1 0.7 pad_add_fusion.5
  68.8 1.2 pad_add_fusion.range_ref
  70.0 13.0 %early.1.refs_1_ = bf16[64,3,128,128]{3,2,1,0:T(8,128)(2,1)} custom-call(s32[2]{0:T(128)} %pad_add_fusion.range_ref, s32[64]{0:T(128)} %get-tuple-element.76.blocks_ref, s32[64]{0:T(128)} %get-tuple-element.75.slots_ref, s32[768]{0:T(1024)} %source_ref.11, s32[1536]{0:T(1024)} %reshape.346.offsets_ref, f32[6144]{0:T(1024)} %copy-done.13, f32[768]{0:T(1024)} %blend_ref.11, ...), custom_call_target="tpu_custom_call" | custom-call | flops 7247757312 | bytes 1179648 | tf_op jit(solution)/shard_map/early/pallas_call | solution.py:163
  83.0 21.3 %early_seams.1 = bf16[64,3,128,128]{3,2,1,0:T(8,128)(2,1)} custom-call(s32[2]{0:T(128)} %pad_add_fusion.range_ref, s32[64]{0:T(128)} %get-tuple-element.76.blocks_ref, s32[64]{0:T(128)} %get-tuple-element.75.slots_ref, s32[768]{0:T(1024)} %source_ref.11, s32[1536]{0:T(1024)} %reshape.346.offsets_ref, ...), custom_call_target="tpu_custom_call", output_to_operand_aliasing={{}: (10, {})} | custom-call | flops 7247757312 | bytes 1179648 | tf_op jit(solution)/shard_map/early_seams/pallas_call | solution.py:163
  104.5 0.7 convert_reduce_fusion.9
  105.2 0.7 convert_reduce_fusion.7
  106.2 0.7 convert_reduce_fusion.13
  107.2 0.6 select_select_fusion
  109.6 0.7 select_select_fusion.1
  111.7 1.3 pad_add_fusion.2.range_ref
  113.1 1.3 pad_add_fusion.4.range_ref
  114.3 1.6 select_reduce_fusion
  116.0 2.7 pick.9
  118.7 1.3 collective-permute-start.18
  120.0 1.4 copy-done.1
  121.4 3.0 pick.7
  124.4 1.3 collective-permute-start.5
  125.7 11.5 %late.3 = (bf16[32,4,128,128]{3,2,1,0:T(8,128)(2,1)}, bf16[16,4,128,128]{3,2,1,0:T(8,128)(2,1)}, bf16[16,4,128,128]{3,2,1,0:T(8,128)(2,1)}) custom-call(s32[2]{0:T(128)} %pad_add_fusion.4.range_ref, s32[64]{0:T(128)} %get-tuple-element.71.blocks_ref, s32[64]{0:T(128)} %get-tuple-element.70.into_ref, s32[64]{0:T(128)} %get-tuple-element.69.side_ref, ...), custom_call_target="tpu_custom_call" | custom-call | flops 9663676416 | bytes 1572864 | tf_op jit(solution)/shard_map/late/pallas_call | solution.py:292
  137.2 14.3 %late.2 = (bf16[32,6,128,128]{3,2,1,0:T(8,128)(2,1)}, bf16[16,6,128,128]{3,2,1,0:T(8,128)(2,1)}, bf16[16,6,128,128]{3,2,1,0:T(8,128)(2,1)}) custom-call(s32[2]{0:T(128)} %pad_add_fusion.2.range_ref, s32[64]{0:T(128)} %get-tuple-element.72.blocks_ref, s32[64]{0:T(128)} %get-tuple-element.74.into_ref, s32[64]{0:T(128)} %get-tuple-element.73.side_ref, ...), custom_call_target="tpu_custom_call" | custom-call | flops 14495514624 | bytes 2359296 | tf_op jit(solution)/shard_map/late/pallas_call | solution.py:292
  151.6 26.9 %collective-permute-done.5.refs_1_ = bf16[2,6,256,256]{3,2,1,0:T(8,128)(2,1)S(1)} collective-permute-done((bf16[2,6,256,256]{3,2,1,0:T(8,128)(2,1)}, bf16[2,6,256,256]{3,2,1,0:T(8,128)(2,1)S(1)}, u32[]{:S(2)}, u32[]{:S(2)}) %collective-permute-start.5) | collective-permute-done | bytes 1572896 | tf_op jit(solution)/shard_map/ppermute | solution.py:22
  178.5 1.2 copy-done.12
  179.6 20.2 %late_seams.2 = (bf16[32,6,128,128]{3,2,1,0:T(8,128)(2,1)}, bf16[16,6,128,128]{3,2,1,0:T(8,128)(2,1)}, bf16[16,6,128,128]{3,2,1,0:T(8,128)(2,1)}) custom-call(s32[2]{0:T(128)} %pad_add_fusion.2.range_ref, s32[64]{0:T(128)} %get-tuple-element.72.blocks_ref, ...), custom_call_target="tpu_custom_call", output_to_operand_aliasing={{0}: (13, {}), {1}: (14, {}), {2}: (15, {})} | custom-call | flops 14495514624 | bytes 2359296 | tf_op jit(solution)/shard_map/late_seams/pallas_call | solution.py:292
  200.0 14.1 %late_seams.3 = (bf16[32,4,128,128]{3,2,1,0:T(8,128)(2,1)}, bf16[16,4,128,128]{3,2,1,0:T(8,128)(2,1)}, bf16[16,4,128,128]{3,2,1,0:T(8,128)(2,1)}) custom-call(s32[2]{0:T(128)} %pad_add_fusion.4.range_ref, s32[64]{0:T(128)} %get-tuple-element.71.blocks_ref, ...), custom_call_target="tpu_custom_call", output_to_operand_aliasing={{0}: (13, {}), {1}: (14, {}), {2}: (15, {})} | custom-call | flops 9663676416 | bytes 1572864 | tf_op jit(solution)/shard_map/late_seams/pallas_call | solution.py:292
  214.1 15.6 %collective-permute-start.19 = (bf16[16,4,128,128]{3,2,1,0:T(8,128)(2,1)}, bf16[16,4,128,128]{3,2,1,0:T(8,128)(2,1)}, u32[]{:S(2)}, u32[]{:S(2)}) collective-permute-start(bf16[16,4,128,128]{3,2,1,0:T(8,128)(2,1)} %get-tuple-element.59), channel_id=1, source_target_pairs={{0,2},{1,3},{2,4},{3,5},{4,6},{5,7},{6,0},{7,1},{8,10},{9,11},{10,... | collective-permute-start | bytes 6291464 | tf_op jit(solution)/shard_map/ppermute | solution.py:43
  229.7 8.5 %all-to-all-start = ((bf16[32,2,3,128,128]{4,3,2,1,0:T(8,128)(2,1)}), bf16[32,2,3,128,128]{4,3,2,1,0:T(8,128)(2,1)}, u32[]{:S(2)}, u32[]{:S(2)}) async-start(bf16[32,2,3,128,128]{4,3,2,1,0:T(8,128)(2,1)} %bitcast.10), calls=%async_computation | async-start | bytes 12582912 | tf_op jit(solution)/shard_map/all_to_all | solution.py:187
  238.2 79.6 %collective-permute-done.19.up_ref = bf16[16,4,128,128]{3,2,1,0:T(8,128)(2,1)} collective-permute-done((bf16[16,4,128,128]{3,2,1,0:T(8,128)(2,1)}, bf16[16,4,128,128]{3,2,1,0:T(8,128)(2,1)}, u32[]{:S(2)}, u32[]{:S(2)}) %collective-permute-start.19) | collective-permute-done | bytes 2097184 | tf_op jit(solution)/shard_map/ppermute | solution.py:43
  317.8 6.6 %pack.3 = (bf16[8,4,128,128]{3,2,1,0:T(8,128)(2,1)}, bf16[8,4,128,128]{3,2,1,0:T(8,128)(2,1)}, bf16[8,4,128,128]{3,2,1,0:T(8,128)(2,1)}, bf16[8,4,128,128]{3,2,1...) custom-call(bf16[32,4,128,128]{3,2,1,0:T(8,128)(2,1)} %get-tuple-ele, ...), custom_call_target="tpu_custom_call" | custom-call | tf_op jit(solution)/shard_map/pack/pallas_call | solution.py:335
  324.7 3.1 collective-permute-start.24
  327.8 9.5 %pack.2 = (bf16[8,6,128,128]{3,2,1,0:T(8,128)(2,1)}, bf16[8,6,128,128]{3,2,1,0:T(8,128)(2,1)}, bf16[8,6,128,128]{3,2,1,0:T(8,128)(2,1)}, bf16[8,6,128,128]{3,2,1...) custom-call(bf16[32,6,128,128]{3,2,1,0:T(8,128)(2,1)} %get-tuple-ele, ...), custom_call_target="tpu_custom_call" | custom-call | tf_op jit(solution)/shard_map/pack/pallas_call | solution.py:335
  337.5 3.9 collective-permute-start.9
  341.4 58.1 %collective-permute-done.22.refs_10_ = bf16[8,4,128,128]{3,2,1,0:T(8,128)(2,1)} collective-permute-done((bf16[8,4,128,128]{3,2,1,0:T(8,128)(2,1)}, bf16[8,4,128,128]{3,2,1,0:T(8,128)(2,1)}, u32[]{:S(2)}, u32[]{:S(2)}) %collective-permute-start.22) | collective-permute-done | bytes 1048608 | tf_op jit(solution)/shard_map/ppermute | solution.py:43
  399.5 24.2 %collective-permute-done.23.refs_11_ = bf16[8,4,128,128]{3,2,1,0:T(8,128)(2,1)} collective-permute-done((bf16[8,4,128,128]{3,2,1,0:T(8,128)(2,1)}, bf16[8,4,128,128]{3,2,1,0:T(8,128)(2,1)}, u32[]{:S(2)}, u32[]{:S(2)}) %collective-permute-start.23) | collective-permute-done | bytes 1048608 | tf_op jit(solution)/shard_map/ppermute | solution.py:43
  423.7 4.3 collective-permute-start.26
  428.1 23.8 %collective-permute-done.26.refs_14_ = bf16[8,4,128,128]{3,2,1,0:T(8,128)(2,1)S(1)} collective-permute-done((bf16[8,4,128,128]{3,2,1,0:T(8,128)(2,1)}, bf16[8,4,128,128]{3,2,1,0:T(8,128)(2,1)S(1)}, u32[]{:S(2)}, u32[]{:S(2)}) %collective-permute-start.26) | collective-permute-done | bytes 1048608 | tf_op jit(solution)/shard_map/ppermute | solution.py:43
  451.9 22.2 %collective-permute-done.27.refs_15_ = bf16[8,4,128,128]{3,2,1,0:T(8,128)(2,1)S(1)} collective-permute-done((bf16[8,4,128,128]{3,2,1,0:T(8,128)(2,1)}, bf16[8,4,128,128]{3,2,1,0:T(8,128)(2,1)S(1)}, u32[]{:S(2)}, u32[]{:S(2)}) %collective-permute-start.27) | collective-permute-done | bytes 1048608 | tf_op jit(solution)/shard_map/ppermute | solution.py:43
  474.2 0.8 copy-done.6
  475.1 3.3 collective-permute-start.14
  479.1 0.6 fusion.39
  479.7 0.5 add.474.x_lane_ref
  480.2 9.7 %collective-permute-done.11.refs_4_ = bf16[8,6,128,128]{3,2,1,0:T(8,128)(2,1)} collective-permute-done((bf16[8,6,128,128]{3,2,1,0:T(8,128)(2,1)}, bf16[8,6,128,128]{3,2,1,0:T(8,128)(2,1)}, u32[]{:S(2)}, u32[]{:S(2)}) %collective-permute-start.11) | collective-permute-done | bytes 1572896 | tf_op jit(solution)/shard_map/ppermute | solution.py:43
  489.9 35.9 %collective-permute-done.12.refs_5_ = bf16[8,6,128,128]{3,2,1,0:T(8,128)(2,1)} collective-permute-done((bf16[8,6,128,128]{3,2,1,0:T(8,128)(2,1)}, bf16[8,6,128,128]{3,2,1,0:T(8,128)(2,1)}, u32[]{:S(2)}, u32[]{:S(2)}) %collective-permute-start.12) | collective-permute-done | bytes 1572896 | tf_op jit(solution)/shard_map/ppermute | solution.py:43
  525.8 32.6 %collective-permute-done.13.refs_6_ = bf16[8,6,128,128]{3,2,1,0:T(8,128)(2,1)} collective-permute-done((bf16[8,6,128,128]{3,2,1,0:T(8,128)(2,1)}, bf16[8,6,128,128]{3,2,1,0:T(8,128)(2,1)}, u32[]{:S(2)}, u32[]{:S(2)}) %collective-permute-start.13) | collective-permute-done | bytes 1572896 | tf_op jit(solution)/shard_map/ppermute | solution.py:43
  558.5 33.5 %collective-permute-done.14.refs_7_ = bf16[8,6,128,128]{3,2,1,0:T(8,128)(2,1)} collective-permute-done((bf16[8,6,128,128]{3,2,1,0:T(8,128)(2,1)}, bf16[8,6,128,128]{3,2,1,0:T(8,128)(2,1)}, u32[]{:S(2)}, u32[]{:S(2)}) %collective-permute-start.14) | collective-permute-done | bytes 1572896 | tf_op jit(solution)/shard_map/ppermute | solution.py:43
  592.0 9.1 %place.1 = bf16[24,13,128,128]{3,2,1,0:T(8,128)(2,1)} custom-call(s32[24]{0:T(128)} %get-tuple-element.137.taken_ref, bf16[64,3,128,128]{3,2,1,0:T(8,128)(2,1)} %bitcast.4.early_ref, s32[24]{0:T(128)} %add.474.x_lane_ref, s32[24]{0:T(128)} %get-tuple-element.144.x_slot_ref, s32[24]{0:T(128)} %get-tuple-element.119.z_lane_ref, ...), custom_call_target="tpu_custom_call" | custom-call | tf_op jit(solution)/shard_map/place/pallas_call | solution.py:396
  (110 shorter events, 5.1 us)
Async XLA Ops:
  0.0 23.3 %collective-permute-start = (s32[2]{0:T(128)}, s32[2]{0:T(128)S(1)}, u32[]{:S(2)}, u32[]{:S(2)}) collective-permute-start(s32[2]{0:T(128)} %listed_ref.5), channel_id=1, source_target_pairs={{0,32},{32,64},{64,96},{1,33},{33,65},{65,97},{2,34},{34,66},{66,9... | collective-permute-start | bytes 32 | tf_op jit(solution)/shard_map/ppermute | solution.py:22
  3.9 79.2 %collective-permute-start.1 = (bf16[2,3,256,256]{3,2,1,0:T(8,128)(2,1)}, bf16[2,3,256,256]{3,2,1,0:T(8,128)(2,1)}, u32[]{:S(2)}, u32[]{:S(2)}) collective-permute-start(bf16[2,3,256,256]{3,2,1,0:T(8,128)(2,1)} %pick.5), channel_id=1, source_target_pairs={{0,32},{32,64},{64,96},{1,33},{33,65},{65,97},{2,34},{34,66},{66,9... | collective-permute-start | bytes 2359304 | tf_op jit(solution)/shard_map/ppermute | solution.py:22
  8.5 111.5 %collective-permute-start.3 = (bf16[3,6,256,256]{3,2,1,0:T(8,128)(2,1)}, bf16[3,6,256,256]{3,2,1,0:T(8,128)(2,1)S(1)}, u32[]{:S(2)}, u32[]{:S(2)}) collective-permute-start(bf16[3,6,256,256]{3,2,1,0:T(8,128)(2,1)} %slice.33), channel_id=1, source_target_pairs={{0,8},{1,9},{2,10},{3,11},{4,12},{5,13},{6,14},{7,15},{8,16},{9,17... | collective-permute-start | bytes 7077896 | tf_op jit(solution)/shard_map/ppermute | solution.py:43
  12.6 6.0 copy-start.7
  12.7 138.9 %collective-permute-start.4 = (bf16[2,6,256,256]{3,2,1,0:T(8,128)(2,1)}, bf16[2,6,256,256]{3,2,1,0:T(8,128)(2,1)}, u32[]{:S(2)}, u32[]{:S(2)}) collective-permute-start(bf16[2,6,256,256]{3,2,1,0:T(8,128)(2,1)} %pick.6), channel_id=1, source_target_pairs={{0,32},{32,64},{64,96},{1,33},{33,65},{65,97},{2,34},{34,66},{66,9... | collective-permute-start | bytes 4718600 | tf_op jit(solution)/shard_map/ppermute | solution.py:22
  16.6 99.3 %collective-permute-start.16 = (bf16[3,4,256,256]{3,2,1,0:T(8,128)(2,1)}, bf16[3,4,256,256]{3,2,1,0:T(8,128)(2,1)}, u32[]{:S(2)}, u32[]{:S(2)}) collective-permute-start(bf16[3,4,256,256]{3,2,1,0:T(8,128)(2,1)} %slice.36), channel_id=1, source_target_pairs={{0,2},{1,3},{2,4},{3,5},{4,6},{5,7},{6,0},{7,1},{8,10},{9,11},{10,... | collective-permute-start | bytes 4718600 | tf_op jit(solution)/shard_map/ppermute | solution.py:43
  18.8 3.3 copy-start.9
  18.8 4.3 copy-start.8
  18.8 4.5 copy-start.10
  23.3 46.7 %copy-start.13 = (f32[6144]{0:T(1024)}, f32[6144]{0:T(1024)S(1)}, u32[]{:S(2)}) copy-start(f32[6144]{0:T(1024)S(1)} %fusion.28.taps_ref) | copy-start | bytes 73732
  23.4 46.7 %copy-start.11 = (s32[2]{0:T(128)}, s32[2]{0:T(128)S(1)}, u32[]{:S(2)}) copy-start(s32[2]{0:T(128)S(1)} %collective-permute-done.listed_ref) | copy-start | bytes 28
  23.4 29.4 %collective-permute-start.15 = (s32[4]{0:T(128)S(1)}, s32[4]{0:T(128)S(1)}, u32[]{:S(2)}, u32[]{:S(2)}) collective-permute-start(s32[4]{0:T(128)S(1)} %pad_add_fusion.1), channel_id=1, source_target_pairs={{0,2},{1,3},{2,4},{3,5},{4,6},{5,7},{6,0},{7,1},{8,10},{9,11},{10,... | collective-permute-start | bytes 56 | tf_op jit(solution)/shard_map/ppermute | solution.py:43
  52.8 8.9 %collective-permute-start.2 = (s32[4]{0:T(128)S(1)}, s32[4]{0:T(128)S(1)}, u32[]{:S(2)}, u32[]{:S(2)}) collective-permute-start(s32[4]{0:T(128)S(1)} %pad_add_fusion.1), channel_id=1, source_target_pairs={{0,8},{1,9},{2,10},{3,11},{4,12},{5,13},{6,14},{7,15},{8,16},{9,17... | collective-permute-start | bytes 56 | tf_op jit(solution)/shard_map/ppermute | solution.py:43
  61.7 138.2 %collective-permute-start.17 = (bf16[2,4,256,256]{3,2,1,0:T(8,128)(2,1)}, bf16[2,4,256,256]{3,2,1,0:T(8,128)(2,1)}, u32[]{:S(2)}, u32[]{:S(2)}) collective-permute-start(bf16[2,4,256,256]{3,2,1,0:T(8,128)(2,1)} %pick.8), channel_id=1, source_target_pairs={{0,32},{32,64},{64,96},{1,33},{33,65},{65,97},{2,34},{34,66},{66,9... | collective-permute-start | bytes 3145736 | tf_op jit(solution)/shard_map/ppermute | solution.py:22
  118.7 81.3 %collective-permute-start.18 = (bf16[2,4,256,256]{3,2,1,0:T(8,128)(2,1)}, bf16[2,4,256,256]{3,2,1,0:T(8,128)(2,1)}, u32[]{:S(2)}, u32[]{:S(2)}) collective-permute-start(bf16[2,4,256,256]{3,2,1,0:T(8,128)(2,1)} %pick.9), channel_id=1, source_target_pairs={{0,32},{32,64},{64,96},{1,33},{33,65},{65,97},{2,34},{34,66},{66,9... | collective-permute-start | bytes 3145736 | tf_op jit(solution)/shard_map/ppermute | solution.py:22
  120.0 1.4 copy-start.1
  124.4 54.1 %collective-permute-start.5 = (bf16[2,6,256,256]{3,2,1,0:T(8,128)(2,1)}, bf16[2,6,256,256]{3,2,1,0:T(8,128)(2,1)S(1)}, u32[]{:S(2)}, u32[]{:S(2)}) collective-permute-start(bf16[2,6,256,256]{3,2,1,0:T(8,128)(2,1)} %pick.7), channel_id=1, source_target_pairs={{0,32},{32,64},{64,96},{1,33},{33,65},{65,97},{2,34},{34,66},{66,9... | collective-permute-start | bytes 4718600 | tf_op jit(solution)/shard_map/ppermute | solution.py:22
  178.5 1.2 copy-start.12
  199.9 124.8 %collective-permute-start.6 = (bf16[16,6,128,128]{3,2,1,0:T(8,128)(2,1)}, bf16[16,6,128,128]{3,2,1,0:T(8,128)(2,1)S(1)}, u32[]{:S(2)}, u32[]{:S(2)}) collective-permute-start(bf16[16,6,128,128]{3,2,1,0:T(8,128)(2,1)} %get-tuple-element.45), channel_id=1, source_target_pairs={{0,8},{1,9},{2,10},{3,11},{4,12},{5,13},{6,14},{7,15},{8,16},{9,17... | collective-permute-start | bytes 9437192 | tf_op jit(solution)/shard_map/ppermute | solution.py:43
  214.1 103.7 %collective-permute-start.19 = (bf16[16,4,128,128]{3,2,1,0:T(8,128)(2,1)}, bf16[16,4,128,128]{3,2,1,0:T(8,128)(2,1)}, u32[]{:S(2)}, u32[]{:S(2)}) collective-permute-start(bf16[16,4,128,128]{3,2,1,0:T(8,128)(2,1)} %get-tuple-element.59), channel_id=1, source_target_pairs={{0,2},{1,3},{2,4},{3,5},{4,6},{5,7},{6,0},{7,1},{8,10},{9,11},{10,... | collective-permute-start | bytes 6291464 | tf_op jit(solution)/shard_map/ppermute | solution.py:43
  229.7 98.2 %collective-permute-start.7 = (bf16[16,6,128,128]{3,2,1,0:T(8,128)(2,1)}, bf16[16,6,128,128]{3,2,1,0:T(8,128)(2,1)}, u32[]{:S(2)}, u32[]{:S(2)}) collective-permute-start(bf16[16,6,128,128]{3,2,1,0:T(8,128)(2,1)} %get-tuple-element.46), channel_id=1, source_target_pairs={{0,24},{1,25},{2,26},{3,27},{4,28},{5,29},{6,30},{7,31},{8,0},{9,1... | collective-permute-start | bytes 9437192 | tf_op jit(solution)/shard_map/ppermute | solution.py:43
  229.7 88.1 %collective-permute-start.20 = (bf16[16,4,128,128]{3,2,1,0:T(8,128)(2,1)}, bf16[16,4,128,128]{3,2,1,0:T(8,128)(2,1)}, u32[]{:S(2)}, u32[]{:S(2)}) collective-permute-start(bf16[16,4,128,128]{3,2,1,0:T(8,128)(2,1)} %get-tuple-element.60), channel_id=1, source_target_pairs={{0,6},{1,7},{2,0},{3,1},{4,2},{5,3},{6,4},{7,5},{8,14},{9,15},{10,... | collective-permute-start | bytes 6291464 | tf_op jit(solution)/shard_map/ppermute | solution.py:43
  229.7 250.5 %all-to-all-start = ((bf16[32,2,3,128,128]{4,3,2,1,0:T(8,128)(2,1)}), bf16[32,2,3,128,128]{4,3,2,1,0:T(8,128)(2,1)}, u32[]{:S(2)}, u32[]{:S(2)}) async-start(bf16[32,2,3,128,128]{4,3,2,1,0:T(8,128)(2,1)} %bitcast.10), calls=%async_computation | async-start | bytes 12582912 | tf_op jit(solution)/shard_map/all_to_all | solution.py:187
  324.4 13.1 %collective-permute-start.21 = (bf16[8,4,128,128]{3,2,1,0:T(8,128)(2,1)}, bf16[8,4,128,128]{3,2,1,0:T(8,128)(2,1)}, u32[]{:S(2)}, u32[]{:S(2)}) collective-permute-start(bf16[8,4,128,128]{3,2,1,0:T(8,128)(2,1)} %get-tuple-element.62), channel_id=1, source_target_pairs={{0,1},{1,0},{2,3},{3,2},{4,5},{5,4},{6,7},{7,6},{8,9},{9,8},{10,11... | collective-permute-start | bytes 3145736 | tf_op jit(solution)/shard_map/ppermute | solution.py:43
  324.5 75.0 %collective-permute-start.22 = (bf16[8,4,128,128]{3,2,1,0:T(8,128)(2,1)}, bf16[8,4,128,128]{3,2,1,0:T(8,128)(2,1)}, u32[]{:S(2)}, u32[]{:S(2)}) collective-permute-start(bf16[8,4,128,128]{3,2,1,0:T(8,128)(2,1)} %get-tuple-element.63), channel_id=1, source_target_pairs={{0,8},{1,9},{2,10},{3,11},{4,12},{5,13},{6,14},{7,15},{8,16},{9,17... | collective-permute-start | bytes 3145736 | tf_op jit(solution)/shard_map/ppermute | solution.py:43
  324.6 99.1 %collective-permute-start.23 = (bf16[8,4,128,128]{3,2,1,0:T(8,128)(2,1)}, bf16[8,4,128,128]{3,2,1,0:T(8,128)(2,1)}, u32[]{:S(2)}, u32[]{:S(2)}) collective-permute-start(bf16[8,4,128,128]{3,2,1,0:T(8,128)(2,1)} %get-tuple-element.64), channel_id=1, source_target_pairs={{0,9},{1,8},{2,11},{3,10},{4,13},{5,12},{6,15},{7,14},{8,17},{9,16... | collective-permute-start | bytes 3145736 | tf_op jit(solution)/shard_map/ppermute | solution.py:43
  324.7 3.1 copy-start
  324.7 103.3 %collective-permute-start.24 = (bf16[8,4,128,128]{3,2,1,0:T(8,128)(2,1)}, bf16[8,4,128,128]{3,2,1,0:T(8,128)(2,1)}, u32[]{:S(2)}, u32[]{:S(2)}) collective-permute-start(bf16[8,4,128,128]{3,2,1,0:T(8,128)(2,1)} %get-tuple-element.65), channel_id=1, source_target_pairs={{0,16},{1,17},{2,18},{3,19},{4,20},{5,21},{6,22},{7,23},{8,24},{9,... | collective-permute-start | bytes 3145736 | tf_op jit(solution)/shard_map/ppermute | solution.py:43
  337.3 136.8 %collective-permute-start.8 = (bf16[8,6,128,128]{3,2,1,0:T(8,128)(2,1)}, bf16[8,6,128,128]{3,2,1,0:T(8,128)(2,1)S(1)}, u32[]{:S(2)}, u32[]{:S(2)}) collective-permute-start(bf16[8,6,128,128]{3,2,1,0:T(8,128)(2,1)} %get-tuple-element.48), channel_id=1, source_target_pairs={{0,1},{1,0},{2,3},{3,2},{4,5},{5,4},{6,7},{7,6},{8,9},{9,8},{10,11... | collective-permute-start | bytes 4718600 | tf_op jit(solution)/shard_map/ppermute | solution.py:43
  337.5 136.7 %collective-permute-start.9 = (bf16[8,6,128,128]{3,2,1,0:T(8,128)(2,1)}, bf16[8,6,128,128]{3,2,1,0:T(8,128)(2,1)S(1)}, u32[]{:S(2)}, u32[]{:S(2)}) collective-permute-start(bf16[8,6,128,128]{3,2,1,0:T(8,128)(2,1)} %get-tuple-element.49), channel_id=1, source_target_pairs={{0,2},{1,3},{2,4},{3,5},{4,6},{5,7},{6,0},{7,1},{8,10},{9,11},{10,... | collective-permute-start | bytes 4718600 | tf_op jit(solution)/shard_map/ppermute | solution.py:43
  399.5 28.5 %collective-permute-start.25 = (bf16[8,4,128,128]{3,2,1,0:T(8,128)(2,1)}, bf16[8,4,128,128]{3,2,1,0:T(8,128)(2,1)S(1)}, u32[]{:S(2)}, u32[]{:S(2)}) collective-permute-start(bf16[8,4,128,128]{3,2,1,0:T(8,128)(2,1)} %get-tuple-element.66), channel_id=1, source_target_pairs={{0,17},{1,16},{2,19},{3,18},{4,21},{5,20},{6,23},{7,22},{8,25},{9,... | collective-permute-start | bytes 3145736 | tf_op jit(solution)/shard_map/ppermute | solution.py:43
  423.7 28.2 %collective-permute-start.26 = (bf16[8,4,128,128]{3,2,1,0:T(8,128)(2,1)}, bf16[8,4,128,128]{3,2,1,0:T(8,128)(2,1)S(1)}, u32[]{:S(2)}, u32[]{:S(2)}) collective-permute-start(bf16[8,4,128,128]{3,2,1,0:T(8,128)(2,1)} %get-tuple-element.67), channel_id=1, source_target_pairs={{0,24},{1,25},{2,26},{3,27},{4,28},{5,29},{6,30},{7,31},{8,0},{9,1... | collective-permute-start | bytes 3145736 | tf_op jit(solution)/shard_map/ppermute | solution.py:43
  428.0 46.1 %collective-permute-start.27 = (bf16[8,4,128,128]{3,2,1,0:T(8,128)(2,1)}, bf16[8,4,128,128]{3,2,1,0:T(8,128)(2,1)S(1)}, u32[]{:S(2)}, u32[]{:S(2)}) collective-permute-start(bf16[8,4,128,128]{3,2,1,0:T(8,128)(2,1)} %get-tuple-element.68), channel_id=1, source_target_pairs={{0,25},{1,24},{2,27},{3,26},{4,29},{5,28},{6,31},{7,30},{8,1},{9,0... | collective-permute-start | bytes 3145736 | tf_op jit(solution)/shard_map/ppermute | solution.py:43
  428.0 46.2 %copy-start.4 = (bf16[8,4,128,128]{3,2,1,0:T(8,128)(2,1)}, bf16[8,4,128,128]{3,2,1,0:T(8,128)(2,1)S(1)}, u32[]{:S(2)}) copy-start(bf16[8,4,128,128]{3,2,1,0:T(8,128)(2,1)S(1)} %collective-permute-done.25.refs_13_) | copy-start | bytes 3145732
  428.0 52.2 %collective-permute-start.10 = (bf16[8,6,128,128]{3,2,1,0:T(8,128)(2,1)}, bf16[8,6,128,128]{3,2,1,0:T(8,128)(2,1)}, u32[]{:S(2)}, u32[]{:S(2)}) collective-permute-start(bf16[8,6,128,128]{3,2,1,0:T(8,128)(2,1)} %get-tuple-element.50), channel_id=1, source_target_pairs={{0,3},{1,2},{2,5},{3,4},{4,7},{5,6},{6,1},{7,0},{8,11},{9,10},{10,... | collective-permute-start | bytes 4718600 | tf_op jit(solution)/shard_map/ppermute | solution.py:43
  451.9 22.4 %copy-start.5 = (bf16[8,4,128,128]{3,2,1,0:T(8,128)(2,1)}, bf16[8,4,128,128]{3,2,1,0:T(8,128)(2,1)S(1)}, u32[]{:S(2)}) copy-start(bf16[8,4,128,128]{3,2,1,0:T(8,128)(2,1)S(1)} %collective-permute-done.26.refs_14_) | copy-start | bytes 3145732
  451.9 38.1 %collective-permute-start.11 = (bf16[8,6,128,128]{3,2,1,0:T(8,128)(2,1)}, bf16[8,6,128,128]{3,2,1,0:T(8,128)(2,1)}, u32[]{:S(2)}, u32[]{:S(2)}) collective-permute-start(bf16[8,6,128,128]{3,2,1,0:T(8,128)(2,1)} %get-tuple-element.51), channel_id=1, source_target_pairs={{0,4},{1,5},{2,6},{3,7},{4,0},{5,1},{6,2},{7,3},{8,12},{9,13},{10,... | collective-permute-start | bytes 4718600 | tf_op jit(solution)/shard_map/ppermute | solution.py:43
  474.1 1.0 copy-start.6
  474.1 51.7 %collective-permute-start.12 = (bf16[8,6,128,128]{3,2,1,0:T(8,128)(2,1)}, bf16[8,6,128,128]{3,2,1,0:T(8,128)(2,1)}, u32[]{:S(2)}, u32[]{:S(2)}) collective-permute-start(bf16[8,6,128,128]{3,2,1,0:T(8,128)(2,1)} %get-tuple-element.52), channel_id=1, source_target_pairs={{0,5},{1,4},{2,7},{3,6},{4,1},{5,0},{6,3},{7,2},{8,13},{9,12},{10,... | collective-permute-start | bytes 4718600 | tf_op jit(solution)/shard_map/ppermute | solution.py:43
  474.1 117.9 %copy-start.2 = (bf16[8,6,128,128]{3,2,1,0:T(8,128)(2,1)}, bf16[8,6,128,128]{3,2,1,0:T(8,128)(2,1)S(1)}, u32[]{:S(2)}) copy-start(bf16[8,6,128,128]{3,2,1,0:T(8,128)(2,1)S(1)} %collective-permute-done.8.refs_1_) | copy-start | bytes 4718596
  474.1 84.3 %collective-permute-start.13 = (bf16[8,6,128,128]{3,2,1,0:T(8,128)(2,1)}, bf16[8,6,128,128]{3,2,1,0:T(8,128)(2,1)}, u32[]{:S(2)}, u32[]{:S(2)}) collective-permute-start(bf16[8,6,128,128]{3,2,1,0:T(8,128)(2,1)} %get-tuple-element.53), channel_id=1, source_target_pairs={{0,6},{1,7},{2,0},{3,1},{4,2},{5,3},{6,4},{7,5},{8,14},{9,15},{10,... | collective-permute-start | bytes 4718600 | tf_op jit(solution)/shard_map/ppermute | solution.py:43
  474.2 117.7 %copy-start.3 = (bf16[8,6,128,128]{3,2,1,0:T(8,128)(2,1)}, bf16[8,6,128,128]{3,2,1,0:T(8,128)(2,1)S(1)}, u32[]{:S(2)}) copy-start(bf16[8,6,128,128]{3,2,1,0:T(8,128)(2,1)S(1)} %collective-permute-done.9.refs_2_) | copy-start | bytes 4718596
  475.1 116.9 %collective-permute-start.14 = (bf16[8,6,128,128]{3,2,1,0:T(8,128)(2,1)}, bf16[8,6,128,128]{3,2,1,0:T(8,128)(2,1)}, u32[]{:S(2)}, u32[]{:S(2)}) collective-permute-start(bf16[8,6,128,128]{3,2,1,0:T(8,128)(2,1)} %get-tuple-element.54), channel_id=1, source_target_pairs={{0,7},{1,6},{2,1},{3,0},{4,3},{5,2},{6,5},{7,4},{8,15},{9,14},{10,... | collective-permute-start | bytes 4718600 | tf_op jit(solution)/shard_map/ppermute | solution.py:43

commit v8 on v3

--- a/solution.py
+++ b/solution.py
@@ -9,7 +9,7 @@
 
 
 EARLY = 3
-PLACE_VMEM = 16 * 1024 * 1024
+PLACE_VMEM = 8 * 1024 * 1024
 ABREAST = 4
 STEPS = (-1, 0, 1, 2)
 
@@ -59,7 +59,7 @@
 
 
 def render_kernel(
-    local_count, first, bands, seams, range_ref, blocks_ref, slots_ref, source_ref, offsets_ref, taps_ref, blend_ref,
+    local_count, first, bands, seams, abreast, range_ref, blocks_ref, slots_ref, source_ref, offsets_ref, taps_ref, blend_ref,
     listed_ref, tiles_ref, *refs,
 ):
     if seams:
@@ -80,7 +80,7 @@
         load_near.wait()
 
     def store(index):
-        way = lax.rem(index - start, 2 * ABREAST)
+        way = lax.rem(index - start, 2 * abreast)
         return pltpu.make_async_copy(done.at[way], out_ref.at[slots_ref[index]], out_sem.at[way])
 
     def kernel_matrix(lag_ref, block, axis):
@@ -108,19 +108,19 @@
         return jnp.dot(row_kernel, beside_each, preferred_element_type=jnp.float32).astype(jnp.bfloat16)
 
     def some(turn, carry):
-        begin = start + turn * ABREAST
-        for ahead in range(ABREAST):
+        begin = start + turn * abreast
+        for ahead in range(abreast):
 
             @pl.when(turn >= 2)
             def _():
-                store(begin + ahead - 2 * ABREAST).wait()
-
-        results = [render_one(jnp.minimum(begin + ahead, stop - 1)) for ahead in range(ABREAST)]
-        for ahead in range(ABREAST):
-            way = lax.rem(turn, 2) * ABREAST + ahead
+                store(begin + ahead - 2 * abreast).wait()
+
+        results = [render_one(jnp.minimum(begin + ahead, stop - 1)) for ahead in range(abreast)]
+        for ahead in range(abreast):
+            way = lax.rem(turn, 2) * abreast + ahead
             for b in range(bands):
                 done[way, b] = results[ahead][:, b * (width // 2) : (b + 1) * (width // 2)]
-        for ahead in range(ABREAST):
+        for ahead in range(abreast):
 
             @pl.when(begin + ahead < stop)
             def _():
@@ -128,24 +128,25 @@
 
         return carry
 
-    turns = lax.div(stop - start + ABREAST - 1, ABREAST)
+    turns = lax.div(stop - start + abreast - 1, abreast)
     lax.fori_loop(0, turns, some, 0)
 
     def drain(index, carry):
         store(index).wait()
         return carry
 
-    lax.fori_loop(start + jnp.maximum(turns - 2, 0) * ABREAST, stop, drain, 0)
+    lax.fori_loop(start + jnp.maximum(turns - 2, 0) * abreast, stop, drain, 0)
 
 
 def render(scalars, tiles, first, bands, slots, near=None, begun=None):
     local_count, _, height, width = tiles.shape
     block = (bands, height // 2, width // 2)
     seams = near is not None
+    abreast = ABREAST
     arrays = (tiles, near, begun) if seams else (tiles,)
     flops = 12 * bands * (2 * height * width * width // 2 + height * width * height // 2)
     return pl.pallas_call(
-        functools.partial(render_kernel, local_count, first, bands, seams),
+        functools.partial(render_kernel, local_count, first, bands, seams, abreast),
         out_shape=jax.ShapeDtypeStruct((slots,) + block, jnp.bfloat16),
         in_specs=[pl.BlockSpec(memory_space=pltpu.SMEM)] * len(scalars)
         + [pl.BlockSpec(memory_space=pl.ANY)] * len(arrays),
@@ -155,9 +156,9 @@
         + [
             pltpu.VMEM((height // 2, height), jnp.int32),
             pltpu.VMEM((width, width // 2), jnp.int32),
-            pltpu.VMEM((2 * ABREAST,) + block, jnp.bfloat16),
+            pltpu.VMEM((2 * abreast,) + block, jnp.bfloat16),
             pltpu.SemaphoreType.DMA((2,)),
-            pltpu.SemaphoreType.DMA((2 * ABREAST,)),
+            pltpu.SemaphoreType.DMA((2 * abreast,)),
         ],
         input_output_aliases={len(scalars) + 2: 0} if seams else {},
         cost_estimate=pl.CostEstimate(flops=8 * flops, bytes_accessed=12 * bands * height * width // 2, transcendentals=0),
@@ -170,27 +171,26 @@
     early, late = early_ref.shape[1], late_ref.shape[1]
 
     def take(index):
+        return pltpu.make_async_copy(early_ref.at[taken_ref[index]], held.at[index], early_sem.at[index])
+
+    def put(index):
+        return pltpu.make_async_copy(held.at[index], out_ref.at[index, pl.ds(0, early)], out_sem.at[index])
+
+    def put_late(index):
         return pltpu.make_async_copy(
-            early_ref.at[taken_ref[index]], held.at[index, pl.ds(0, early)], early_sem.at[index]
+            late_ref.at[taken_ref[index]], out_ref.at[index, pl.ds(early, late)], late_sem.at[index]
         )
 
-    def take_late(index):
-        return pltpu.make_async_copy(
-            late_ref.at[taken_ref[index]], held.at[index, pl.ds(early, late)], late_sem.at[index]
-        )
-
-    def put(index):
-        return pltpu.make_async_copy(held.at[index], out_ref.at[index], out_sem.at[index])
-
     for index in range(count):
         take(index).start()
-        take_late(index).start()
+    for index in range(count):
+        put_late(index).start()
     for index in range(count):
         take(index).wait()
-        take_late(index).wait()
         put(index).start()
     for index in range(count):
         put(index).wait()
+        put_late(index).wait()
 
 
 def place(taken, early, late, count):
@@ -201,7 +201,7 @@
         in_specs=[pl.BlockSpec(memory_space=pltpu.SMEM)] + [pl.BlockSpec(memory_space=pl.ANY)] * 2,
         out_specs=pl.BlockSpec(memory_space=pl.ANY),
         scratch_shapes=[
-            pltpu.VMEM(shape, jnp.bfloat16),
+            pltpu.VMEM((count,) + early.shape[1:], jnp.bfloat16),
             pltpu.SemaphoreType.DMA((count,)),
             pltpu.SemaphoreType.DMA((count,)),
             pltpu.SemaphoreType.DMA((count,)),
@@ -254,7 +254,7 @@
     slot_ids = owner_ids[:, None] * capacity + plain_rank + seam_rank
     blocks = jnp.sum(jnp.where(hit, block_ids[None], 0), axis=(1, 2))
     into = jnp.sum(jnp.where(hit, slot_ids[None], 0), axis=(1, 2))
-    ranges = jnp.stack([plain_count, plain_count + seam_count])
+    ranges = plain_count + jnp.arange(2, dtype=jnp.int32) * seam_count
 
     own = lax.dynamic_index_in_dim(src_device, myself, 0, keepdims=False)
     own_rank = jnp.sum(((own[:, None] == own[None, :]) & earlier).astype(jnp.int32), axis=1)

time: 423 us -> 420 us (level)
  transfers between devices with their start and end apart: 4 -> 4, of which waited for: 1 -> 1; matrix products, arithmetic and copies ran while one was open for 2% -> 2% of each run, Pallas kernels for 21% -> 22%
where the time goes in v8:
time: 420 us; the launch traced here: 413 us
  blocking collectives  237 us (56%)
  Pallas kernels  116 us (28%)
  waiting for transfers between devices  35.8 us (9%)
  starting transfers between devices  11.4 us (3%)
  other arithmetic  7.33 us (2%)
  local copies, waits for them, and re-layouts  4.74 us (1%)
    all_to_all x1, blocking collectives, swap(): lax.all_to_all(pairs, 'tile', split_axis=0, concat_axis=0, tiled=True)  237 us
    pallas_call x4, Pallas kernels, render(): pl.pallas_call(functools.partial(render_kernel, local_count, first, bands...  105 us
    ppermute x3, waiting for transfers between devices, passed_along(): lax.ppermute(value, axis, [(source, source + steps) for source in range(i...  35.8 us
  transfers between devices with their start and end apart: 4, of which 1 were waited for; matrix products, arithmetic and copies ran while one was open for 2% of the time, Pallas kernels for 22%

profile of v8, /device:TPU:60, one launch (start us, length us, event | category | flops | bytes accessed | tf_op | source)
XLA Modules:
  0.0 413.0 jit_solution(6603865305671374799)
XLA Ops:
  0.0 1.3 collective-permute-start
  1.3 2.6 pick.3
  3.9 1.3 collective-permute-start.2
  5.2 0.7 add_select_fusion
  5.9 0.7 broadcast_compare_fusion.1
  6.6 0.1 reshape.167
  6.7 0.1 copy.12
  6.8 0.1 eq.68
  6.9 0.1 copy.10
  6.9 0.1 iota_add_fusion
  7.0 0.8 abs_reduce_fusion
  7.9 0.9 copy.15
  8.7 0.8 reshape.168.offsets_ref
  9.7 0.0 copy-start.3
  9.7 0.0 collective-permute-done.listed_ref
  9.7 0.0 copy-start
  9.7 0.1 compare_reduce_fusion
  9.8 0.1 copy.11
  10.0 0.1 reduce_or.12
  10.1 0.2 convert_reduce_fusion.1
  10.3 0.1 select_reduce_fusion.2
  10.4 0.7 convert_reduce_fusion.6
  11.1 0.7 select_select_fusion
  11.7 0.1 copy.13
  11.8 0.1 copy.14
  11.9 1.1 select_reduce_fusion
  12.9 1.8 multiply_add_fusion.1.range_ref
  14.8 0.0 copy-done.3
  14.8 0.0 copy-done
  14.8 13.0 %render.3.refs_1_ = bf16[64,3,128,128]{3,2,1,0:T(8,128)(2,1)} custom-call(s32[2]{0:T(128)} %multiply_add_fusion.1.range_ref, s32[64]{0:T(128)} %get-tuple-element.10.blocks_ref, s32[64]{0:T(128)} %get-tuple-element.9.slots_ref, s32[768]{0:T(1024)} %source_ref.7, s32[1536]{0:T(1024)} %reshape.168.offsets_ref, f32[6144]{0:T(1024)} %copy-done.3, ...), custom_call_target="tpu_custom_call" | custom-call | flops 7247757312 | bytes 1179648 | tf_op jit(solution)/shard_map/render/pallas_call | solution.py:148
  27.8 0.0 collective-permute-done.2.refs_0_
  27.8 0.0 copy-start.2
  27.8 0.9 copy-done.2
  28.7 21.3 %seams.3 = bf16[64,3,128,128]{3,2,1,0:T(8,128)(2,1)} custom-call(s32[2]{0:T(128)} %multiply_add_fusion.1.range_ref, s32[64]{0:T(128)} %get-tuple-element.10.blocks_ref, s32[64]{0:T(128)} %get-tuple-element.9.slots_ref, s32[768]{0:T(1024)} %source_ref.7, s32[1536]{0:T(1024)} %reshape.168.offsets_ref, ...), custom_call_target="tpu_custom_call", output_to_operand_aliasing={{}: (10, {})} | custom-call | flops 7247757312 | bytes 1179648 | tf_op jit(solution)/shard_map/seams/pallas_call | solution.py:148
  50.0 7.5 %all-to-all-start = ((bf16[32,2,3,128,128]{4,3,2,1,0:T(8,128)(2,1)}), bf16[32,2,3,128,128]{4,3,2,1,0:T(8,128)(2,1)}, u32[]{:S(2)}, u32[]{:S(2)}) async-start(bf16[32,2,3,128,128]{4,3,2,1,0:T(8,128)(2,1)} %bitcast.10), calls=%async_computation | async-start | bytes 12582912 | tf_op jit(solution)/shard_map/all_to_all | solution.py:217
  57.5 3.5 pick.2
  61.0 1.3 collective-permute-start.1
  62.3 0.2 convert_reduce_fusion.2
  62.5 25.6 %render.2.refs_1_ = bf16[64,10,128,128]{3,2,1,0:T(8,128)(2,1)} custom-call(s32[2]{0:T(128)} %multiply_add_fusion.1.range_ref, s32[64]{0:T(128)} %get-tuple-element.10.blocks_ref, s32[64]{0:T(128)} %get-tuple-element.9.slots_ref, s32[768]{0:T(1024)} %source_ref.7, s32[1536]{0:T(1024)} %reshape.168.offsets_ref, f32[6144]{0:T(1024)} %copy-done.3, ...), custom_call_target="tpu_custom_call" | custom-call | flops 24159191040 | bytes 3932160 | tf_op jit(solution)/shard_map/render/pallas_call | solution.py:148
  88.2 35.8 %collective-permute-done.1.refs_0_ = bf16[2,10,256,256]{3,2,1,0:T(8,128)(2,1)S(1)} collective-permute-done((bf16[2,10,256,256]{3,2,1,0:T(8,128)(2,1)}, bf16[2,10,256,256]{3,2,1,0:T(8,128)(2,1)S(1)}, u32[]{:S(2)}, u32[]{:S(2)}) %collective-permute-start.1) | collective-permute-done | bytes 2621472 | tf_op jit(solution)/shard_map/ppermute | solution.py:20
  124.0 0.0 copy-start.1
  124.0 1.5 copy-done.1
  125.5 44.6 %seams.2 = bf16[64,10,128,128]{3,2,1,0:T(8,128)(2,1)} custom-call(s32[2]{0:T(128)} %multiply_add_fusion.1.range_ref, s32[64]{0:T(128)} %get-tuple-element.10.blocks_ref, s32[64]{0:T(128)} %get-tuple-element.9.slots_ref, s32[768]{0:T(1024)} %source_ref.7, s32[1536]{0:T(1024)} %reshape.168.offsets_ref, ...), custom_call_target="tpu_custom_call", output_to_operand_aliasing={{}: (10, {})} | custom-call | flops 24159191040 | bytes 3932160 | tf_op jit(solution)/shard_map/seams/pallas_call | solution.py:148
  170.0 0.0 all-to-all-done
  170.1 237.5 %all_to_all.10 = bf16[32,2,10,128,128]{4,3,2,1,0:T(8,128)(2,1)S(1)} all-to-all(bf16[32,2,10,128,128]{4,3,2,1,0:T(8,128)(2,1)} %bitcast.9), channel_id=1, replica_groups=mesh['zone'=4,'tile'=32] {'tile'}, dimensions={0} | all-to-all | bytes 41943040 | tf_op jit(solution)/shard_map/all_to_all | solution.py:217
  407.6 5.5 %place.1 = bf16[24,13,128,128]{3,2,1,0:T(8,128)(2,1)} custom-call(s32[24]{0:T(128)S(1)} %multiply_add_fusion.taken_ref, bf16[64,3,128,128]{3,2,1,0:T(8,128)(2,1)} %bitcast.2.early_ref, bf16[64,10,128,128]{3,2,1,0:T(8,128)(2,1)S(1)} %bitcast.8), custom_call_target="tpu_custom_call" | custom-call | tf_op jit(solution)/shard_map/place/pallas_call | solution.py:198
  (16 shorter events, 0.2 us)
Async XLA Ops:
  0.0 9.7 %collective-permute-start = (s32[2]{0:T(128)}, s32[2]{0:T(128)S(1)}, u32[]{:S(2)}, u32[]{:S(2)}) collective-permute-start(s32[2]{0:T(128)} %listed_ref.3), channel_id=1, source_target_pairs={{0,32},{32,64},{64,96},{1,33},{33,65},{65,97},{2,34},{34,66},{66,9... | collective-permute-start | bytes 32 | tf_op jit(solution)/shard_map/ppermute | solution.py:20
  3.9 23.9 %collective-permute-start.2 = (bf16[2,3,256,256]{3,2,1,0:T(8,128)(2,1)}, bf16[2,3,256,256]{3,2,1,0:T(8,128)(2,1)S(1)}, u32[]{:S(2)}, u32[]{:S(2)}) collective-permute-start(bf16[2,3,256,256]{3,2,1,0:T(8,128)(2,1)} %pick.3), channel_id=1, source_target_pairs={{0,32},{32,64},{64,96},{1,33},{33,65},{65,97},{2,34},{34,66},{66,9... | collective-permute-start | bytes 2359304 | tf_op jit(solution)/shard_map/ppermute | solution.py:20
  9.7 5.1 %copy-start.3 = (f32[6144]{0:T(1024)}, f32[6144]{0:T(1024)S(1)}, u32[]{:S(2)}) copy-start(f32[6144]{0:T(1024)S(1)} %fusion.23.taps_ref) | copy-start | bytes 73732
  9.7 5.1 %copy-start = (s32[2]{0:T(128)}, s32[2]{0:T(128)S(1)}, u32[]{:S(2)}) copy-start(s32[2]{0:T(128)S(1)} %collective-permute-done.listed_ref) | copy-start | bytes 28
  27.8 0.9 copy-start.2
  50.0 120.1 %all-to-all-start = ((bf16[32,2,3,128,128]{4,3,2,1,0:T(8,128)(2,1)}), bf16[32,2,3,128,128]{4,3,2,1,0:T(8,128)(2,1)}, u32[]{:S(2)}, u32[]{:S(2)}) async-start(bf16[32,2,3,128,128]{4,3,2,1,0:T(8,128)(2,1)} %bitcast.10), calls=%async_computation | async-start | bytes 12582912 | tf_op jit(solution)/shard_map/all_to_all | solution.py:217
  61.0 62.9 %collective-permute-start.1 = (bf16[2,10,256,256]{3,2,1,0:T(8,128)(2,1)}, bf16[2,10,256,256]{3,2,1,0:T(8,128)(2,1)S(1)}, u32[]{:S(2)}, u32[]{:S(2)}) collective-permute-start(bf16[2,10,256,256]{3,2,1,0:T(8,128)(2,1)} %pick.2), channel_id=1, source_target_pairs={{0,32},{32,64},{64,96},{1,33},{33,65},{65,97},{2,34},{34,66},{66,9... | collective-permute-start | bytes 7864328 | tf_op jit(solution)/shard_map/ppermute | solution.py:20
  124.0 1.5 copy-start.1
